TPU v7x, 32 devices: a whole 2x2x4 slice. The times are simulated.
32 devices in a mesh: dp: 16 (over z, y, x), mp: 2 (over core).
Axes of the slice: x: 2, y: 2, z: 4, core: 2. Of those that a mesh axis runs over, the one named last changes fastest.
Arguments:
- hidden: bfloat16 [24576, 3584], P('dp', 'mp'), may hold values from -6 to 6
- frozen_value_weight: bfloat16 [3584, 512], P('mp'), may hold values from -0.09375 to 0.09375
- adapter_down_weight: bfloat16 [16, 3584, 32], P('dp', 'mp'), may hold values from -0.09375 to 0.09375
- adapter_up_weight: bfloat16 [16, 32, 512], P('dp', None, 'mp'), may hold values from -1 to 1
- value_output_gradient: bfloat16 [24576, 512], P('dp', 'mp'), may hold values from -6 to 6
- sequence_tenant_index: int32 [32], P('dp'), may hold values from 0 to 15
- tenant_slot_table: int32 [16], replicated, may hold values from 0 to 15, each once
Outputs:
- values: bfloat16 [24576, 512], P('dp', 'mp')
- hidden_grad: bfloat16 [24576, 3584], P('dp', 'mp')
- down_grad: float32 [16, 3584, 32], P('dp', 'mp')
- up_grad: float32 [16, 32, 512], P('dp', None, 'mp')
Inputs may be any that keep to these rules, and one draw needn't show every extreme that they name: `sequence_tenant_index`: tenant of each sequence; several sequences may share a tenant. `tenant_slot_table`: every slot holds exactly one tenant.
All inputs are finite; a program needn't handle non-finite values.
Results may differ from a plain program's by a relative error of at most 0.0039.
Values may be sent and summed in bfloat16 or wider, within the bound.
No kernel may reach another device: no remote copies, remote signals or barrier semaphores. Data moves between devices by JAX's collectives and lax.ppermute only.
A program may use at most 128 MiB of HBM per device.

v0:
```python
import jax
import jax.numpy as jnp
from jax import lax
from jax.sharding import PartitionSpec as P

highest_precision = lax.Precision.HIGHEST


def local(
    hidden,
    frozen_value_weight,
    adapter_down_weight,
    adapter_up_weight,
    value_output_gradient,
    sequence_tenant_index,
    tenant_slot_table,
):
    seq_count = sequence_tenant_index.shape[0]
    token_rows, shard_width = hidden.shape
    reduced_rank_hidden = adapter_down_weight.shape[2]
    column_total = value_output_gradient.shape[1]
    seq_len = token_rows // seq_count
    down_all, up_all = (
        lax.all_gather(adapter_down_weight, "dp", axis=0, tiled=True),
        lax.all_gather(adapter_up_weight, "dp", axis=0, tiled=True),
    )
    slot_count = down_all.shape[0]
    slot_ids = tenant_slot_table[sequence_tenant_index]
    pick_rows = slot_ids[:, None] == jnp.arange(slot_count, dtype=jnp.int32)[None, :]
    pick_half = pick_rows.astype(jnp.bfloat16)
    pick_full = pick_rows.astype(jnp.float32)
    chosen_down_factor = jnp.einsum(
        "st,tdr->sdr", pick_half, down_all, preferred_element_type=jnp.float32
    ).astype(jnp.bfloat16)
    sequence_input_rows = hidden.reshape(seq_count, seq_len, shard_width)
    seq_grads = value_output_gradient.reshape(seq_count, seq_len, column_total)
    seq_grads_full = seq_grads.astype(jnp.float32)
    reduced_rank_partial = jnp.einsum(
        "bcp,bpk->bck", sequence_input_rows, chosen_down_factor, preferred_element_type=jnp.float32
    )
    frozen_value_output = jnp.dot(hidden, frozen_value_weight, preferred_element_type=jnp.float32)
    chosen_up_factor = jnp.einsum(
        "st,trk->srk", pick_full, up_all.astype(jnp.float32), precision=highest_precision
    )
    reduced_total = lax.psum_scatter(frozen_value_output, "mp", scatter_dimension=1, tiled=True)
    reduced_rank_full = lax.psum(reduced_rank_partial, "mp")
    adapter_shard_output = jnp.einsum(
        "pmy,pyd->pmd", reduced_rank_full, chosen_up_factor, precision=highest_precision
    )
    reduced_total = reduced_total + adapter_shard_output.reshape(token_rows, column_total)
    values = reduced_total.astype(jnp.bfloat16)
    back_part = jnp.einsum(
        "slk,srk->slr", seq_grads_full, chosen_up_factor, precision=highest_precision
    )
    back_full = lax.psum(back_part, "mp")
    up_seq = jnp.einsum(
        "slr,slk->srk", reduced_rank_full, seq_grads_full, precision=highest_precision
    )
    backward_lowrank_term = back_full.astype(jnp.bfloat16)
    adapter_gradient = jnp.einsum(
        "abq,ajq->abj",
        backward_lowrank_term,
        chosen_down_factor,
        preferred_element_type=jnp.float32,
    )
    hidden_grad = (
        lax.dot_general(
            lax.all_gather(value_output_gradient, "mp", axis=1, tiled=True),
            frozen_value_weight,
            (((1,), (1,)), ((), ())),
            preferred_element_type=jnp.float32,
        )
        + adapter_gradient.reshape(token_rows, shard_width)
    ).astype(jnp.bfloat16)
    sequence_down_factor = jnp.einsum(
        "ikp,ikf->ipf",
        sequence_input_rows,
        backward_lowrank_term,
        preferred_element_type=jnp.float32,
    )
    down_slots = jnp.einsum(
        "st,sdr->tdr", pick_full, sequence_down_factor, precision=highest_precision
    )
    up_slots = jnp.einsum("st,srk->trk", pick_full, up_seq, precision=highest_precision)
    down_home, up_home = (
        lax.all_to_all(down_slots, "dp", split_axis=0, concat_axis=0, tiled=True),
        lax.all_to_all(up_slots, "dp", split_axis=0, concat_axis=0, tiled=True),
    )
    owners = lax.axis_size("dp")
    down_grad = down_home.reshape(owners, -1, shard_width, reduced_rank_hidden).sum(axis=0)
    up_grad = up_home.reshape(owners, -1, reduced_rank_hidden, column_total).sum(axis=0)
    return (values, hidden_grad, down_grad, up_grad)


def solution(mesh):
    return jax.shard_map(
        local,
        mesh=mesh,
        in_specs=(
            P("dp", "mp"),
            P("mp", None),
            P("dp", "mp", None),
            P("dp", None, "mp"),
            P("dp", "mp"),
            P("dp"),
            P(),
        ),
        out_specs=(P("dp", "mp"), P("dp", "mp"), P("dp", "mp", None), P("dp", None, "mp")),
        check_vma=False,
    )
```

profile of v0, /device:TPU:14, one launch (start us, length us, event | category | flops | bytes accessed | tf_op | source)
XLA Modules:
  0.0 244.1 jit_solution(3903025227871726788)
XLA Ops:
  7.2 0.0 copy-start
  7.2 0.0 all-gather.3.cloned.1.call-start
  7.2 0.7 all-gather.3.cloned.1.call-update
  7.9 0.0 all-reduce.3.cloned.1.call-start
  8.0 0.7 compare_select_fusion
  8.6 1.3 gather_fusion
  9.9 59.5 %all-gather.3.cloned.1.call-done = bf16[16,1792,32]{1,2,0:T(8,128)(2,1)} async-done(((bf16[1,1792,32]{1,2,0:T(8,128)(2,1)}), bf16[16,1792,32]{1,2,0:T(8,128)(2,1)}) %all-gather.3.cloned.1.call-update) | async-done | bytes 1835024 | tf_op jit(solution)/shard_map/all_gather | solution.py:24
  69.4 3.0 %convolution_convert_fusion = bf16[2,1792,32]{1,0,2:T(2,128)(2,1)S(1)} fusion(bf16[16,1792,32]{1,2,0:T(8,128)(2,1)} %all-gather.3.cloned.1.call-done, s32[2]{0:T(128)S(1)} %gather_fusion), kind=kOutput, calls=%fused_computation.4 | convolution fusion | flops 3784736 | bytes 2064392 | tf_op jit(solution)/shard_map/st,tdr->sdr/dot_general | solution.py:32
  72.4 0.0 copy-start.4
  72.4 0.0 copy-start.1
  72.4 5.0 %convolution_bitcast_fusion.2 = f32[2,768,32]{1,2,0:T(8,128)} fusion(bf16[2,768,1792]{2,1,0:T(8,128)(2,1)} %bitcast.39, bf16[2,1792,32]{1,0,2:T(2,128)(2,1)S(1)} %convolution_convert_fusion), kind=kOutput, calls=%fused_computation.9 | convolution fusion | flops 176160768 | bytes 5931008 | tf_op jit(solution)/shard_map/bcp,bpk->bck/dot_general | solution.py:38
  77.5 0.0 all-reduce.3.cloned.1.call-update
  77.5 0.0 all-gather.5.cloned.1.call-start
  77.5 0.7 all-gather.5.cloned.1.call-update
  78.2 0.0 copy-done.4
  78.2 29.6 %all_gather.10 = bf16[16,32,256]{2,1,0:T(8,128)(2,1)S(1)} all-gather(bf16[1,32,256]{2,1,0:T(8,128)(2,1)S(1)} %copy-done.4), channel_id=1, replica_groups=mesh['dp'=16,'mp'=2] {'dp'}, dimensions={0}, use_global_device_ids=true | all-gather | bytes 278528 | tf_op jit(solution)/shard_map/all_gather | solution.py:25
  107.9 0.3 fusion.5
  108.1 0.0 all-reduce.3.cloned.1.call-done
  108.1 0.0 copy-done.1
  108.1 1.4 fusion.26
  109.5 0.5 fusion.10
  110.1 1.1 copy.32
  111.2 15.5 %all-to-all-start.1 = ((f32[16,32,256]{2,1,0:T(8,128)}), f32[16,32,256]{2,1,0:T(8,128)S(1)}, u32[]{:S(2)}, u32[]{:S(2)}) async-start(f32[16,32,256]{2,1,0:T(8,128)} %copy.32), calls=%async_computation.2 | async-start | bytes 1048576 | tf_op jit(solution)/shard_map/all_to_all | solution.py:87
  126.7 1.5 convolution_bitcast_fusion.1
  128.2 4.7 %all-reduce.4 = bf16[2,768,32]{1,2,0:T(8,128)(2,1)S(1)} all-reduce(f32[2,768,32]{1,2,0:T(8,128)} %convolution_bitcast_fusion.1), channel_id=1, replica_groups=mesh['dp'=16,'mp'=2] {'mp'}, use_global_device_ids=true, to_apply=%region_2.0 | all-reduce | flops 49152 | bytes 294912 | tf_op jit(solution)/shard_map/psum | solution.py:55
  132.9 3.6 %convolution_bitcast_fusion = f32[2,1792,32]{1,2,0:T(8,128)S(1)} fusion(bf16[2,768,1792]{2,1,0:T(8,128)(2,1)} %bitcast.40, bf16[2,768,32]{1,2,0:T(8,128)(2,1)S(1)} %all-reduce.4), kind=kOutput, calls=%fused_computation.3 | convolution fusion | flops 176160768 | bytes 6062080 | tf_op jit(solution)/shard_map/ikp,ikf->ipf/dot_general | solution.py:75
  136.5 2.0 fusion.3
  138.5 3.9 %copy.30 = f32[16,1792,32]{1,2,0:T(8,128)} copy(f32[16,1792,32]{1,0,2:T(8,128)S(1)} %fusion.3) | data formatting | bytes 7340032 | tf_op jit(solution)/shard_map/st,sdr->tdr/dot_general | solution.py:81
  142.4 0.0 all-to-all-done.1
  142.4 0.0 copy-start.2
  142.4 0.8 copy-done.2
  143.2 7.0 %all-to-all-start = ((f32[16,1792,32]{1,2,0:T(8,128)}), f32[16,1792,32]{1,2,0:T(8,128)}, u32[]{:S(2)}, u32[]{:S(2)}) async-start(f32[16,1792,32]{1,2,0:T(8,128)} %copy.30), calls=%async_computation.1 | async-start | bytes 7340032 | tf_op jit(solution)/shard_map/all_to_all | solution.py:86
  150.2 0.2 reduce-scatter.2.cloned.1.call-start
  150.4 0.0 copy-done
  150.4 7.2 %fusion.25 = f32[1536,512]{1,0:T(8,128)} fusion(bf16[1536,1792]{1,0:T(8,128)(2,1)} %param.7, bf16[1792,512]{1,0:T(8,128)(2,1)S(1)} %copy-done), kind=kOutput, calls=%fused_computation.35 | convolution fusion | flops 2818572288 | bytes 10485760 | tf_op jit(solution)/shard_map/dot_general | solution.py:41
  157.7 0.0 reduce-scatter.2.cloned.1.call-update
  157.7 5.8 %fusion.7 = f32[2,768,1792]{2,1,0:T(8,128)} fusion(bf16[2,1792,32]{1,0,2:T(2,128)(2,1)S(1)} %convolution_convert_fusion, bf16[2,768,32]{1,2,0:T(8,128)(2,1)S(1)} %all-reduce.4), kind=kOutput, calls=%fused_computation.14 | convolution fusion | flops 176160768 | bytes 11337728 | tf_op jit(solution)/shard_map/abq,ajq->abj/dot_general | solution.py:60
  163.5 0.0 all-gather.5.cloned.1.call-done
  163.5 0.0 copy-start.3
  163.5 9.4 %fusion = bf16[1536,1792]{1,0:T(8,128)(2,1)} fusion(f32[2,768,1792]{2,1,0:T(8,128)} %fusion.7, bf16[1536,512]{1,0:T(8,128)(2,1)} %all-gather.5.cloned.1.call-done, bf16[1792,512]{1,0:T(8,128)(2,1)S(1)} %copy-done), kind=kOutput, calls=%fused_computation.2 | convolution fusion | flops 2824077312 | bytes 19922944 | tf_op jit(solution)/shard_map/dot_general | solution.py:67
  172.9 0.0 copy-done.3
  172.9 1.4 fusion.13
  174.3 1.7 reduce_sum.24
  176.0 0.0 reduce-scatter.2.cloned.1.call-done
  176.0 2.5 %fusion.2 = bf16[1536,256]{1,0:T(8,128)(2,1)} fusion(f32[1536,256]{1,0:T(8,128)} %reduce-scatter.2.cloned.1.call-done, f32[2,768,256]{2,1,0:T(8,128)S(1)} %fusion.13), kind=kLoop, calls=%fused_computation.7 | loop fusion | flops 786432 | bytes 3932160 | tf_op jit(solution)/shard_map/convert_element_type | solution.py:51
  178.5 56.1 %all-to-all-done = f32[16,1792,32]{1,2,0:T(8,128)} async-done(((f32[16,1792,32]{1,2,0:T(8,128)}), f32[16,1792,32]{1,2,0:T(8,128)}, u32[]{:S(2)}, u32[]{:S(2)}) %all-to-all-start) | async-done | bytes 3670048 | tf_op jit(solution)/shard_map/all_to_all | solution.py:86
  234.6 2.9 %reduce_sum.22 = f32[1792,32]{0,1:T(8,128)} reduce(f32[16,1792,32]{1,2,0:T(8,128)} %all-to-all-done, f32[]{:T(128)} %constant.2.clone.1), dimensions={0}, to_apply=%region_3.0 | reduce | flops 860160 | bytes 3899396 | tf_op jit(solution)/shard_map/reduce_sum | solution.py:90
  (1 shorter events, 0.0 us)
Async XLA Ops:
  7.2 143.3 %copy-start = (bf16[1792,512]{1,0:T(8,128)(2,1)S(1)}, bf16[1792,512]{1,0:T(8,128)(2,1)}, u32[]{:S(2)}) copy-start(bf16[1792,512]{1,0:T(8,128)(2,1)} %param.8) | copy-start | bytes 5505028
  7.2 62.2 %all-gather.3.cloned.1.call-start = ((), (), s32[]{:S(2)}) async-start(), calls=%async_computation.4 | async-start | bytes 1949696 | tf_op jit(solution)/shard_map/all_gather | solution.py:24
  7.9 100.2 %all-reduce.3.cloned.1.call-start = ((), (), s32[]{:S(2)}) async-start(), calls=%async_computation.5 | async-start | bytes 393216 | tf_op jit(solution)/shard_map/psum | solution.py:46
  72.4 5.8 %copy-start.4 = (bf16[1,32,256]{2,1,0:T(8,128)(2,1)S(1)}, bf16[1,32,256]{2,1,0:T(8,128)(2,1)}, u32[]{:S(2)}) copy-start(bf16[1,32,256]{2,1,0:T(8,128)(2,1)} %param.10) | copy-start | bytes 49156
  72.4 35.7 %copy-start.1 = (bf16[1536,256]{1,0:T(8,128)(2,1)S(1)}, bf16[1536,256]{1,0:T(8,128)(2,1)}, u32[]{:S(2)}) copy-start(bf16[1536,256]{1,0:T(8,128)(2,1)} %param.11) | copy-start | bytes 2359300
  77.5 86.0 %all-gather.5.cloned.1.call-start = ((), (), s32[]{:S(2)}) async-start(), calls=%async_computation.6 | async-start | bytes 2359296 | tf_op jit(solution)/shard_map/all_gather | solution.py:68
  111.2 31.3 %all-to-all-start.1 = ((f32[16,32,256]{2,1,0:T(8,128)}), f32[16,32,256]{2,1,0:T(8,128)S(1)}, u32[]{:S(2)}, u32[]{:S(2)}) async-start(f32[16,32,256]{2,1,0:T(8,128)} %copy.32), calls=%async_computation.2 | async-start | bytes 1048576 | tf_op jit(solution)/shard_map/all_to_all | solution.py:87
  142.4 0.8 copy-start.2
  143.2 91.4 %all-to-all-start = ((f32[16,1792,32]{1,2,0:T(8,128)}), f32[16,1792,32]{1,2,0:T(8,128)}, u32[]{:S(2)}, u32[]{:S(2)}) async-start(f32[16,1792,32]{1,2,0:T(8,128)} %copy.30), calls=%async_computation.1 | async-start | bytes 7340032 | tf_op jit(solution)/shard_map/all_to_all | solution.py:86
  150.2 25.8 %reduce-scatter.2.cloned.1.call-start = ((), (), s32[]{:S(2)}) async-start(), calls=%async_computation.3 | async-start | bytes 4718592 | tf_op jit(solution)/shard_map/reduce_scatter | solution.py:45
  163.5 9.4 %copy-start.3 = (f32[2,768,32]{1,2,0:T(8,128)S(1)}, f32[2,768,32]{1,2,0:T(8,128)}, u32[]{:S(2)}) copy-start(f32[2,768,32]{1,2,0:T(8,128)} %all-reduce.3.cloned.1.call-done) | copy-start | bytes 589828
Sparse Core Ops, SparseCore 0:
  10.7 58.6 all-gather.2
  77.6 18.5 all-reduce.2
  97.7 10.6 all-gather.4
  157.8 12.1 reduce-scatter.1
where the time goes:
time: 245 us; the launch traced here: 244 us
  waiting for transfers between devices  117 us (48%)
  matrix products  41.2 us (17%)
  blocking collectives  34.3 us (14%)
  starting transfers between devices  22.8 us (9%)
  between operations  13.8 us (6%)
  other arithmetic  7.77 us (3%)
  local copies, waits for them, and re-layouts  7.13 us (3%)
    all_gather x1, waiting for transfers between devices, local(): lax.all_gather(adapter_down_weight, 'dp', axis=0, tiled=True)  59.5 us
    all_to_all x1, waiting for transfers between devices, local(): lax.all_to_all(down_slots, 'dp', split_axis=0, concat_axis=0, tiled=True)  56.1 us
    all_gather x1, blocking collectives, local(): lax.all_gather(adapter_up_weight, 'dp', axis=0, tiled=True)  29.6 us
    all_to_all x1, starting transfers between devices, local(): lax.all_to_all(up_slots, 'dp', split_axis=0, concat_axis=0, tiled=True)  15.5 us
    dot_general x1, matrix products, local(): lax.dot_general(lax.all_gather(value_output_gradient, 'mp', axis=1, tiled...  9.38 us
    dot_general x1, matrix products, local(): jnp.dot(hidden, frozen_value_weight, preferred_element_type=jnp.float32)  7.23 us
    all_to_all x1, starting transfers between devices, local(): lax.all_to_all(down_slots, 'dp', split_axis=0, concat_axis=0, tiled=True)  6.97 us
    dot_general x1, matrix products, local(): jnp.einsum('abq,ajq->abj', backward_lowrank_term, chosen_down_factor, pre...  5.82 us
  transfers between devices with their start and end apart: 6, of which 2 were waited for; matrix products, arithmetic and copies ran while one was open for 18% of the time, Pallas kernels for 0%

commit v1 on v0

v1 whole, which is shorter than its diff:
```python
import jax
import jax.numpy as jnp
from jax import lax
from jax.sharding import PartitionSpec as P

HIGH = lax.Precision.HIGHEST
F32 = jnp.float32
BF16 = jnp.bfloat16


def inner_size(n):
    return max(q for q in range(1, n + 1) if n % q == 0 and q * q <= n)


def peer(i, d, n):
    return i ^ d if n & (n - 1) == 0 else (i + d) % n


def back(i, d, n):
    return i ^ d if n & (n - 1) == 0 else (i - d) % n


def offset(dst, src, n):
    return dst ^ src if n & (n - 1) == 0 else (dst - src) % n


def program(n, m):
    q = inner_size(n)
    r = n // q

    def send_inner(x, d):
        return lax.ppermute(x, "dp", [(i, i // q * q + peer(i % q, d, q)) for i in range(n)])

    def send_outer(x, d):
        return lax.ppermute(x, "dp", [(i, peer(i // q, d, r) * q + i % q) for i in range(n)])

    def swap(x):
        return lax.ppermute(x, "mp", [(0, 1), (1, 0)])

    def mp_sum(x):
        return x + swap(x) if m == 2 else lax.psum(x, "mp")

    def local(hidden, weight, down, up, grad, tenant, table):
        seqs = tenant.shape[0]
        rows, width = hidden.shape
        rank = down.shape[2]
        cols = grad.shape[1]
        length = rows // seqs
        me = lax.axis_index("dp")
        my_in, my_out = me % q, me // q
        core = lax.axis_index("mp")

        mine = jnp.concatenate([jnp.swapaxes(down[0], 0, 1), up[0]], axis=1)
        held = [mine] + [send_outer(mine, d) for d in range(1, r)]
        ids = table[tenant]
        near_ids = [ids] + [send_inner(ids, d) for d in range(1, q)]
        where_out = [offset(my_out, v // q, r) for v in near_ids]

        def pick(choice, parts):
            out = parts[0]
            for k in range(1, len(parts)):
                out = jnp.where(choice == k, parts[k], out)
            return out

        def wanted(d):
            o = d if q & (q - 1) == 0 else (q - d) % q
            return jnp.stack([pick(where_out[o][j], held) for j in range(seqs)])

        got = [wanted(0)] + [send_inner(wanted(d), d) for d in range(1, q)]
        from_in = offset(my_in, ids % q, q)
        chosen = jnp.stack([pick(from_in[j], [g[j] for g in got]) for j in range(seqs)])
        down_s, up_s = chosen[:, :, :width], chosen[:, :, width:]

        h3 = hidden.reshape(seqs, length, width)
        g3 = grad.reshape(seqs, length, cols)
        if m == 2:
            other = swap(grad)
            grad_full = jnp.where(core == 0, jnp.concatenate([grad, other], 1), jnp.concatenate([other, grad], 1))
        else:
            grad_full = lax.all_gather(grad, "mp", axis=1, tiled=True)
        base = jnp.dot(hidden, weight, preferred_element_type=F32)
        if m == 2:
            theirs = jnp.where(core == 0, base[:, cols:], base[:, :cols])
            ours = jnp.where(core == 0, base[:, :cols], base[:, cols:])
            base_own = ours + swap(theirs)
        else:
            base_own = lax.psum_scatter(base, "mp", scatter_dimension=1, tiled=True)

        back_low = mp_sum(jnp.einsum("slk,srk->srl", g3, up_s, preferred_element_type=F32)).astype(BF16)
        low = mp_sum(jnp.einsum("slw,srw->srl", h3, down_s, preferred_element_type=F32))
        up_f = up_s.astype(F32)
        values = (base_own.reshape(seqs, length, cols) + jnp.einsum("srl,srk->slk", low, up_f, precision=HIGH)).astype(BF16)
        up_seq = jnp.einsum("srl,slk->srk", low, g3.astype(F32), precision=HIGH)
        down_seq = jnp.einsum("srl,slw->srw", back_low, h3, preferred_element_type=F32)
        hidden_grad = (
            lax.dot_general(grad_full, weight, (((1,), (1,)), ((), ())), preferred_element_type=F32)
            + jnp.einsum("srl,srw->slw", back_low, down_s, preferred_element_type=F32).reshape(rows, width)
        ).astype(BF16)

        items = jnp.concatenate([down_seq, up_seq], axis=2)
        small = items.astype(BF16)
        near = [items] + [send_inner(small, d) for d in range(1, q)]
        totals = []
        for k in range(r):
            total = jnp.zeros((rank, width + cols), F32)
            for d in range(q):
                here = (near_ids[d] % q == my_in) & (where_out[d] == k)
                for j in range(seqs):
                    total = total + jnp.where(here[j], near[d][j].astype(F32), 0.0)
            totals.append(total)
        result = totals[0]
        for k in range(1, r):
            o = k if r & (r - 1) == 0 else (r - k) % r
            result = result + send_outer(totals[k].astype(BF16), o).astype(F32)
        down_grad = jnp.swapaxes(result[:, :width], 0, 1)[None]
        up_grad = result[None, :, width:]
        return values.reshape(rows, cols), hidden_grad, down_grad, up_grad

    return local


def solution(mesh):
    return jax.shard_map(
        program(mesh.shape["dp"], mesh.shape["mp"]),
        mesh=mesh,
        in_specs=(
            P("dp", "mp"),
            P("mp", None),
            P("dp", "mp", None),
            P("dp", None, "mp"),
            P("dp", "mp"),
            P("dp"),
            P(),
        ),
        out_specs=(P("dp", "mp"), P("dp", "mp"), P("dp", "mp", None), P("dp", None, "mp")),
        check_vma=False,
    )
```

time: 245 us -> 128 us (0.52)
  the two profiles are of different devices: /device:TPU:14 before, /device:TPU:0 now
where the time goes in v1:
time: 128 us
  other arithmetic  34.4 us (27%)
  starting transfers between devices  21.4 us (17%)
  between operations  20.3 us (16%)
  waiting for transfers between devices  19.4 us (15%)
  matrix products  18.8 us (15%)
  local copies, waits for them, and re-layouts  13.4 us (10%)
    ppermute x9, waiting for transfers between devices, send_inner(): lax.ppermute(x, 'dp', [(i, i // q * q + peer(i % q, d, q)) for i in range...  19.3 us
    convert_element_type x3, other arithmetic, local(): result = result + send_outer(totals[k].astype(BF16), o).astype(F32)  17.5 us
    ppermute x9, starting transfers between devices, send_inner(): lax.ppermute(x, 'dp', [(i, i // q * q + peer(i % q, d, q)) for i in range...  12 us
    ppermute x6, starting transfers between devices, send_outer(): lax.ppermute(x, 'dp', [(i, peer(i // q, d, r) * q + i % q) for i in range...  8.64 us
    dot_general x1, matrix products, local(): lax.dot_general(grad_full, weight, (((1,), (1,)), ((), ())), preferred_el...  7.49 us
    slice x12, local copies, waits for them, and re-layouts, local(): total = total + jnp.where(here[j], near[d][j].astype(F32), 0.0)  7.18 us
    add x1, other arithmetic, local(): result = result + send_outer(totals[k].astype(BF16), o).astype(F32)  6.43 us
    dot_general x1, matrix products, local(): base = jnp.dot(hidden, weight, preferred_element_type=F32)  5.36 us
  transfers between devices with their start and end apart: 19, of which 5 were waited for; matrix products, arithmetic and copies ran while one was open for 48% of the time, Pallas kernels for 0%

profile of v1, /device:TPU:0, one launch (start us, length us, event | category | flops | bytes accessed | tf_op | source)
XLA Modules:
  0.0 127.6 jit_solution(580431832377051305)
XLA Ops:
  0.6 0.8 compare_select_fusion
  1.4 1.8 %gather_fusion = s32[2]{0:T(128)} fusion(s32[16]{0:T(128)} %param.13, s32[1024]{0:T(1024)S(1)} %pad_clamp_fusion), kind=kCustom, calls=%fused_computation | custom fusion | bytes 24 | tf_op jit(solution)/shard_map/gather | solution.py:55
  3.2 3.9 %collective-permute-start.1 = (s32[2]{0:T(128)}, s32[2]{0:T(128)}, u32[]{:S(2)}, u32[]{:S(2)}) collective-permute-start(s32[2]{0:T(128)} %gather_fusion), channel_id=1, source_target_pairs={{0,6},{2,4},{4,2},{6,0},{8,14},{10,12},{12,10},{14,8},{16,22},{18,... | collective-permute-start | bytes 32 | tf_op jit(solution)/shard_map/ppermute | solution.py:32
  7.7 1.7 %pad_maximum_fusion.4 = bf16[32,2048]{1,0:T(8,128)(2,1)} fusion(bf16[32,256]{1,0:T(8,128)(2,1)} %bitcast.170, bf16[32,1792]{1,0:T(8,128)(2,1)} %bitcast.164), kind=kLoop, calls=%fused_computation.98 | loop fusion | flops 262144 | bytes 262144 | tf_op jit(solution)/shard_map/concatenate | solution.py:53
  9.4 3.6 %collective-permute-start.2 = (bf16[32,2048]{1,0:T(8,128)(2,1)}, bf16[32,2048]{1,0:T(8,128)(2,1)S(1)}, u32[]{:S(2)}, u32[]{:S(2)}) collective-permute-start(bf16[32,2048]{1,0:T(8,128)(2,1)} %pad_maximum_fusion.4), channel_id=1, source_target_pairs={{0,24},{2,26},{4,28},{6,30},{8,16},{10,18},{12,20},{14,22},{16,8},... | collective-permute-start | bytes 393224 | tf_op jit(solution)/shard_map/ppermute | solution.py:35
  13.0 0.8 collective-permute-start.4
  13.8 1.2 compare_and_fusion.15
  16.8 0.7 fusion.95
  23.8 0.7 compare_and_fusion.7
  24.4 0.6 fusion.87
  25.6 0.6 fusion.82
  26.2 5.4 %fusion.99 = f32[1536,512]{1,0:T(8,128)S(1)} fusion(bf16[1536,1792]{1,0:T(8,128)(2,1)} %param.7, bf16[1792,512]{1,0:T(8,128)(2,1)S(1)} %copy-done), kind=kOutput, calls=%fused_computation.185 | convolution fusion | flops 2818572288 | bytes 10485760 | tf_op jit(solution)/shard_map/dot_general | solution.py:81
  31.6 1.4 %slice_select_fusion = f32[1536,256]{1,0:T(8,128)} fusion(f32[1536,512]{1,0:T(8,128)S(1)} %fusion.99, pred[]{:T(512)S(6)} %eq.293), kind=kLoop, calls=%fused_computation.12 | loop fusion | flops 393216 | bytes 4718593 | tf_op jit(solution)/shard_map/jit(_where)/select_n | solution.py:83
  33.3 0.6 compare_and_fusion.12
  34.5 0.6 compare_and_fusion.14
  35.2 0.7 fusion.98
  35.8 0.6 fusion.91
  37.5 0.6 fusion.93
  38.7 0.6 fusion.80
  39.3 0.6 fusion.97
  51.7 0.6 fusion.83
  52.7 2.7 %collective-permute-start.5 = (bf16[2,32,2048]{2,1,0:T(8,128)(2,1)S(1)}, bf16[2,32,2048]{2,1,0:T(8,128)(2,1)S(1)}, u32[]{:S(2)}, u32[]{:S(2)}) collective-permute-start(bf16[2,32,2048]{2,1,0:T(8,128)(2,1)S(1)} %pad_maximum_fusion.1), channel_id=1, source_target_pairs={{0,6},{2,4},{4,2},{6,0},{8,14},{10,12},{12,10},{14,8},{16,22},{18,... | collective-permute-start | bytes 786440 | tf_op jit(solution)/shard_map/ppermute | solution.py:32
  56.5 0.6 fusion.81
  57.1 0.6 fusion.84
  57.7 0.6 fusion.85
  58.3 4.6 %collective-permute-done.5 = bf16[2,32,2048]{2,1,0:T(8,128)(2,1)S(1)} collective-permute-done((bf16[2,32,2048]{2,1,0:T(8,128)(2,1)S(1)}, bf16[2,32,2048]{2,1,0:T(8,128)(2,1)S(1)}, u32[]{:S(2)}, u32[]{:S(2)}) %collective-permute-start.5) | collective-permute-done | bytes 262176 | tf_op jit(solution)/shard_map/ppermute | solution.py:32
  62.9 4.9 %collective-permute-done.7 = bf16[2,32,2048]{2,1,0:T(8,128)(2,1)S(1)} collective-permute-done((bf16[2,32,2048]{2,1,0:T(8,128)(2,1)S(1)}, bf16[2,32,2048]{2,1,0:T(8,128)(2,1)S(1)}, u32[]{:S(2)}, u32[]{:S(2)}) %collective-permute-start.7) | collective-permute-done | bytes 262176 | tf_op jit(solution)/shard_map/ppermute | solution.py:32
  68.5 1.7 %fusion.67 = f32[2,32,768]{2,1,0:T(8,128)S(1)} fusion(bf16[2,768,1792]{2,1,0:T(8,128)(2,1)S(1)} %bitcast.159, bf16[1,32,2048]{2,1,0:T(8,128)(2,1)S(1)} %fusion.49, bf16[1,32,2048]{2,1,0:T(8,128)(2,1)S(1)} %fusion.45), kind=kOutput, calls=%fused_computation.163 | convolution fusion | flops 176275456 | bytes 5963776 | tf_op jit(solution)/shard_map/slw,srw->srl/dot_general | solution.py:90
  70.7 1.0 fusion.101
  72.3 1.6 %collective-permute-start.13 = (bf16[2,32,2048]{2,1,0:T(8,128)(2,1)S(1)}, bf16[2,32,2048]{2,1,0:T(8,128)(2,1)S(1)}, u32[]{:S(2)}, u32[]{:S(2)}) collective-permute-start(bf16[2,32,2048]{2,1,0:T(8,128)(2,1)S(1)} %fusion.7), channel_id=1, source_target_pairs={{0,2},{2,0},{4,6},{6,4},{8,10},{10,8},{12,14},{14,12},{16,18},{18,... | collective-permute-start | bytes 786440 | tf_op jit(solution)/shard_map/ppermute | solution.py:32
  73.9 0.9 collective-permute-start.14
  74.7 1.1 collective-permute-start.15
  75.9 1.6 %fusion.65 = f32[2,768,1792]{2,1,0:T(8,128)S(1)} fusion(bf16[2,32,768]{2,1,0:T(8,128)(2,1)S(1)} %add_convert_fusion.1, bf16[1,32,2048]{2,1,0:T(8,128)(2,1)S(1)} %fusion.49, bf16[1,32,2048]{2,1,0:T(8,128)(2,1)S(1)} %fusion.45), kind=kOutput, calls=%fused_computation.162 | convolution fusion | flops 176275456 | bytes 11370496 | tf_op jit(solution)/shard_map/srl,srw->slw/dot_general | solution.py:97
  77.5 0.8 fusion.55
  78.3 3.2 %collective-permute-done.13 = bf16[2,32,2048]{2,1,0:T(8,128)(2,1)S(1)} collective-permute-done((bf16[2,32,2048]{2,1,0:T(8,128)(2,1)S(1)}, bf16[2,32,2048]{2,1,0:T(8,128)(2,1)S(1)}, u32[]{:S(2)}, u32[]{:S(2)}) %collective-permute-start.13) | collective-permute-done | bytes 262176 | tf_op jit(solution)/shard_map/ppermute | solution.py:32
  81.5 6.2 %collective-permute-done.14 = bf16[2,32,2048]{2,1,0:T(8,128)(2,1)S(1)} collective-permute-done((bf16[2,32,2048]{2,1,0:T(8,128)(2,1)S(1)}, bf16[2,32,2048]{2,1,0:T(8,128)(2,1)S(1)}, u32[]{:S(2)}, u32[]{:S(2)}) %collective-permute-start.14) | collective-permute-done | bytes 262176 | tf_op jit(solution)/shard_map/ppermute | solution.py:32
  87.8 5.9 %fusion.52 = (bf16[32,2048]{1,0:T(8,128)(2,1)}, f32[1,32,2048]{2,1,0:T(8,128)S(1)}, f32[1,32,2048]{2,1,0:T(8,128)S(1)}) fusion(pred[]{:T(512)} %bitcast.68, pred[]{:T(512)} %bitcast.67, pred[]{:T(512)} %bitcast.66, pred[]{:T(512)} %bitcast.65, pred[]{:T(512)} %bitcast.64, pred[]{:T(512)} %bitcast.63, pred[]{:T(512)} %bitcast.62, pred[]{:T(512)} %bitcast.61, ...), kind=kLoop, calls=%fused_computation.107 | loop fusion | flops 1572864 | bytes 1966088 | tf_op jit(solution)/shard_map/convert_element_type | solution.py:114
  93.7 5.8 %fusion.51 = bf16[32,2048]{1,0:T(8,128)(2,1)} fusion(pred[]{:T(512)} %bitcast.77, pred[]{:T(512)} %bitcast.76, pred[]{:T(512)} %bitcast.75, pred[]{:T(512)} %bitcast.74, pred[]{:T(512)} %bitcast.73, pred[]{:T(512)} %bitcast.72, f32[1,32,2048]{2,1,0:T(8,128)S(1)} %get-tuple-element.19, pred[]{:T(512)} %bitcast.71, f32[1,32,2048]{2,1,0:T(8,128)S(1)} %get-tuple-element.18, ...), kind=kLoop, calls=%fused_computation.106 | loop fusion | flops 1441792 | bytes 1441800 | tf_op jit(solution)/shard_map/convert_element_type | solution.py:114
  99.5 2.1 %collective-permute-start.17 = (bf16[32,2048]{1,0:T(8,128)(2,1)}, bf16[32,2048]{1,0:T(8,128)(2,1)}, u32[]{:S(2)}, u32[]{:S(2)}) collective-permute-start(bf16[32,2048]{1,0:T(8,128)(2,1)} %fusion.51), channel_id=1, source_target_pairs={{0,16},{2,18},{4,20},{6,22},{8,24},{10,26},{12,28},{14,30},{16,0},... | collective-permute-start | bytes 393224 | tf_op jit(solution)/shard_map/ppermute | solution.py:35
  101.6 5.8 %fusion.50 = bf16[32,2048]{1,0:T(8,128)(2,1)} fusion(pred[]{:T(512)} %bitcast.86, pred[]{:T(512)} %bitcast.85, pred[]{:T(512)} %bitcast.84, pred[]{:T(512)} %bitcast.83, pred[]{:T(512)} %bitcast.82, pred[]{:T(512)} %bitcast.81, f32[1,32,2048]{2,1,0:T(8,128)S(1)} %get-tuple-element.19, pred[]{:T(512)} %bitcast.80, f32[1,32,2048]{2,1,0:T(8,128)S(1)} %get-tuple-element.18, ...), kind=kLoop, calls=%fused_computation.105 | loop fusion | flops 1441792 | bytes 1441800 | tf_op jit(solution)/shard_map/convert_element_type | solution.py:114
  107.4 1.5 %collective-permute-start.18 = (bf16[32,2048]{1,0:T(8,128)(2,1)}, bf16[32,2048]{1,0:T(8,128)(2,1)}, u32[]{:S(2)}, u32[]{:S(2)}) collective-permute-start(bf16[32,2048]{1,0:T(8,128)(2,1)} %fusion.50), channel_id=1, source_target_pairs={{0,24},{2,26},{4,28},{6,30},{8,16},{10,18},{12,20},{14,22},{16,8},... | collective-permute-start | bytes 393224 | tf_op jit(solution)/shard_map/ppermute | solution.py:35
  108.9 0.6 collective-permute-start.16
  109.6 7.5 %fusion = bf16[1536,1792]{1,0:T(8,128)(2,1)} fusion(f32[2,768,1792]{2,1,0:T(8,128)S(1)} %fusion.65, bf16[1792,512]{1,0:T(8,128)(2,1)S(1)} %copy-done, bf16[1536,256]{1,0:T(8,128)(2,1)} %collective-permute-done.11, bf16[1536,256]{1,0:T(8,128)(2,1)} %param.11, pred[]{:T(512)S(6)} %eq.293), kind=kOutput, calls=%fused_computation.2 | convolution fusion | flops 2831155200 | bytes 19922944 | tf_op jit(solution)/shard_map/dot_general | solution.py:96
  117.1 6.4 %fusion.17 = f32[32,2048]{1,0:T(8,128)S(1)} fusion(bf16[32,2048]{1,0:T(8,128)(2,1)} %collective-permute-done.18, bf16[32,2048]{1,0:T(8,128)(2,1)} %collective-permute-done.17, bf16[32,2048]{1,0:T(8,128)(2,1)} %collective-permute-done.16, f32[1,32,2048]{2,1,0:T(8,128)} %copy-done.4, f32[1,32,2048]{2,1,0:T(8,128)} %copy-done.3, pred[]{:T(512)} %bitcast.59, ...), kind=kLoop, calls=%fused_computation.52 | loop fusion | flops 1769472 | bytes 1966088 | tf_op jit(solution)/shard_map/add | solution.py:114
  123.5 0.6 slice_bitcast_fusion.7
  124.1 0.7 slice_bitcast_fusion
  124.8 1.7 %select_add_fusion = f32[1536,256]{1,0:T(8,128)S(1)} fusion(f32[1536,256]{1,0:T(8,128)} %collective-permute-done, f32[1536,512]{1,0:T(8,128)S(1)} %fusion.99, pred[]{:T(512)S(6)} %eq.293), kind=kLoop, calls=%fused_computation.10 | loop fusion | flops 786432 | bytes 6291457 | tf_op jit(solution)/shard_map/add | solution.py:85
  126.5 1.1 add_convert_fusion
  (68 shorter events, 7.3 us)
Async XLA Ops:
  0.6 25.6 %copy-start = (bf16[1792,512]{1,0:T(8,128)(2,1)S(1)}, bf16[1792,512]{1,0:T(8,128)(2,1)}, u32[]{:S(2)}) copy-start(bf16[1792,512]{1,0:T(8,128)(2,1)} %param.8) | copy-start | bytes 5505028
  3.2 29.8 %collective-permute-start.1 = (s32[2]{0:T(128)}, s32[2]{0:T(128)}, u32[]{:S(2)}, u32[]{:S(2)}) collective-permute-start(s32[2]{0:T(128)} %gather_fusion), channel_id=1, source_target_pairs={{0,6},{2,4},{4,2},{6,0},{8,14},{10,12},{12,10},{14,8},{16,22},{18,... | collective-permute-start | bytes 32 | tf_op jit(solution)/shard_map/ppermute | solution.py:32
  7.2 27.4 %collective-permute-start.8 = (s32[2]{0:T(128)}, s32[2]{0:T(128)}, u32[]{:S(2)}, u32[]{:S(2)}) collective-permute-start(s32[2]{0:T(128)} %gather_fusion), channel_id=1, source_target_pairs={{0,2},{2,0},{4,6},{6,4},{8,10},{10,8},{12,14},{14,12},{16,18},{18,... | collective-permute-start | bytes 32 | tf_op jit(solution)/shard_map/ppermute | solution.py:32
  7.7 60.8 %slice-start = ((s8[5505024]{0:T(1024)(128)(4,1)}), s8[1310720]{0:T(1024)(128)(4,1)S(1)}, s32[]{:S(2)}) async-start(s8[5505024]{0:T(1024)(128)(4,1)} %bitcast.157), calls=%async_computation | async-start | bytes 2621440
  9.4 43.0 %collective-permute-start.2 = (bf16[32,2048]{1,0:T(8,128)(2,1)}, bf16[32,2048]{1,0:T(8,128)(2,1)S(1)}, u32[]{:S(2)}, u32[]{:S(2)}) collective-permute-start(bf16[32,2048]{1,0:T(8,128)(2,1)} %pad_maximum_fusion.4), channel_id=1, source_target_pairs={{0,24},{2,26},{4,28},{6,30},{8,16},{10,18},{12,20},{14,22},{16,8},... | collective-permute-start | bytes 393224 | tf_op jit(solution)/shard_map/ppermute | solution.py:35
  13.0 39.4 %collective-permute-start.3 = (bf16[32,2048]{1,0:T(8,128)(2,1)}, bf16[32,2048]{1,0:T(8,128)(2,1)S(1)}, u32[]{:S(2)}, u32[]{:S(2)}) collective-permute-start(bf16[32,2048]{1,0:T(8,128)(2,1)} %pad_maximum_fusion.4), channel_id=1, source_target_pairs={{0,16},{2,18},{4,20},{6,22},{8,24},{10,26},{12,28},{14,30},{16,0},... | collective-permute-start | bytes 393224 | tf_op jit(solution)/shard_map/ppermute | solution.py:35
  13.0 39.4 %collective-permute-start.4 = (bf16[32,2048]{1,0:T(8,128)(2,1)}, bf16[32,2048]{1,0:T(8,128)(2,1)S(1)}, u32[]{:S(2)}, u32[]{:S(2)}) collective-permute-start(bf16[32,2048]{1,0:T(8,128)(2,1)} %pad_maximum_fusion.4), channel_id=1, source_target_pairs={{0,8},{2,10},{4,12},{6,14},{8,0},{10,2},{12,4},{14,6},{16,24},{18,... | collective-permute-start | bytes 393224 | tf_op jit(solution)/shard_map/ppermute | solution.py:35
  26.2 42.2 %slice-start.1 = ((s8[5505024]{0:T(1024)(128)(4,1)}), s8[4194304]{0:T(1024)(128)(4,1)S(1)}, s32[]{:S(2)}) async-start(s8[5505024]{0:T(1024)(128)(4,1)} %bitcast.157), calls=%async_computation.1 | async-start | bytes 8388608
  31.6 2.9 %copy-start.5 = (bf16[1536,256]{1,0:T(8,128)(2,1)S(1)}, bf16[1536,256]{1,0:T(8,128)(2,1)}, u32[]{:S(2)}) copy-start(bf16[1536,256]{1,0:T(8,128)(2,1)} %param.11) | copy-start | bytes 2359300
  31.6 20.8 %copy-start.6 = (bf16[1,1792,32]{1,2,0:T(8,128)(2,1)S(1)}, bf16[1,1792,32]{1,2,0:T(8,128)(2,1)}, u32[]{:S(2)}) copy-start(bf16[1,1792,32]{1,2,0:T(8,128)(2,1)} %param.9) | copy-start | bytes 344068
  31.6 20.8 %copy-start.7 = (bf16[1,32,256]{2,1,0:T(8,128)(2,1)S(1)}, bf16[1,32,256]{2,1,0:T(8,128)(2,1)}, u32[]{:S(2)}) copy-start(bf16[1,32,256]{2,1,0:T(8,128)(2,1)} %param.10) | copy-start | bytes 49156
  33.0 3.7 %collective-permute-start.6 = (s32[2]{0:T(128)}, s32[2]{0:T(128)S(1)}, u32[]{:S(2)}, u32[]{:S(2)}) collective-permute-start(s32[2]{0:T(128)} %gather_fusion), channel_id=1, source_target_pairs={{0,4},{2,6},{4,0},{6,2},{8,12},{10,14},{12,8},{14,10},{16,20},{18,... | collective-permute-start | bytes 32 | tf_op jit(solution)/shard_map/ppermute | solution.py:32
  34.5 75.0 %collective-permute-start.11 = (bf16[1536,256]{1,0:T(8,128)(2,1)S(1)}, bf16[1536,256]{1,0:T(8,128)(2,1)}, u32[]{:S(2)}, u32[]{:S(2)}) collective-permute-start(bf16[1536,256]{1,0:T(8,128)(2,1)S(1)} %copy-done.5), channel_id=1, source_target_pairs={{0,1},{1,0},{2,3},{3,2},{4,5},{5,4},{6,7},{7,6},{8,9},{9,8},{10,11... | collective-permute-start | bytes 2359304 | tf_op jit(solution)/shard_map/ppermute | solution.py:38
  36.7 88.1 %collective-permute-start = (f32[1536,256]{1,0:T(8,128)}, f32[1536,256]{1,0:T(8,128)}, u32[]{:S(2)}, u32[]{:S(2)}) collective-permute-start(f32[1536,256]{1,0:T(8,128)} %slice_select_fusion), channel_id=1, source_target_pairs={{0,1},{1,0},{2,3},{3,2},{4,5},{5,4},{6,7},{7,6},{8,9},{9,8},{10,11... | collective-permute-start | bytes 4718600 | tf_op jit(solution)/shard_map/ppermute | solution.py:38
  52.7 10.2 %collective-permute-start.5 = (bf16[2,32,2048]{2,1,0:T(8,128)(2,1)S(1)}, bf16[2,32,2048]{2,1,0:T(8,128)(2,1)S(1)}, u32[]{:S(2)}, u32[]{:S(2)}) collective-permute-start(bf16[2,32,2048]{2,1,0:T(8,128)(2,1)S(1)} %pad_maximum_fusion.1), channel_id=1, source_target_pairs={{0,6},{2,4},{4,2},{6,0},{8,14},{10,12},{12,10},{14,8},{16,22},{18,... | collective-permute-start | bytes 786440 | tf_op jit(solution)/shard_map/ppermute | solution.py:32
  55.5 12.3 %collective-permute-start.7 = (bf16[2,32,2048]{2,1,0:T(8,128)(2,1)S(1)}, bf16[2,32,2048]{2,1,0:T(8,128)(2,1)S(1)}, u32[]{:S(2)}, u32[]{:S(2)}) collective-permute-start(bf16[2,32,2048]{2,1,0:T(8,128)(2,1)S(1)} %pad_maximum_fusion.2), channel_id=1, source_target_pairs={{0,4},{2,6},{4,0},{6,2},{8,12},{10,14},{12,8},{14,10},{16,20},{18,... | collective-permute-start | bytes 786440 | tf_op jit(solution)/shard_map/ppermute | solution.py:32
  56.1 11.8 %collective-permute-start.9 = (bf16[2,32,2048]{2,1,0:T(8,128)(2,1)S(1)}, bf16[2,32,2048]{2,1,0:T(8,128)(2,1)S(1)}, u32[]{:S(2)}, u32[]{:S(2)}) collective-permute-start(bf16[2,32,2048]{2,1,0:T(8,128)(2,1)S(1)} %pad_maximum_fusion.3), channel_id=1, source_target_pairs={{0,2},{2,0},{4,6},{6,4},{8,10},{10,8},{12,14},{14,12},{16,18},{18,... | collective-permute-start | bytes 786440 | tf_op jit(solution)/shard_map/ppermute | solution.py:32
  68.4 2.2 %collective-permute-start.12 = (f32[2,32,768]{2,1,0:T(8,128)S(1)}, f32[2,32,768]{2,1,0:T(8,128)S(1)}, u32[]{:S(2)}, u32[]{:S(2)}) collective-permute-start(f32[2,32,768]{2,1,0:T(8,128)S(1)} %fusion.100), channel_id=1, source_target_pairs={{0,1},{1,0},{2,3},{3,2},{4,5},{5,4},{6,7},{7,6},{8,9},{9,8},{10,11... | collective-permute-start | bytes 589832 | tf_op jit(solution)/shard_map/ppermute | solution.py:38
  70.2 1.6 %collective-permute-start.10 = (f32[2,32,768]{2,1,0:T(8,128)S(1)}, f32[2,32,768]{2,1,0:T(8,128)S(1)}, u32[]{:S(2)}, u32[]{:S(2)}) collective-permute-start(f32[2,32,768]{2,1,0:T(8,128)S(1)} %fusion.67), channel_id=1, source_target_pairs={{0,1},{1,0},{2,3},{3,2},{4,5},{5,4},{6,7},{7,6},{8,9},{9,8},{10,11... | collective-permute-start | bytes 589832 | tf_op jit(solution)/shard_map/ppermute | solution.py:38
  72.3 9.2 %collective-permute-start.13 = (bf16[2,32,2048]{2,1,0:T(8,128)(2,1)S(1)}, bf16[2,32,2048]{2,1,0:T(8,128)(2,1)S(1)}, u32[]{:S(2)}, u32[]{:S(2)}) collective-permute-start(bf16[2,32,2048]{2,1,0:T(8,128)(2,1)S(1)} %fusion.7), channel_id=1, source_target_pairs={{0,2},{2,0},{4,6},{6,4},{8,10},{10,8},{12,14},{14,12},{16,18},{18,... | collective-permute-start | bytes 786440 | tf_op jit(solution)/shard_map/ppermute | solution.py:32
  73.9 13.9 %collective-permute-start.14 = (bf16[2,32,2048]{2,1,0:T(8,128)(2,1)S(1)}, bf16[2,32,2048]{2,1,0:T(8,128)(2,1)S(1)}, u32[]{:S(2)}, u32[]{:S(2)}) collective-permute-start(bf16[2,32,2048]{2,1,0:T(8,128)(2,1)S(1)} %fusion.7), channel_id=1, source_target_pairs={{0,4},{2,6},{4,0},{6,2},{8,12},{10,14},{12,8},{14,10},{16,20},{18,... | collective-permute-start | bytes 786440 | tf_op jit(solution)/shard_map/ppermute | solution.py:32
  74.7 13.0 %collective-permute-start.15 = (bf16[2,32,2048]{2,1,0:T(8,128)(2,1)S(1)}, bf16[2,32,2048]{2,1,0:T(8,128)(2,1)S(1)}, u32[]{:S(2)}, u32[]{:S(2)}) collective-permute-start(bf16[2,32,2048]{2,1,0:T(8,128)(2,1)S(1)} %fusion.7), channel_id=1, source_target_pairs={{0,6},{2,4},{4,2},{6,0},{8,14},{10,12},{12,10},{14,8},{16,22},{18,... | collective-permute-start | bytes 786440 | tf_op jit(solution)/shard_map/ppermute | solution.py:32
  87.8 19.7 %copy-start.1 = (bf16[2,32,2048]{2,1,0:T(8,128)(2,1)}, bf16[2,32,2048]{2,1,0:T(8,128)(2,1)S(1)}, u32[]{:S(2)}) copy-start(bf16[2,32,2048]{2,1,0:T(8,128)(2,1)S(1)} %collective-permute-done.14) | copy-start | bytes 786436
  87.8 19.7 %copy-start.2 = (bf16[2,32,2048]{2,1,0:T(8,128)(2,1)}, bf16[2,32,2048]{2,1,0:T(8,128)(2,1)S(1)}, u32[]{:S(2)}) copy-start(bf16[2,32,2048]{2,1,0:T(8,128)(2,1)S(1)} %collective-permute-done.15) | copy-start | bytes 786436
  93.7 15.2 %copy-start.3 = (f32[1,32,2048]{2,1,0:T(8,128)}, f32[1,32,2048]{2,1,0:T(8,128)S(1)}, u32[]{:S(2)}) copy-start(f32[1,32,2048]{2,1,0:T(8,128)S(1)} %get-tuple-element.18) | copy-start | bytes 786436
  93.7 15.2 %copy-start.4 = (f32[1,32,2048]{2,1,0:T(8,128)}, f32[1,32,2048]{2,1,0:T(8,128)S(1)}, u32[]{:S(2)}) copy-start(f32[1,32,2048]{2,1,0:T(8,128)S(1)} %get-tuple-element.19) | copy-start | bytes 786436
  99.5 17.5 %collective-permute-start.17 = (bf16[32,2048]{1,0:T(8,128)(2,1)}, bf16[32,2048]{1,0:T(8,128)(2,1)}, u32[]{:S(2)}, u32[]{:S(2)}) collective-permute-start(bf16[32,2048]{1,0:T(8,128)(2,1)} %fusion.51), channel_id=1, source_target_pairs={{0,16},{2,18},{4,20},{6,22},{8,24},{10,26},{12,28},{14,30},{16,0},... | collective-permute-start | bytes 393224 | tf_op jit(solution)/shard_map/ppermute | solution.py:35
  107.4 9.6 %collective-permute-start.18 = (bf16[32,2048]{1,0:T(8,128)(2,1)}, bf16[32,2048]{1,0:T(8,128)(2,1)}, u32[]{:S(2)}, u32[]{:S(2)}) collective-permute-start(bf16[32,2048]{1,0:T(8,128)(2,1)} %fusion.50), channel_id=1, source_target_pairs={{0,24},{2,26},{4,28},{6,30},{8,16},{10,18},{12,20},{14,22},{16,8},... | collective-permute-start | bytes 393224 | tf_op jit(solution)/shard_map/ppermute | solution.py:35
  108.9 8.1 %collective-permute-start.16 = (bf16[32,2048]{1,0:T(8,128)(2,1)}, bf16[32,2048]{1,0:T(8,128)(2,1)}, u32[]{:S(2)}, u32[]{:S(2)}) collective-permute-start(bf16[32,2048]{1,0:T(8,128)(2,1)} %get-tuple-element.17), channel_id=1, source_target_pairs={{0,8},{2,10},{4,12},{6,14},{8,0},{10,2},{12,4},{14,6},{16,24},{18,... | collective-permute-start | bytes 393224 | tf_op jit(solution)/shard_map/ppermute | solution.py:35

commit v2 on v1

v2 whole, which is shorter than its diff:
```python
import jax
import jax.numpy as jnp
from jax import lax
from jax.experimental import pallas as pl
from jax.experimental.pallas import tpu as pltpu
from jax.sharding import PartitionSpec as P


HIGH = lax.Precision.HIGHEST
F32 = jnp.float32
BF16 = jnp.bfloat16


def inner_size(n):
    return max(q for q in range(1, n + 1) if n % q == 0 and q * q <= n)


def peer(i, d, n):
    return i ^ d if n & (n - 1) == 0 else (i + d) % n


def offset(dst, src, n):
    return dst ^ src if n & (n - 1) == 0 else (dst - src) % n


SMEM = pl.BlockSpec(memory_space=pltpu.SMEM)
VMEM = pl.BlockSpec(memory_space=pltpu.VMEM)
SMALL = pltpu.CompilerParams(vmem_limit_bytes=8 << 20)


def kernel_call(body, ints, arrays, outs, scratch=(), inside=True):
    arrays = [pltpu.with_memory_space_constraint(a, pltpu.VMEM) for a in arrays]
    return pl.pallas_call(
        body,
        out_shape=[pltpu.VMEM(o.shape, o.dtype) if inside else o for o in outs],
        in_specs=[SMEM] * len(ints) + [VMEM] * len(arrays),
        out_specs=[VMEM] * len(outs),
        scratch_shapes=list(scratch),
        compiler_params=SMALL,
    )(*ints, *arrays)


def program(n, m):
    q = inner_size(n)
    r = n // q

    def send_inner(x, d):
        return lax.ppermute(x, "dp", [(i, i // q * q + peer(i % q, d, q)) for i in range(n)])

    def send_outer(x, d):
        return lax.ppermute(x, "dp", [(i, peer(i // q, d, r) * q + i % q) for i in range(n)])

    def swap(x):
        return lax.ppermute(x, "mp", [(0, 1), (1, 0)])

    def mp_sum(x):
        return x + swap(x) if m == 2 else lax.psum(x, "mp")

    def opposite(d, size):
        return d if size & (size - 1) == 0 else (size - d) % size

    def local(hidden, weight, down, up, grad, tenant, table):
        seqs = tenant.shape[0]
        rows, width = hidden.shape
        rank = down.shape[2]
        cols = grad.shape[1]
        length = rows // seqs
        me = lax.axis_index("dp").astype(jnp.int32)[None]
        core = lax.axis_index("mp")

        def join(down_ref, up_ref, out):
            out[:, :width] = down_ref[...]
            out[:, width:] = up_ref[...]

        mine = pl.pallas_call(
            join, out_shape=pltpu.VMEM((rank, width + cols), BF16), compiler_params=SMALL, name="join"
        )(
            pltpu.with_memory_space_constraint(jnp.swapaxes(down[0], 0, 1), pltpu.HBM),
            pltpu.with_memory_space_constraint(up[0], pltpu.HBM),
        )
        held, tenants = [mine], [tenant]
        for d in range(1, r):
            held.append(send_outer(mine, d))
        for d in range(1, q):
            tenants.append(send_inner(tenant, d))
        ints = [me, table] + tenants

        def load(source, target, sem):
            pltpu.make_async_copy(source, target, sem).start()
            pltpu.make_async_copy(source, target, sem).wait()

        hidden = pl.pallas_call(
            load,
            out_shape=pltpu.VMEM(hidden.shape, BF16),
            in_specs=[pl.BlockSpec(memory_space=pl.ANY)],
            out_specs=VMEM,
            scratch_shapes=[pltpu.SemaphoreType.DMA(())],
            compiler_params=SMALL,
            name="load",
        )(hidden)

        def slot(refs, d, j):
            return refs[1][refs[2 + d][j]]

        def pick(*refs):
            ins, parts, outs = refs[: 2 + q], refs[2 + q : 2 + q + r], refs[2 + q + r :]
            outer = ins[0][0] // q
            for d in range(1, q):
                for j in range(seqs):
                    have = offset(outer, slot(ins, opposite(d, q), j) // q, r)
                    for k in range(r):

                        @pl.when(have == k)
                        def _(d=d, j=j, k=k):
                            outs[d - 1][j] = parts[k][...]

        sent = kernel_call(pick, ints, held, [jax.ShapeDtypeStruct((seqs, rank, width + cols), BF16)] * (q - 1))
        got = []
        for d in range(1, q):
            got.append(send_inner(sent[d - 1], d))

        def choose(*refs):
            ins, parts = refs[: 2 + q], refs[2 + q : 2 + q + r]
            gots, (down_out, up_out) = refs[2 + q + r : 1 + 2 * q + r], refs[1 + 2 * q + r :]
            inner, outer = ins[0][0] % q, ins[0][0] // q
            for j in range(seqs):
                wanted = slot(ins, 0, j)
                way = offset(inner, wanted % q, q)
                have = offset(outer, wanted // q, r)
                for d in range(1, q):

                    @pl.when(way == d)
                    def _(d=d, j=j):
                        down_out[j] = gots[d - 1][j, :, :width]
                        up_out[j] = gots[d - 1][j, :, width:]

                for k in range(r):

                    @pl.when((way == 0) & (have == k))
                    def _(j=j, k=k):
                        down_out[j] = parts[k][:, :width]
                        up_out[j] = parts[k][:, width:]

        down_s, up_s = kernel_call(
            choose,
            ints,
            held + got,
            [jax.ShapeDtypeStruct((seqs, rank, width), BF16), jax.ShapeDtypeStruct((seqs, rank, cols), BF16)],
        )

        h3 = hidden.reshape(seqs, length, width)
        g3 = grad.reshape(seqs, length, cols)
        if m == 2:
            other = swap(grad)
            grad_full = jnp.where(core == 0, jnp.concatenate([grad, other], 1), jnp.concatenate([other, grad], 1))
        else:
            grad_full = lax.all_gather(grad, "mp", axis=1, tiled=True)
        base = jnp.dot(hidden, weight, preferred_element_type=F32)
        if m == 2:
            theirs = jnp.where(core == 0, base[:, cols:], base[:, :cols])
            ours = jnp.where(core == 0, base[:, :cols], base[:, cols:])
            base_got = swap(theirs)
            base_own = ours + base_got
        else:
            base_own = lax.psum_scatter(base, "mp", scatter_dimension=1, tiled=True)

        back_low = mp_sum(jnp.einsum("slk,srk->srl", g3, up_s, preferred_element_type=F32)).astype(BF16)
        low = mp_sum(jnp.einsum("slw,srw->srl", h3, down_s, preferred_element_type=F32))
        up_f = up_s.astype(F32)
        values = (base_own.reshape(seqs, length, cols) + jnp.einsum("srl,srk->slk", low, up_f, precision=HIGH)).astype(BF16)
        up_seq = jnp.einsum("srl,slk->srk", low, g3.astype(F32), precision=HIGH)
        down_seq = jnp.einsum("srl,slw->srw", back_low, h3, preferred_element_type=F32)
        hidden_grad = (
            lax.dot_general(grad_full, weight, (((1,), (1,)), ((), ())), preferred_element_type=F32)
            + jnp.einsum("srl,srw->slw", back_low, down_s, preferred_element_type=F32).reshape(rows, width)
        ).astype(BF16)

        items = jnp.concatenate([down_seq, up_seq], axis=2)
        small = items.astype(BF16)
        near = []
        for d in range(1, q):
            near.append(send_inner(small, d))

        def gather_items(*refs):
            ins, own, others = refs[: 2 + q], refs[2 + q], refs[3 + q : 2 + 2 * q]
            outs, acc = refs[2 + 2 * q : -1], refs[-1]
            inner, outer = ins[0][0] % q, ins[0][0] // q
            acc[...] = jnp.zeros_like(acc)
            for d in range(q):
                for j in range(seqs):
                    holder = slot(ins, d, j)

                    @pl.when(holder % q == inner)
                    def _(d=d, j=j, holder=holder):
                        k = offset(outer, holder // q, r)
                        item = own[j] if d == 0 else others[d - 1][j].astype(F32)
                        acc[k] += item

            outs[0][...] = acc[0]
            for k in range(1, r):
                outs[k][...] = acc[k].astype(BF16)

        shape = (rank, width + cols)
        totals = kernel_call(
            gather_items,
            ints,
            [items] + near,
            [jax.ShapeDtypeStruct(shape, F32)] + [jax.ShapeDtypeStruct(shape, BF16)] * (r - 1),
            [pltpu.VMEM((r,) + shape, F32)],
        )
        arrived = []
        for k in range(1, r):
            arrived.append(send_outer(totals[k], opposite(k, r)))
        values, hidden_grad, arrived = lax.optimization_barrier((values, hidden_grad, arrived))

        def finish(*refs):
            own, others, down_out, up_out = refs[0], refs[1:r], refs[r], refs[r + 1]
            total = own[...]
            for other in others:
                total = total + other[...].astype(F32)
            down_out[...] = total[:, :width]
            up_out[...] = total[:, width:]

        down_grad, up_grad = kernel_call(
            finish,
            [],
            [totals[0]] + arrived,
            [jax.ShapeDtypeStruct((rank, width), F32), jax.ShapeDtypeStruct((rank, cols), F32)],
            inside=False,
        )
        down_grad = jnp.swapaxes(down_grad, 0, 1)[None]
        return values.reshape(rows, cols), hidden_grad, down_grad, up_grad[None]

    return local


def solution(mesh):
    n, m = mesh.shape["dp"], mesh.shape["mp"]
    return jax.shard_map(
        program(n, m),
        mesh=mesh,
        in_specs=(
            P("dp", "mp"),
            P("mp", None),
            P("dp", "mp", None),
            P("dp", None, "mp"),
            P("dp", "mp"),
            P("dp"),
            P(),
        ),
        out_specs=(P("dp", "mp"), P("dp", "mp"), P("dp", "mp", None), P("dp", None, "mp")),
        check_vma=False,
    )
```

time: 128 us -> 73.7 us (0.58)
  other arithmetic: 34.4 us -> 6.25 us
  between operations: 20.3 us -> 0.83 us
  local copies, waits for them, and re-layouts: 13.4 us -> 2.6 us
  Pallas kernels: 0 us -> 4.32 us
  waiting for transfers between devices: 19.4 us -> 16.2 us
  matrix products: 18.8 us -> 21.7 us
    convert_element_type x3 -> x0, other arithmetic: 17.5 us -> none  [local(): result = result + send_outer(totals[k].astype(BF16), o).astype(F32)]
    slice x17 -> x0, local copies, waits for them, and re-layouts: 10.3 us -> none  [the longest x12 7.18 us: local(): total = total + jnp.where(here[j], near[d][j].astype(F32), 0.0)]
    ppermute x9, waiting for transfers between devices: 19.3 us -> 9.19 us  [send_inner(): lax.ppermute(x, 'dp', [(i, i // q * q + peer(i % q, d, q)) for i in range...]
    ppermute x6, waiting for transfers between devices: 0.02 us -> 7.02 us  [send_outer(): lax.ppermute(x, 'dp', [(i, peer(i // q, d, r) * q + i % q) for i in range...]
    add x2 -> x1, other arithmetic: 8.14 us -> 1.72 us  [local(): base_own = ours + base_got]
    pallas_call x0 -> x6, Pallas kernels: none -> 4.32 us  [the longest x4 3.03 us: kernel_call(): pl.pallas_call(body, out_shape=[pltpu.VMEM(o.shape, o.dtype) if inside el...]
    and x8 -> x0, other arithmetic: 3.13 us -> none  [local(): here = (near_ids[d] % q == my_in) & (where_out[d] == k)]
    unnamed x20 -> x16, local copies, waits for them, and re-layouts: 0.05 us -> 2.6 us
  transfers between devices with their start and end apart: 19 -> 19, of which waited for: 5 -> 8; matrix products, arithmetic and copies ran while one was open for 48% -> 38% of each run, Pallas kernels for 0% -> 5%
where the time goes in v2:
time: 73.7 us; the launch traced here: 73.4 us
  matrix products  21.7 us (29%)
  starting transfers between devices  21.6 us (29%)
  waiting for transfers between devices  16.2 us (22%)
  other arithmetic  6.25 us (8%)
  Pallas kernels  4.32 us (6%)
  local copies, waits for them, and re-layouts  2.6 us (4%)
  between operations  0.83 us (1%)
    ppermute x9, starting transfers between devices, send_inner(): lax.ppermute(x, 'dp', [(i, i // q * q + peer(i % q, d, q)) for i in range...  12.1 us
    ppermute x9, waiting for transfers between devices, send_inner(): lax.ppermute(x, 'dp', [(i, i // q * q + peer(i % q, d, q)) for i in range...  9.19 us
    ppermute x6, starting transfers between devices, send_outer(): lax.ppermute(x, 'dp', [(i, peer(i // q, d, r) * q + i % q) for i in range...  8.9 us
    dot_general x1, matrix products, local(): lax.dot_general(grad_full, weight, (((1,), (1,)), ((), ())), preferred_el...  7.54 us
    ppermute x6, waiting for transfers between devices, send_outer(): lax.ppermute(x, 'dp', [(i, peer(i // q, d, r) * q + i % q) for i in range...  7.02 us
    dot_general x1, matrix products, local(): base = jnp.dot(hidden, weight, preferred_element_type=F32)  4.66 us
    select_n x1, other arithmetic, local(): theirs = jnp.where(core == 0, base[:, cols:], base[:, :cols])  3.39 us
    pallas_call x4, Pallas kernels, kernel_call(): pl.pallas_call(body, out_shape=[pltpu.VMEM(o.shape, o.dtype) if inside el...  3.03 us
  transfers between devices with their start and end apart: 19, of which 8 were waited for; matrix products, arithmetic and copies ran while one was open for 38% of the time, Pallas kernels for 5%

profile of v2, /device:TPU:0, one launch (start us, length us, event | category | flops | bytes accessed | tf_op | source)
XLA Modules:
  0.0 73.4 jit_solution(16259953635808894926)
XLA Ops:
  0.6 0.0 copy-start
  0.6 4.0 %collective-permute-start.3 = (s32[2]{0:T(128)}, s32[2]{0:T(128)S(1)}, u32[]{:S(2)}, u32[]{:S(2)}) collective-permute-start(s32[2]{0:T(128)} %refs_2_.5), channel_id=1, source_target_pairs={{0,6},{2,4},{4,2},{6,0},{8,14},{10,12},{12,10},{14,8},{16,22},{18,... | collective-permute-start | bytes 32 | tf_op jit(solution)/shard_map/ppermute | solution.py:48
  4.6 0.5 collective-permute-start.2
  5.1 0.9 %join.1.refs_6_ = bf16[32,2048]{1,0:T(8,128)(2,1)S(1)} custom-call(bf16[32,1792]{1,0:T(8,128)(2,1)} %bitcast.34, bf16[32,256]{1,0:T(8,128)(2,1)} %bitcast.35), custom_call_target="tpu_custom_call" | custom-call | tf_op jit(solution)/shard_map/join/pallas_call | solution.py:75
  6.1 3.7 %collective-permute-start.6 = (bf16[32,2048]{1,0:T(8,128)(2,1)S(1)}, bf16[32,2048]{1,0:T(8,128)(2,1)S(1)}, u32[]{:S(2)}, u32[]{:S(2)}) collective-permute-start(bf16[32,2048]{1,0:T(8,128)(2,1)S(1)} %join.1.refs_6_), channel_id=1, source_target_pairs={{0,24},{2,26},{4,28},{6,30},{8,16},{10,18},{12,20},{14,22},{16,8},... | collective-permute-start | bytes 393224 | tf_op jit(solution)/shard_map/ppermute | solution.py:51
  9.7 0.0 collective-permute-start.5
  9.7 0.8 %collective-permute-start.4 = (bf16[32,2048]{1,0:T(8,128)(2,1)S(1)}, bf16[32,2048]{1,0:T(8,128)(2,1)S(1)}, u32[]{:S(2)}, u32[]{:S(2)}) collective-permute-start(bf16[32,2048]{1,0:T(8,128)(2,1)S(1)} %join.1.refs_6_), channel_id=1, source_target_pairs={{0,8},{2,10},{4,12},{6,14},{8,0},{10,2},{12,4},{14,6},{16,24},{18,... | collective-permute-start | bytes 393224 | tf_op jit(solution)/shard_map/ppermute | solution.py:51
  10.5 2.6 %copy-done.3 = bf16[1536,1792]{1,0:T(8,128)(2,1)S(1)} copy-done((bf16[1536,1792]{1,0:T(8,128)(2,1)S(1)}, bf16[1536,1792]{1,0:T(8,128)(2,1)}, u32[]{:S(2)}) %copy-start.3) | copy-done | bytes 5505048
  13.1 0.4 load.1
  13.5 0.0 copy-start.1
  13.5 0.0 copy-start.5
  13.5 0.0 copy-start.4
  13.5 4.7 %fusion.13 = f32[1536,512]{1,0:T(8,128)} fusion(bf16[1536,1792]{1,0:T(8,128)(2,1)S(1)} %load.1, bf16[1792,512]{1,0:T(8,128)(2,1)S(1)} %copy-done), kind=kOutput, calls=%fused_computation.20 | convolution fusion | flops 2818572288 | bytes 10485760 | tf_op jit(solution)/shard_map/dot_general | solution.py:158
  18.2 0.5 collective-permute-start.1
  18.6 3.2 %collective-permute-done.1.refs_3_ = s32[2]{0:T(128)S(1)} collective-permute-done((s32[2]{0:T(128)S(1)}, s32[2]{0:T(128)S(1)}, u32[]{:S(2)}, u32[]{:S(2)}) %collective-permute-start.1) | collective-permute-done | bytes 40 | tf_op jit(solution)/shard_map/ppermute | solution.py:48
  21.8 0.8 %shard_map.102 = (bf16[2,32,2048]{2,1,0:T(8,128)(2,1)S(1)}, bf16[2,32,2048]{2,1,0:T(8,128)(2,1)S(1)}, bf16[2,32,2048]{2,1,0:T(8,128)(2,1)S(1)}) custom-call(s32[1]{0:T(128)} %bitcast.1.refs_0_, s32[16]{0:T(128)S(1)} %copy-done.4, s32[2]{0:T(128)S(1)} %copy-done.5, s32[2]{0:T(128)S(1)} %collective-permute-done.1.refs_3_, ...), custom_call_target="tpu_custom_call" | custom-call | tf_op jit(solution)/shard_map/pallas_call | solution.py:33
  22.6 0.5 collective-permute-start.7
  23.1 1.7 %collective-permute-start.8 = (bf16[2,32,2048]{2,1,0:T(8,128)(2,1)S(1)}, bf16[2,32,2048]{2,1,0:T(8,128)(2,1)S(1)}, u32[]{:S(2)}, u32[]{:S(2)}) collective-permute-start(bf16[2,32,2048]{2,1,0:T(8,128)(2,1)S(1)} %get-tuple-element.21), channel_id=1, source_target_pairs={{0,4},{2,6},{4,0},{6,2},{8,12},{10,14},{12,8},{14,10},{16,20},{18,... | collective-permute-start | bytes 786440 | tf_op jit(solution)/shard_map/ppermute | solution.py:48
  24.7 1.4 %collective-permute-start.9 = (bf16[2,32,2048]{2,1,0:T(8,128)(2,1)S(1)}, bf16[2,32,2048]{2,1,0:T(8,128)(2,1)S(1)}, u32[]{:S(2)}, u32[]{:S(2)}) collective-permute-start(bf16[2,32,2048]{2,1,0:T(8,128)(2,1)S(1)} %get-tuple-element.22), channel_id=1, source_target_pairs={{0,6},{2,4},{4,2},{6,0},{8,14},{10,12},{12,10},{14,8},{16,22},{18,... | collective-permute-start | bytes 786440 | tf_op jit(solution)/shard_map/ppermute | solution.py:48
  26.2 3.4 %slice_select_fusion = f32[1536,256]{1,0:T(8,128)} fusion(f32[1536,512]{1,0:T(8,128)} %fusion.13, pred[]{:T(512)S(6)} %eq.2), kind=kLoop, calls=%fused_computation.11 | loop fusion | flops 393216 | bytes 4718593 | tf_op jit(solution)/shard_map/jit(_where)/select_n | solution.py:160
  29.6 1.9 %collective-permute-done.7.refs_10_ = bf16[2,32,2048]{2,1,0:T(8,128)(2,1)S(1)} collective-permute-done((bf16[2,32,2048]{2,1,0:T(8,128)(2,1)S(1)}, bf16[2,32,2048]{2,1,0:T(8,128)(2,1)S(1)}, u32[]{:S(2)}, u32[]{:S(2)}) %collective-permute-start.7) | collective-permute-done | bytes 262176 | tf_op jit(solution)/shard_map/ppermute | solution.py:48
  31.4 2.8 %collective-permute-done.8.refs_11_ = bf16[2,32,2048]{2,1,0:T(8,128)(2,1)S(1)} collective-permute-done((bf16[2,32,2048]{2,1,0:T(8,128)(2,1)S(1)}, bf16[2,32,2048]{2,1,0:T(8,128)(2,1)S(1)}, u32[]{:S(2)}, u32[]{:S(2)}) %collective-permute-start.8) | collective-permute-done | bytes 262176 | tf_op jit(solution)/shard_map/ppermute | solution.py:48
  34.3 1.0 %collective-permute-done.9.refs_12_ = bf16[2,32,2048]{2,1,0:T(8,128)(2,1)S(1)} collective-permute-done((bf16[2,32,2048]{2,1,0:T(8,128)(2,1)S(1)}, bf16[2,32,2048]{2,1,0:T(8,128)(2,1)S(1)}, u32[]{:S(2)}, u32[]{:S(2)}) %collective-permute-start.9) | collective-permute-done | bytes 262176 | tf_op jit(solution)/shard_map/ppermute | solution.py:48
  35.2 0.7 shard_map.103
  35.9 1.5 %fusion.15 = f32[2,32,768]{2,1,0:T(8,128)S(1)} fusion(bf16[2,32,256]{2,1,0:T(8,128)(2,1)S(1)} %get-tuple-element.24, bf16[2,768,256]{2,1,0:T(8,128)(2,1)} %bitcast.6), kind=kOutput, calls=%fused_computation.22 | convolution fusion | flops 25165824 | bytes 1015808 | tf_op jit(solution)/shard_map/slk,srk->srl/dot_general | solution.py:167
  37.4 0.0 collective-permute-start.12
  37.4 1.7 %fusion.14 = f32[2,32,768]{2,1,0:T(8,128)S(1)} fusion(bf16[2,32,1792]{2,1,0:T(8,128)(2,1)S(1)} %get-tuple-element.23, bf16[2,768,1792]{2,1,0:T(8,128)(2,1)S(1)} %bitcast.30), kind=kOutput, calls=%fused_computation.21 | convolution fusion | flops 176160768 | bytes 5931008 | tf_op jit(solution)/shard_map/slw,srw->srl/dot_general | solution.py:168
  39.1 0.5 collective-permute-start.10
  39.6 1.0 %fusion.17 = f32[2,32,1792]{2,1,0:T(8,128)S(1)} fusion(bf16[2,32,768]{2,1,0:T(8,128)(2,1)S(1)} %add_convert_fusion.1, bf16[2,768,1792]{2,1,0:T(8,128)(2,1)S(1)} %bitcast.31), kind=kOutput, calls=%fused_computation.24 | convolution fusion | flops 176160768 | bytes 6062080 | tf_op jit(solution)/shard_map/srl,slw->srw/dot_general | solution.py:172
  40.7 0.0 collective-permute-done.10
  40.7 1.6 %fusion.7 = f32[2,32,256]{2,1,0:T(8,128)S(1)} fusion(bf16[2,768,256]{2,1,0:T(8,128)(2,1)} %bitcast.6, f32[2,32,768]{2,1,0:T(8,128)S(1)} %fusion.14, f32[2,32,768]{2,1,0:T(8,128)S(1)} %collective-permute-done.10), kind=kOutput, calls=%fused_computation.14 | convolution fusion | flops 151044096 | bytes 1245184 | tf_op jit(solution)/shard_map/srl,slk->srk/dot_general | solution.py:171
  42.3 2.1 %collective-permute-start.15 = (bf16[2,32,2048]{2,1,0:T(8,128)(2,1)S(1)}, bf16[2,32,2048]{2,1,0:T(8,128)(2,1)S(1)}, u32[]{:S(2)}, u32[]{:S(2)}) collective-permute-start(bf16[2,32,2048]{2,1,0:T(8,128)(2,1)S(1)} %fusion.12), channel_id=1, source_target_pairs={{0,6},{2,4},{4,2},{6,0},{8,14},{10,12},{12,10},{14,8},{16,22},{18,... | collective-permute-start | bytes 786440 | tf_op jit(solution)/shard_map/ppermute | solution.py:48
  44.4 2.0 %fusion.9 = f32[2,768,256]{2,1,0:T(8,128)} fusion(bf16[2,32,256]{2,1,0:T(8,128)(2,1)S(1)} %get-tuple-element.24, f32[2,32,768]{2,1,0:T(8,128)S(1)} %fusion.14, f32[2,32,768]{2,1,0:T(8,128)S(1)} %collective-permute-done.10), kind=kOutput, calls=%fused_computation.16 | convolution fusion | flops 151044096 | bytes 1998848 | tf_op jit(solution)/shard_map/srl,srk->slk/dot_general | solution.py:170
  46.5 1.0 %collective-permute-start.14 = (bf16[2,32,2048]{2,1,0:T(8,128)(2,1)S(1)}, bf16[2,32,2048]{2,1,0:T(8,128)(2,1)S(1)}, u32[]{:S(2)}, u32[]{:S(2)}) collective-permute-start(bf16[2,32,2048]{2,1,0:T(8,128)(2,1)S(1)} %fusion.12), channel_id=1, source_target_pairs={{0,4},{2,6},{4,0},{6,2},{8,12},{10,14},{12,8},{14,10},{16,20},{18,... | collective-permute-start | bytes 786440 | tf_op jit(solution)/shard_map/ppermute | solution.py:48
  47.5 0.5 collective-permute-start.13
  48.0 1.6 %fusion.16 = f32[2,768,1792]{2,1,0:T(8,128)S(1)} fusion(bf16[2,32,768]{2,1,0:T(8,128)(2,1)S(1)} %add_convert_fusion.1, bf16[2,32,1792]{2,1,0:T(8,128)(2,1)S(1)} %get-tuple-element.23), kind=kOutput, calls=%fused_computation.23 | convolution fusion | flops 176160768 | bytes 11337728 | tf_op jit(solution)/shard_map/srl,srw->slw/dot_general | solution.py:175
  49.7 7.5 %fusion = bf16[1536,1792]{1,0:T(8,128)(2,1)} fusion(f32[2,768,1792]{2,1,0:T(8,128)S(1)} %fusion.16, bf16[1792,512]{1,0:T(8,128)(2,1)S(1)} %copy-done, bf16[1536,256]{1,0:T(8,128)(2,1)} %collective-permute-done.11, bf16[1536,256]{1,0:T(8,128)(2,1)} %param.11, pred[]{:T(512)S(6)} %eq.2), kind=kOutput, calls=%fused_computation.1 | convolution fusion | flops 2831155200 | bytes 19922944 | tf_op jit(solution)/shard_map/dot_general | solution.py:174
  57.2 0.3 collective-permute-done.14.refs_8_
  57.5 0.1 collective-permute-done.13.refs_7_
  57.6 0.8 %shard_map.104 = (f32[32,2048]{1,0:T(8,128)S(1)}, bf16[32,2048]{1,0:T(8,128)(2,1)S(1)}, bf16[32,2048]{1,0:T(8,128)(2,1)S(1)}, bf16[32,2048]{1,0:T(8,128)(2,1)S(1)}) custom-call(s32[1]{0:T(128)} %bitcast.1.refs_0_, s32[16]{0:T(128)S(1)} %copy-done.4, s32[2]{0:T(128)S(1)} %copy-done.5, s32[2]{0:T(128)S(1)} %collective-permute-done.1.refs_3_, ...), custom_call_target="tpu_custom_call" | custom-call | tf_op jit(solution)/shard_map/pallas_call | solution.py:33
  58.4 1.4 %collective-permute-start.16 = (bf16[32,2048]{1,0:T(8,128)(2,1)S(1)}, bf16[32,2048]{1,0:T(8,128)(2,1)S(1)}, u32[]{:S(2)}, u32[]{:S(2)}) collective-permute-start(bf16[32,2048]{1,0:T(8,128)(2,1)S(1)} %get-tuple-element.25), channel_id=1, source_target_pairs={{0,8},{2,10},{4,12},{6,14},{8,0},{10,2},{12,4},{14,6},{16,24},{18,... | collective-permute-start | bytes 393224 | tf_op jit(solution)/shard_map/ppermute | solution.py:51
  59.8 2.9 %collective-permute-start.17 = (bf16[32,2048]{1,0:T(8,128)(2,1)S(1)}, bf16[32,2048]{1,0:T(8,128)(2,1)S(1)}, u32[]{:S(2)}, u32[]{:S(2)}) collective-permute-start(bf16[32,2048]{1,0:T(8,128)(2,1)S(1)} %get-tuple-element.26), channel_id=1, source_target_pairs={{0,16},{2,18},{4,20},{6,22},{8,24},{10,26},{12,28},{14,30},{16,0},... | collective-permute-start | bytes 393224 | tf_op jit(solution)/shard_map/ppermute | solution.py:51
  62.7 0.2 collective-permute-start.18
  62.9 1.7 %select_add_fusion = f32[1536,256]{1,0:T(8,128)S(1)} fusion(f32[1536,256]{1,0:T(8,128)} %collective-permute-done, f32[1536,512]{1,0:T(8,128)S(1)} %copy-done.6, pred[]{:T(512)S(6)} %eq.2), kind=kLoop, calls=%fused_computation.9 | loop fusion | flops 786432 | bytes 6291457 | tf_op jit(solution)/shard_map/add | solution.py:163
  64.6 1.0 %add_convert_fusion = bf16[2,768,256]{2,1,0:T(8,128)(2,1)} fusion(f32[2,768,256]{2,1,0:T(8,128)S(1)} %bitcast.32, f32[2,768,256]{2,1,0:T(8,128)S(1)} %copy-done.7), kind=kLoop, calls=%fused_computation.8 | loop fusion | flops 786432 | bytes 3932160 | tf_op jit(solution)/shard_map/convert_element_type | solution.py:170
  65.7 0.1 collective-permute-done.16.refs_1_
  65.8 6.9 %collective-permute-done.17.refs_2_ = bf16[32,2048]{1,0:T(8,128)(2,1)S(1)} collective-permute-done((bf16[32,2048]{1,0:T(8,128)(2,1)S(1)}, bf16[32,2048]{1,0:T(8,128)(2,1)S(1)}, u32[]{:S(2)}, u32[]{:S(2)}) %collective-permute-start.17) | collective-permute-done | bytes 131104 | tf_op jit(solution)/shard_map/ppermute | solution.py:51
  72.7 0.7 %shard_map.105 = (f32[32,1792]{1,0:T(8,128)}, f32[32,256]{1,0:T(8,128)}) custom-call(f32[32,2048]{1,0:T(8,128)S(1)} %get-tuple-element.30.refs_0_, bf16[32,2048]{1,0:T(8,128)(2,1)S(1)} %collective-permute-done.16.refs_1_, bf16[32,2048]{1,0:T(8,128)(2,1)S(1)} %collective-permute-done.17.refs_2_, bf16[32,2048]{1,0:T(8,128)(2,1)S(1)} %collective-permute-done.18.refs_3_), custom_call_target="tpu_custom_call" | custom-call | tf_op jit(solution)/shard_map/pallas_call | solution.py:33
  (26 shorter events, 0.1 us)
Async XLA Ops:
  0.6 12.8 %copy-start = (bf16[1792,512]{1,0:T(8,128)(2,1)S(1)}, bf16[1792,512]{1,0:T(8,128)(2,1)}, u32[]{:S(2)}) copy-start(bf16[1792,512]{1,0:T(8,128)(2,1)} %param.8) | copy-start | bytes 5505028
  0.6 17.5 %collective-permute-start.3 = (s32[2]{0:T(128)}, s32[2]{0:T(128)S(1)}, u32[]{:S(2)}, u32[]{:S(2)}) collective-permute-start(s32[2]{0:T(128)} %refs_2_.5), channel_id=1, source_target_pairs={{0,6},{2,4},{4,2},{6,0},{8,14},{10,12},{12,10},{14,8},{16,22},{18,... | collective-permute-start | bytes 32 | tf_op jit(solution)/shard_map/ppermute | solution.py:48
  4.6 14.0 %collective-permute-start.2 = (s32[2]{0:T(128)}, s32[2]{0:T(128)S(1)}, u32[]{:S(2)}, u32[]{:S(2)}) collective-permute-start(s32[2]{0:T(128)} %refs_2_.5), channel_id=1, source_target_pairs={{0,4},{2,6},{4,0},{6,2},{8,12},{10,14},{12,8},{14,10},{16,20},{18,... | collective-permute-start | bytes 32 | tf_op jit(solution)/shard_map/ppermute | solution.py:48
  6.1 15.8 %collective-permute-start.6 = (bf16[32,2048]{1,0:T(8,128)(2,1)S(1)}, bf16[32,2048]{1,0:T(8,128)(2,1)S(1)}, u32[]{:S(2)}, u32[]{:S(2)}) collective-permute-start(bf16[32,2048]{1,0:T(8,128)(2,1)S(1)} %join.1.refs_6_), channel_id=1, source_target_pairs={{0,24},{2,26},{4,28},{6,30},{8,16},{10,18},{12,20},{14,22},{16,8},... | collective-permute-start | bytes 393224 | tf_op jit(solution)/shard_map/ppermute | solution.py:51
  9.7 12.1 %collective-permute-start.5 = (bf16[32,2048]{1,0:T(8,128)(2,1)S(1)}, bf16[32,2048]{1,0:T(8,128)(2,1)S(1)}, u32[]{:S(2)}, u32[]{:S(2)}) collective-permute-start(bf16[32,2048]{1,0:T(8,128)(2,1)S(1)} %join.1.refs_6_), channel_id=1, source_target_pairs={{0,16},{2,18},{4,20},{6,22},{8,24},{10,26},{12,28},{14,30},{16,0},... | collective-permute-start | bytes 393224 | tf_op jit(solution)/shard_map/ppermute | solution.py:51
  9.7 12.1 %collective-permute-start.4 = (bf16[32,2048]{1,0:T(8,128)(2,1)S(1)}, bf16[32,2048]{1,0:T(8,128)(2,1)S(1)}, u32[]{:S(2)}, u32[]{:S(2)}) collective-permute-start(bf16[32,2048]{1,0:T(8,128)(2,1)S(1)} %join.1.refs_6_), channel_id=1, source_target_pairs={{0,8},{2,10},{4,12},{6,14},{8,0},{10,2},{12,4},{14,6},{16,24},{18,... | collective-permute-start | bytes 393224 | tf_op jit(solution)/shard_map/ppermute | solution.py:51
  10.5 2.6 %copy-start.3 = (bf16[1536,1792]{1,0:T(8,128)(2,1)S(1)}, bf16[1536,1792]{1,0:T(8,128)(2,1)}, u32[]{:S(2)}) copy-start(bf16[1536,1792]{1,0:T(8,128)(2,1)} %source.1) | copy-start | bytes 16515076
  13.5 4.7 %copy-start.1 = (bf16[1536,1792]{1,0:T(8,128)(2,1)}, bf16[1536,1792]{1,0:T(8,128)(2,1)S(1)}, u32[]{:S(2)}) copy-start(bf16[1536,1792]{1,0:T(8,128)(2,1)S(1)} %load.1) | copy-start | bytes 16515076
  13.5 4.7 %copy-start.5 = (s32[2]{0:T(128)S(1)}, s32[2]{0:T(128)}, u32[]{:S(2)}) copy-start(s32[2]{0:T(128)} %refs_2_.5) | copy-start | bytes 28
  13.5 8.3 %copy-start.4 = (s32[16]{0:T(128)S(1)}, s32[16]{0:T(128)}, u32[]{:S(2)}) copy-start(s32[16]{0:T(128)} %refs_1_.5) | copy-start | bytes 196
  18.2 3.6 %collective-permute-start.1 = (s32[2]{0:T(128)S(1)}, s32[2]{0:T(128)S(1)}, u32[]{:S(2)}, u32[]{:S(2)}) collective-permute-start(s32[2]{0:T(128)S(1)} %copy-done.5), channel_id=1, source_target_pairs={{0,2},{2,0},{4,6},{6,4},{8,10},{10,8},{12,14},{14,12},{16,18},{18,... | collective-permute-start | bytes 32 | tf_op jit(solution)/shard_map/ppermute | solution.py:48
  18.6 31.0 %collective-permute-start.11 = (bf16[1536,256]{1,0:T(8,128)(2,1)}, bf16[1536,256]{1,0:T(8,128)(2,1)}, u32[]{:S(2)}, u32[]{:S(2)}) collective-permute-start(bf16[1536,256]{1,0:T(8,128)(2,1)} %param.11), channel_id=1, source_target_pairs={{0,1},{1,0},{2,3},{3,2},{4,5},{5,4},{6,7},{7,6},{8,9},{9,8},{10,11... | collective-permute-start | bytes 2359304 | tf_op jit(solution)/shard_map/ppermute | solution.py:54
  22.6 8.8 %collective-permute-start.7 = (bf16[2,32,2048]{2,1,0:T(8,128)(2,1)S(1)}, bf16[2,32,2048]{2,1,0:T(8,128)(2,1)S(1)}, u32[]{:S(2)}, u32[]{:S(2)}) collective-permute-start(bf16[2,32,2048]{2,1,0:T(8,128)(2,1)S(1)} %get-tuple-element.20), channel_id=1, source_target_pairs={{0,2},{2,0},{4,6},{6,4},{8,10},{10,8},{12,14},{14,12},{16,18},{18,... | collective-permute-start | bytes 786440 | tf_op jit(solution)/shard_map/ppermute | solution.py:48
  23.1 11.2 %collective-permute-start.8 = (bf16[2,32,2048]{2,1,0:T(8,128)(2,1)S(1)}, bf16[2,32,2048]{2,1,0:T(8,128)(2,1)S(1)}, u32[]{:S(2)}, u32[]{:S(2)}) collective-permute-start(bf16[2,32,2048]{2,1,0:T(8,128)(2,1)S(1)} %get-tuple-element.21), channel_id=1, source_target_pairs={{0,4},{2,6},{4,0},{6,2},{8,12},{10,14},{12,8},{14,10},{16,20},{18,... | collective-permute-start | bytes 786440 | tf_op jit(solution)/shard_map/ppermute | solution.py:48
  24.7 10.5 %collective-permute-start.9 = (bf16[2,32,2048]{2,1,0:T(8,128)(2,1)S(1)}, bf16[2,32,2048]{2,1,0:T(8,128)(2,1)S(1)}, u32[]{:S(2)}, u32[]{:S(2)}) collective-permute-start(bf16[2,32,2048]{2,1,0:T(8,128)(2,1)S(1)} %get-tuple-element.22), channel_id=1, source_target_pairs={{0,6},{2,4},{4,2},{6,0},{8,14},{10,12},{12,10},{14,8},{16,22},{18,... | collective-permute-start | bytes 786440 | tf_op jit(solution)/shard_map/ppermute | solution.py:48
  26.2 11.2 %copy-start.2 = (bf16[1536,1792]{1,0:T(8,128)(2,1)S(1)}, bf16[1536,1792]{1,0:T(8,128)(2,1)}, u32[]{:S(2)}) copy-start(bf16[1536,1792]{1,0:T(8,128)(2,1)} %copy-done.1) | copy-start | bytes 16515076
  29.6 33.3 %collective-permute-start = (f32[1536,256]{1,0:T(8,128)}, f32[1536,256]{1,0:T(8,128)}, u32[]{:S(2)}, u32[]{:S(2)}) collective-permute-start(f32[1536,256]{1,0:T(8,128)} %slice_select_fusion), channel_id=1, source_target_pairs={{0,1},{1,0},{2,3},{3,2},{4,5},{5,4},{6,7},{7,6},{8,9},{9,8},{10,11... | collective-permute-start | bytes 4718600 | tf_op jit(solution)/shard_map/ppermute | solution.py:54
  37.4 2.2 %collective-permute-start.12 = (f32[2,32,768]{2,1,0:T(8,128)S(1)}, f32[2,32,768]{2,1,0:T(8,128)S(1)}, u32[]{:S(2)}, u32[]{:S(2)}) collective-permute-start(f32[2,32,768]{2,1,0:T(8,128)S(1)} %fusion.15), channel_id=1, source_target_pairs={{0,1},{1,0},{2,3},{3,2},{4,5},{5,4},{6,7},{7,6},{8,9},{9,8},{10,11... | collective-permute-start | bytes 589832 | tf_op jit(solution)/shard_map/ppermute | solution.py:54
  39.1 1.6 %collective-permute-start.10 = (f32[2,32,768]{2,1,0:T(8,128)S(1)}, f32[2,32,768]{2,1,0:T(8,128)S(1)}, u32[]{:S(2)}, u32[]{:S(2)}) collective-permute-start(f32[2,32,768]{2,1,0:T(8,128)S(1)} %fusion.14), channel_id=1, source_target_pairs={{0,1},{1,0},{2,3},{3,2},{4,5},{5,4},{6,7},{7,6},{8,9},{9,8},{10,11... | collective-permute-start | bytes 589832 | tf_op jit(solution)/shard_map/ppermute | solution.py:54
  42.3 14.9 %collective-permute-start.15 = (bf16[2,32,2048]{2,1,0:T(8,128)(2,1)S(1)}, bf16[2,32,2048]{2,1,0:T(8,128)(2,1)S(1)}, u32[]{:S(2)}, u32[]{:S(2)}) collective-permute-start(bf16[2,32,2048]{2,1,0:T(8,128)(2,1)S(1)} %fusion.12), channel_id=1, source_target_pairs={{0,6},{2,4},{4,2},{6,0},{8,14},{10,12},{12,10},{14,8},{16,22},{18,... | collective-permute-start | bytes 786440 | tf_op jit(solution)/shard_map/ppermute | solution.py:48
  46.5 11.0 %collective-permute-start.14 = (bf16[2,32,2048]{2,1,0:T(8,128)(2,1)S(1)}, bf16[2,32,2048]{2,1,0:T(8,128)(2,1)S(1)}, u32[]{:S(2)}, u32[]{:S(2)}) collective-permute-start(bf16[2,32,2048]{2,1,0:T(8,128)(2,1)S(1)} %fusion.12), channel_id=1, source_target_pairs={{0,4},{2,6},{4,0},{6,2},{8,12},{10,14},{12,8},{14,10},{16,20},{18,... | collective-permute-start | bytes 786440 | tf_op jit(solution)/shard_map/ppermute | solution.py:48
  47.5 10.1 %collective-permute-start.13 = (bf16[2,32,2048]{2,1,0:T(8,128)(2,1)S(1)}, bf16[2,32,2048]{2,1,0:T(8,128)(2,1)S(1)}, u32[]{:S(2)}, u32[]{:S(2)}) collective-permute-start(bf16[2,32,2048]{2,1,0:T(8,128)(2,1)S(1)} %fusion.12), channel_id=1, source_target_pairs={{0,2},{2,0},{4,6},{6,4},{8,10},{10,8},{12,14},{14,12},{16,18},{18,... | collective-permute-start | bytes 786440 | tf_op jit(solution)/shard_map/ppermute | solution.py:48
  49.7 13.2 %copy-start.6 = (f32[1536,512]{1,0:T(8,128)S(1)}, f32[1536,512]{1,0:T(8,128)}, u32[]{:S(2)}) copy-start(f32[1536,512]{1,0:T(8,128)} %fusion.13) | copy-start | bytes 9437188
  58.4 7.3 %collective-permute-start.16 = (bf16[32,2048]{1,0:T(8,128)(2,1)S(1)}, bf16[32,2048]{1,0:T(8,128)(2,1)S(1)}, u32[]{:S(2)}, u32[]{:S(2)}) collective-permute-start(bf16[32,2048]{1,0:T(8,128)(2,1)S(1)} %get-tuple-element.25), channel_id=1, source_target_pairs={{0,8},{2,10},{4,12},{6,14},{8,0},{10,2},{12,4},{14,6},{16,24},{18,... | collective-permute-start | bytes 393224 | tf_op jit(solution)/shard_map/ppermute | solution.py:51
  59.8 12.9 %collective-permute-start.17 = (bf16[32,2048]{1,0:T(8,128)(2,1)S(1)}, bf16[32,2048]{1,0:T(8,128)(2,1)S(1)}, u32[]{:S(2)}, u32[]{:S(2)}) collective-permute-start(bf16[32,2048]{1,0:T(8,128)(2,1)S(1)} %get-tuple-element.26), channel_id=1, source_target_pairs={{0,16},{2,18},{4,20},{6,22},{8,24},{10,26},{12,28},{14,30},{16,0},... | collective-permute-start | bytes 393224 | tf_op jit(solution)/shard_map/ppermute | solution.py:51
  62.7 1.9 %copy-start.7 = (f32[2,768,256]{2,1,0:T(8,128)S(1)}, f32[2,768,256]{2,1,0:T(8,128)}, u32[]{:S(2)}) copy-start(f32[2,768,256]{2,1,0:T(8,128)} %fusion.9) | copy-start | bytes 4718596
  62.7 10.0 %collective-permute-start.18 = (bf16[32,2048]{1,0:T(8,128)(2,1)S(1)}, bf16[32,2048]{1,0:T(8,128)(2,1)S(1)}, u32[]{:S(2)}, u32[]{:S(2)}) collective-permute-start(bf16[32,2048]{1,0:T(8,128)(2,1)S(1)} %get-tuple-element.27), channel_id=1, source_target_pairs={{0,24},{2,26},{4,28},{6,30},{8,16},{10,18},{12,20},{14,22},{16,8},... | collective-permute-start | bytes 393224 | tf_op jit(solution)/shard_map/ppermute | solution.py:51

commit v3 on v2

v3 whole, which is shorter than its diff:
```python
import math

import jax
import jax.numpy as jnp
from jax import lax
from jax.experimental import pallas as pl
from jax.experimental.pallas import tpu as pltpu
from jax.sharding import PartitionSpec as P


HIGH = lax.Precision.HIGHEST
F32 = jnp.float32
BF16 = jnp.bfloat16


def inner_size(n):
    return max(q for q in range(1, n + 1) if n % q == 0 and q * q <= n)


def peer(i, d, n):
    return i ^ d if n & (n - 1) == 0 else (i + d) % n


def offset(dst, src, n):
    return dst ^ src if n & (n - 1) == 0 else (dst - src) % n


SMEM = pl.BlockSpec(memory_space=pltpu.SMEM)
VMEM = pl.BlockSpec(memory_space=pltpu.VMEM)
SMALL = pltpu.CompilerParams(vmem_limit_bytes=8 << 20)


def fixed(x):
    return pltpu.with_memory_space_constraint(x, pltpu.HBM)


def kernel_call(body, ints, arrays, outs, scratch=(), inside=True):
    arrays = [pltpu.with_memory_space_constraint(a, pltpu.VMEM) for a in arrays]
    return pl.pallas_call(
        body,
        out_shape=[pltpu.VMEM(o.shape, o.dtype) if inside else o for o in outs],
        in_specs=[SMEM] * len(ints) + [VMEM] * len(arrays),
        out_specs=[VMEM] * len(outs),
        scratch_shapes=list(scratch),
        compiler_params=SMALL,
    )(*ints, *arrays)


def program(n, m):
    q = inner_size(n)
    r = n // q

    def send_inner(x, d):
        return lax.ppermute(x, "dp", [(i, i // q * q + peer(i % q, d, q)) for i in range(n)])

    def send_outer(x, d):
        return lax.ppermute(x, "dp", [(i, peer(i // q, d, r) * q + i % q) for i in range(n)])

    def swap(x):
        return lax.ppermute(x, "mp", [(0, 1), (1, 0)])

    def mp_sum(x):
        return x + swap(x) if m == 2 else lax.psum(x, "mp")

    def opposite(d, size):
        return d if size & (size - 1) == 0 else (size - d) % size

    def local(hidden, weight, down, up, grad, tenant, table):
        seqs = tenant.shape[0]
        rows, width = hidden.shape
        rank = down.shape[2]
        cols = grad.shape[1]
        length = rows // seqs
        block = math.gcd(length, 384)
        me = lax.axis_index("dp").astype(jnp.int32)[None]
        core = lax.axis_index("mp").astype(jnp.int32)[None]
        low_core = lax.axis_index("mp") == 0
        me, core, low_core, down, up, tenant = lax.optimization_barrier((me, core, low_core, down, up, tenant))

        first = max(width - cols, 256) // 256 * 128
        rest = width - first

        def join(down_ref, up_ref, out0, out1):
            out0[:, :first] = down_ref[:, :first]
            out0[:, first:] = up_ref[...]
            out1[...] = down_ref[:, first:]

        mine = pl.pallas_call(
            join,
            out_shape=[pltpu.VMEM((rank, first + cols), BF16), pltpu.VMEM((rank, rest), BF16)],
            compiler_params=SMALL,
            name="join",
        )(
            fixed(jnp.swapaxes(down[0], 0, 1)),
            fixed(up[0]),
        )
        held, tenants = [[mine[0]], [mine[1]]], [tenant]
        for p in range(2):
            for d in range(1, r):
                held[p].append(send_outer(mine[p], d))
        for d in range(1, q):
            tenants.append(send_inner(tenant, d))
        ints = [me, fixed(table), fixed(tenant)] + tenants[1:]

        def load(x_ref, g_ref, x_out, g_out, sems):
            copies = [
                pltpu.make_async_copy(x_ref, x_out, sems.at[0]),
                pltpu.make_async_copy(g_ref, g_out, sems.at[1]),
            ]
            for c in copies:
                c.start()
            for c in copies:
                c.wait()

        hidden, grad_in = pl.pallas_call(
            load,
            out_shape=[pltpu.VMEM(hidden.shape, BF16), pltpu.VMEM(grad.shape, BF16)],
            in_specs=[pl.BlockSpec(memory_space=pl.ANY)] * 2,
            out_specs=[VMEM] * 2,
            scratch_shapes=[pltpu.SemaphoreType.DMA((2,))],
            compiler_params=SMALL,
            name="load",
        )(fixed(hidden), fixed(grad))

        def slot(refs, d, j):
            return refs[1][refs[2 + d][j]]

        def pick(*refs):
            ins, parts, outs = refs[: 2 + q], refs[2 + q : 2 + q + r], refs[2 + q + r :]
            outer = ins[0][0] // q
            for d in range(1, q):
                for j in range(seqs):
                    have = offset(outer, slot(ins, opposite(d, q), j) // q, r)
                    for k in range(r):

                        @pl.when(have == k)
                        def _(d=d, j=j, k=k):
                            outs[d - 1][j] = parts[k][...]

        got = []
        for p in range(2):
            sent = kernel_call(pick, ints, held[p], [jax.ShapeDtypeStruct((seqs,) + held[p][0].shape, BF16)] * (q - 1))
            got.append([])
            for d in range(1, q):
                got[p].append(send_inner(sent[d - 1], d))

        def chosen(refs, store):
            ins, parts, gots = refs[: 2 + q], refs[2 + q : 2 + q + r], refs[2 + q + r : 1 + 2 * q + r]
            inner, outer = ins[0][0] % q, ins[0][0] // q
            for j in range(seqs):
                wanted = slot(ins, 0, j)
                way = offset(inner, wanted % q, q)
                have = offset(outer, wanted // q, r)
                for d in range(1, q):

                    @pl.when(way == d)
                    def _(d=d, j=j):
                        store(j, gots[d - 1].at[j])

                for k in range(r):

                    @pl.when((way == 0) & (have == k))
                    def _(j=j, k=k):
                        store(j, parts[k])

        def choose0(*refs):
            down_out, up_out = refs[-2:]

            def store(j, ref):
                down_out[j] = ref[:, :first]
                up_out[j] = ref[:, first:]

            chosen(refs, store)

        def choose1(*refs):
            down_in, down_out = refs[-2:]
            down_out[:, :, :first] = down_in[...]

            def store(j, ref):
                down_out[j, :, first:] = ref[...]

            chosen(refs, store)

        down_first, up_s = kernel_call(
            choose0,
            ints,
            held[0] + got[0],
            [jax.ShapeDtypeStruct((seqs, rank, first), BF16), jax.ShapeDtypeStruct((seqs, rank, cols), BF16)],
        )
        (down_s,) = kernel_call(
            choose1, ints, held[1] + got[1] + [down_first], [jax.ShapeDtypeStruct((seqs, rank, width), BF16)]
        )

        h3 = hidden.reshape(seqs, length, width)
        g3 = grad_in.reshape(seqs, length, cols)
        if m == 2:
            other = swap(grad_in)
        else:
            grad_full = lax.all_gather(grad, "mp", axis=1, tiled=True)
        base = []
        for j in range(seqs):
            base.append(jnp.dot(h3[j], weight, preferred_element_type=F32))
        base = jnp.concatenate(base)
        if m == 2:
            theirs = jnp.where(low_core, base[:, cols:], base[:, :cols])
            ours = jnp.where(low_core, base[:, :cols], base[:, cols:])
            base_got = swap(theirs)
            base_own = ours + base_got
        else:
            base_own = lax.psum_scatter(base, "mp", scatter_dimension=1, tiled=True)

        back_low = mp_sum(jnp.einsum("slk,srk->srl", g3, up_s, preferred_element_type=F32)).astype(BF16)
        low = mp_sum(jnp.einsum("slw,srw->srl", h3, down_s, preferred_element_type=F32))
        up_f = up_s.astype(F32)
        values = (base_own.reshape(seqs, length, cols) + jnp.einsum("srl,srk->slk", low, up_f, precision=HIGH)).astype(BF16)
        up_seq = jnp.einsum("srl,slk->srk", low, g3.astype(F32), precision=HIGH)
        down_seq = jnp.einsum("srl,slw->srw", back_low, h3, preferred_element_type=F32)
        if m == 2:
            per = length // block

            def widen(core_ref, own, mate, w, coeff, factor, out):
                def part(x, half):
                    at = pl.multiple_of(half * cols, math.gcd(cols, 128))
                    return lax.dot_general(
                        x[...], w[:, pl.ds(at, cols)], (((1,), (1,)), ((), ())), preferred_element_type=F32
                    )

                total = part(own, core_ref[0]) + part(mate, 1 - core_ref[0])
                total += lax.dot_general(
                    coeff[0], factor[0], (((0,), (0,)), ((), ())), preferred_element_type=F32
                )
                out[...] = total.astype(BF16)

            rows_of = pl.BlockSpec((block, cols), lambda i: (i, 0))
            hidden_grad = pl.pallas_call(
                widen,
                grid=(rows // block,),
                out_shape=jax.ShapeDtypeStruct((rows, width), BF16),
                in_specs=[
                    SMEM,
                    rows_of,
                    rows_of,
                    pl.BlockSpec((width, m * cols), lambda i: (0, 0)),
                    pl.BlockSpec((1, rank, block), lambda i: (i // per, 0, i % per)),
                    pl.BlockSpec((1, rank, width), lambda i: (i // per, 0, 0)),
                ],
                out_specs=pl.BlockSpec((block, width), lambda i: (i, 0)),
                compiler_params=pltpu.CompilerParams(vmem_limit_bytes=24 << 20),
                name="widen",
            )(core, grad_in, other, weight, back_low, down_s)
        else:
            hidden_grad = (
                lax.dot_general(grad_full, weight, (((1,), (1,)), ((), ())), preferred_element_type=F32)
                + jnp.einsum("srl,srw->slw", back_low, down_s, preferred_element_type=F32).reshape(rows, width)
            ).astype(BF16)

        items = [down_seq[:, :, :rest], jnp.concatenate([down_seq[:, :, rest:], up_seq], axis=2)]
        near = [[], []]
        for p in range(2):
            small = items[p].astype(BF16)
            for d in range(1, q):
                near[p].append(send_inner(small, d))

        def gather_items(*refs):
            ins, own, others = refs[: 2 + q], refs[2 + q : 4 + q], refs[4 + q : 2 + 3 * q]
            outs, acc = refs[2 + 3 * q : -1], refs[-1]
            inner, outer = ins[0][0] % q, ins[0][0] // q
            acc[...] = jnp.zeros_like(acc)
            for d in range(q):
                for j in range(seqs):
                    holder = slot(ins, d, j)

                    @pl.when(holder % q == inner)
                    def _(d=d, j=j, holder=holder):
                        k = offset(outer, holder // q, r)
                        for p, at in ((0, slice(0, rest)), (1, slice(rest, None))):
                            piece = own[p] if d == 0 else others[p * (q - 1) + d - 1]
                            acc[k, :, at] += piece[j].astype(F32)

            outs[0][...] = acc[0]
            for k in range(1, r):
                outs[k][...] = acc[k].astype(BF16)

        shape = (rank, width + cols)
        parts = kernel_call(
            gather_items,
            ints,
            items + near[0] + near[1],
            [jax.ShapeDtypeStruct(shape, F32)] + [jax.ShapeDtypeStruct(shape, BF16)] * (r - 1),
            [pltpu.VMEM((r,) + shape, F32)],
        )
        arrived = []
        for k in range(1, r):
            arrived.append(send_outer(parts[k], opposite(k, r)))
        values, hidden_grad, arrived = lax.optimization_barrier((values, hidden_grad, arrived))

        def finish(*refs):
            others, down_out, up_out = refs[:r], refs[r], refs[r + 1]
            total = others[0][...]
            for other in others[1:]:
                total = total + other[...].astype(F32)
            down_out[...] = total[:, :width]
            up_out[...] = total[:, width:]

        down_grad, up_grad = kernel_call(
            finish,
            [],
            [parts[0]] + arrived,
            [jax.ShapeDtypeStruct((rank, width), F32), jax.ShapeDtypeStruct((rank, cols), F32)],
            inside=False,
        )
        down_grad = jnp.swapaxes(down_grad, 0, 1)[None]
        return values.reshape(rows, cols), hidden_grad, down_grad, up_grad[None]

    return local


def solution(mesh):
    n, m = mesh.shape["dp"], mesh.shape["mp"]
    return jax.shard_map(
        program(n, m),
        mesh=mesh,
        in_specs=(
            P("dp", "mp"),
            P("mp", None),
            P("dp", "mp", None),
            P("dp", None, "mp"),
            P("dp", "mp"),
            P("dp"),
            P(),
        ),
        out_specs=(P("dp", "mp"), P("dp", "mp"), P("dp", "mp", None), P("dp", None, "mp")),
        check_vma=False,
    )
```

time: 73.7 us -> 78.2 us (1.061)
  matrix products: 21.7 us -> 7.5 us
  starting transfers between devices: 21.6 us -> 33.3 us
  Pallas kernels: 4.32 us -> 15 us
  other arithmetic: 6.25 us -> 1.6 us
  waiting for transfers between devices: 16.2 us -> 19.6 us
  local copies, waits for them, and re-layouts: 2.6 us -> 0.07 us
    dot_general x3 -> x2, matrix products: 13.8 us -> 3.15 us  [local(): base.append(jnp.dot(h3[j], weight, preferred_element_type=F32))]
    pallas_call x2 -> x3, Pallas kernels: 1.28 us -> 9.97 us  [the longest x1 6.29 us: local(): pl.pallas_call(widen, grid=(rows // block,), out_shape=jax.ShapeDtypeStru...]
    ppermute x9 -> x15, waiting for transfers between devices: 9.19 us -> 17.7 us  [send_inner(): lax.ppermute(x, 'dp', [(i, i // q * q + peer(i % q, d, q)) for i in range...]
    ppermute x6 -> x9, starting transfers between devices: 8.9 us -> 14.9 us  [send_outer(): lax.ppermute(x, 'dp', [(i, peer(i // q, d, r) * q + i % q) for i in range...]
    ppermute x9 -> x15, starting transfers between devices: 12.1 us -> 17.8 us  [send_inner(): lax.ppermute(x, 'dp', [(i, i // q * q + peer(i % q, d, q)) for i in range...]
    ppermute x6 -> x9, waiting for transfers between devices: 7.02 us -> 1.88 us  [send_outer(): lax.ppermute(x, 'dp', [(i, peer(i // q, d, r) * q + i % q) for i in range...]
    select_n x1, other arithmetic: 3.39 us -> 0.2 us  [local(): theirs = jnp.where(low_core, base[:, cols:], base[:, :cols])]
    unnamed x16 -> x4, local copies, waits for them, and re-layouts: 2.6 us -> 0.01 us
  transfers between devices with their start and end apart: 19 -> 28, of which waited for: 8 -> 10; matrix products, arithmetic and copies ran while one was open for 38% -> 12% of each run, Pallas kernels for 5% -> 17%
where the time goes in v3:
time: 78.2 us; the launch traced here: 77.9 us
  starting transfers between devices  33.3 us (43%)
  waiting for transfers between devices  19.6 us (25%)
  Pallas kernels  15 us (19%)
  matrix products  7.5 us (10%)
  other arithmetic  1.6 us (2%)
  between operations  0.88 us (1%)
    ppermute x15, starting transfers between devices, send_inner(): lax.ppermute(x, 'dp', [(i, i // q * q + peer(i % q, d, q)) for i in range...  17.8 us
    ppermute x15, waiting for transfers between devices, send_inner(): lax.ppermute(x, 'dp', [(i, i // q * q + peer(i % q, d, q)) for i in range...  17.7 us
    ppermute x9, starting transfers between devices, send_outer(): lax.ppermute(x, 'dp', [(i, peer(i // q, d, r) * q + i % q) for i in range...  14.9 us
    pallas_call x1, Pallas kernels, local(): pl.pallas_call(widen, grid=(rows // block,), out_shape=jax.ShapeDtypeStru...  6.29 us
    pallas_call x6, Pallas kernels, kernel_call(): pl.pallas_call(body, out_shape=[pltpu.VMEM(o.shape, o.dtype) if inside el...  5.02 us
    dot_general x2, matrix products, local(): base.append(jnp.dot(h3[j], weight, preferred_element_type=F32))  3.15 us
    pallas_call x1, Pallas kernels, local(): pl.pallas_call(load, out_shape=[pltpu.VMEM(hidden.shape, BF16), pltpu.VME...  2.77 us
    ppermute x9, waiting for transfers between devices, send_outer(): lax.ppermute(x, 'dp', [(i, peer(i // q, d, r) * q + i % q) for i in range...  1.88 us
  transfers between devices with their start and end apart: 28, of which 10 were waited for; matrix products, arithmetic and copies ran while one was open for 12% of the time, Pallas kernels for 17%

profile of v3, /device:TPU:0, one launch (start us, length us, event | category | flops | bytes accessed | tf_op | source)
XLA Modules:
  0.0 77.9 jit_solution(5142119836533223375)
XLA Ops:
  0.6 0.9 %join.1 = (bf16[32,1024]{1,0:T(8,128)(2,1)S(1)}, bf16[32,1024]{1,0:T(8,128)(2,1)S(1)}) custom-call(bf16[32,1792]{1,0:T(8,128)(2,1)} %bitcast.30, bf16[32,256]{1,0:T(8,128)(2,1)} %bitcast.31), custom_call_target="tpu_custom_call" | custom-call | tf_op jit(solution)/shard_map/join/pallas_call | solution.py:88
  1.6 5.1 %collective-permute-start.12 = (bf16[32,1024]{1,0:T(8,128)(2,1)S(1)}, bf16[32,1024]{1,0:T(8,128)(2,1)S(1)}, u32[]{:S(2)}, u32[]{:S(2)}) collective-permute-start(bf16[32,1024]{1,0:T(8,128)(2,1)S(1)} %get-tuple-element.43.refs_6_), channel_id=1, source_target_pairs={{0,24},{2,26},{4,28},{6,30},{8,16},{10,18},{12,20},{14,22},{16,8},... | collective-permute-start | bytes 196616 | tf_op jit(solution)/shard_map/ppermute | solution.py:57
  6.7 0.6 collective-permute-start.10
  7.3 2.6 %collective-permute-start.3 = (s32[2]{0:T(128)}, s32[2]{0:T(128)S(1)}, u32[]{:S(2)}, u32[]{:S(2)}) collective-permute-start(s32[2]{0:T(128)} %refs_2_.4), channel_id=1, source_target_pairs={{0,6},{2,4},{4,2},{6,0},{8,14},{10,12},{12,10},{14,8},{16,22},{18,... | collective-permute-start | bytes 32 | tf_op jit(solution)/shard_map/ppermute | solution.py:54
  9.9 3.6 %collective-permute-start.6 = (bf16[32,1024]{1,0:T(8,128)(2,1)S(1)}, bf16[32,1024]{1,0:T(8,128)(2,1)S(1)}, u32[]{:S(2)}, u32[]{:S(2)}) collective-permute-start(bf16[32,1024]{1,0:T(8,128)(2,1)S(1)} %get-tuple-element.39.refs_6_), channel_id=1, source_target_pairs={{0,24},{2,26},{4,28},{6,30},{8,16},{10,18},{12,20},{14,22},{16,8},... | collective-permute-start | bytes 196616 | tf_op jit(solution)/shard_map/ppermute | solution.py:57
  13.5 2.8 %load.1 = (bf16[1536,1792]{1,0:T(8,128)(2,1)S(1)}, bf16[1536,256]{1,0:T(8,128)(2,1)S(1)}) custom-call(bf16[1536,1792]{1,0:T(8,128)(2,1)} %x_ref.1, bf16[1536,256]{1,0:T(8,128)(2,1)} %g_ref.1), custom_call_target="tpu_custom_call" | custom-call | tf_op jit(solution)/shard_map/load/pallas_call | solution.py:115
  16.3 1.6 %fusion = f32[768,512]{1,0:T(8,128)S(1)} fusion(bf16[1792,512]{1,0:T(8,128)(2,1)S(1)} %copy-done, bf16[1536,1792]{1,0:T(8,128)(2,1)S(1)} %get-tuple-element.34), kind=kOutput, calls=%fused_computation.2 | convolution fusion | flops 1409286144 | bytes 6160384 | tf_op jit(solution)/shard_map/dot_general | solution.py:202
  17.9 1.6 %fusion.2 = f32[768,512]{1,0:T(8,128)S(1)} fusion(bf16[1792,512]{1,0:T(8,128)(2,1)S(1)} %copy-done, bf16[1536,1792]{1,0:T(8,128)(2,1)S(1)} %get-tuple-element.34), kind=kOutput, calls=%fused_computation.4 | convolution fusion | flops 1409286144 | bytes 6160384 | tf_op jit(solution)/shard_map/dot_general | solution.py:202
  19.5 0.6 collective-permute-start.2
  20.1 3.1 %collective-permute-done.2.refs_4_ = s32[2]{0:T(128)S(1)} collective-permute-done((s32[2]{0:T(128)S(1)}, s32[2]{0:T(128)S(1)}, u32[]{:S(2)}, u32[]{:S(2)}) %collective-permute-start.2) | collective-permute-done | bytes 40 | tf_op jit(solution)/shard_map/ppermute | solution.py:54
  23.1 0.5 collective-permute-start.1
  23.7 3.0 %collective-permute-done.1.refs_3_ = s32[2]{0:T(128)S(1)} collective-permute-done((s32[2]{0:T(128)S(1)}, s32[2]{0:T(128)S(1)}, u32[]{:S(2)}, u32[]{:S(2)}) %collective-permute-start.1) | collective-permute-done | bytes 40 | tf_op jit(solution)/shard_map/ppermute | solution.py:54
  26.7 1.1 %collective-permute-start.4 = (bf16[32,1024]{1,0:T(8,128)(2,1)S(1)}, bf16[32,1024]{1,0:T(8,128)(2,1)S(1)}, u32[]{:S(2)}, u32[]{:S(2)}) collective-permute-start(bf16[32,1024]{1,0:T(8,128)(2,1)S(1)} %get-tuple-element.39.refs_6_), channel_id=1, source_target_pairs={{0,8},{2,10},{4,12},{6,14},{8,0},{10,2},{12,4},{14,6},{16,24},{18,... | collective-permute-start | bytes 196616 | tf_op jit(solution)/shard_map/ppermute | solution.py:57
  27.8 0.9 %shard_map.103 = (bf16[2,32,1024]{2,1,0:T(8,128)(2,1)S(1)}, bf16[2,32,1024]{2,1,0:T(8,128)(2,1)S(1)}, bf16[2,32,1024]{2,1,0:T(8,128)(2,1)S(1)}) custom-call(s32[1]{0:T(128)} %bitcast.refs_0_, s32[16]{0:T(128)} %refs_1_.9, s32[2]{0:T(128)} %refs_2_.4, s32[2]{0:T(128)S(1)} %collective-permute-done.1.refs_3_, s32[2]{0:T(128)S(1)} %collective-permute-done.2.refs_4_, ...), custom_call_target="tpu_custom_call" | custom-call | tf_op jit(solution)/shard_map/pallas_call | solution.py:39
  28.7 0.6 collective-permute-start.13
  29.3 0.5 collective-permute-start.14
  29.8 2.4 %collective-permute-start.15 = (bf16[2,32,1024]{2,1,0:T(8,128)(2,1)S(1)}, bf16[2,32,1024]{2,1,0:T(8,128)(2,1)S(1)}, u32[]{:S(2)}, u32[]{:S(2)}) collective-permute-start(bf16[2,32,1024]{2,1,0:T(8,128)(2,1)S(1)} %get-tuple-element.46), channel_id=1, source_target_pairs={{0,6},{2,4},{4,2},{6,0},{8,14},{10,12},{12,10},{14,8},{16,22},{18,... | collective-permute-start | bytes 393224 | tf_op jit(solution)/shard_map/ppermute | solution.py:54
  32.6 0.5 collective-permute-start
  33.1 0.9 %shard_map.102 = (bf16[2,32,1024]{2,1,0:T(8,128)(2,1)S(1)}, bf16[2,32,1024]{2,1,0:T(8,128)(2,1)S(1)}, bf16[2,32,1024]{2,1,0:T(8,128)(2,1)S(1)}) custom-call(s32[1]{0:T(128)} %bitcast.refs_0_, s32[16]{0:T(128)} %refs_1_.9, s32[2]{0:T(128)} %refs_2_.4, s32[2]{0:T(128)S(1)} %collective-permute-done.1.refs_3_, s32[2]{0:T(128)S(1)} %collective-permute-done.2.refs_4_, ...), custom_call_target="tpu_custom_call" | custom-call | tf_op jit(solution)/shard_map/pallas_call | solution.py:39
  34.0 0.6 collective-permute-start.7
  34.6 0.5 collective-permute-start.8
  35.1 0.6 collective-permute-done.15.refs_12_
  35.7 2.4 %collective-permute-start.9 = (bf16[2,32,1024]{2,1,0:T(8,128)(2,1)S(1)}, bf16[2,32,1024]{2,1,0:T(8,128)(2,1)S(1)}, u32[]{:S(2)}, u32[]{:S(2)}) collective-permute-start(bf16[2,32,1024]{2,1,0:T(8,128)(2,1)S(1)} %get-tuple-element.42), channel_id=1, source_target_pairs={{0,6},{2,4},{4,2},{6,0},{8,14},{10,12},{12,10},{14,8},{16,22},{18,... | collective-permute-start | bytes 393224 | tf_op jit(solution)/shard_map/ppermute | solution.py:54
  38.2 0.8 %shard_map.104 = (bf16[2,32,768]{2,1,0:T(8,128)(2,1)S(1)}, bf16[2,32,256]{2,1,0:T(8,128)(2,1)S(1)}) custom-call(s32[1]{0:T(128)} %bitcast.refs_0_, s32[16]{0:T(128)} %refs_1_.9, s32[2]{0:T(128)} %refs_2_.4, s32[2]{0:T(128)S(1)} %collective-permute-done.1.refs_3_, s32[2]{0:T(128)S(1)} %collective-permute-done.2.refs_4_, s32[2]{0:T(128)S(1)} %collective-permute-done.3.refs_5_, ...), custom_call_target="tpu_custom_call" | custom-call | tf_op jit(solution)/shard_map/pallas_call | solution.py:39
  39.3 1.1 %collective-permute-done.7.refs_10_ = bf16[2,32,1024]{2,1,0:T(8,128)(2,1)S(1)} collective-permute-done((bf16[2,32,1024]{2,1,0:T(8,128)(2,1)S(1)}, bf16[2,32,1024]{2,1,0:T(8,128)(2,1)S(1)}, u32[]{:S(2)}, u32[]{:S(2)}) %collective-permute-start.7) | collective-permute-done | bytes 131104 | tf_op jit(solution)/shard_map/ppermute | solution.py:54
  40.4 2.2 %collective-permute-done.8.refs_11_ = bf16[2,32,1024]{2,1,0:T(8,128)(2,1)S(1)} collective-permute-done((bf16[2,32,1024]{2,1,0:T(8,128)(2,1)S(1)}, bf16[2,32,1024]{2,1,0:T(8,128)(2,1)S(1)}, u32[]{:S(2)}, u32[]{:S(2)}) %collective-permute-start.8) | collective-permute-done | bytes 131104 | tf_op jit(solution)/shard_map/ppermute | solution.py:54
  42.6 0.8 %shard_map.105.factor = bf16[2,32,1792]{2,1,0:T(8,128)(2,1)S(1)} custom-call(s32[1]{0:T(128)} %bitcast.refs_0_, s32[16]{0:T(128)} %refs_1_.9, s32[2]{0:T(128)} %refs_2_.4, s32[2]{0:T(128)S(1)} %collective-permute-done.1.refs_3_, s32[2]{0:T(128)S(1)} %collective-permute-done.2.refs_4_, s32[2]{0:T(128)S(1)} %collective-permute-done.3.refs_5_, ...), custom_call_target="tpu_custom_call" | custom-call | tf_op jit(solution)/shard_map/pallas_call | solution.py:39
  43.4 1.7 %fusion.10 = f32[2,32,768]{2,1,0:T(8,128)S(1)} fusion(bf16[2,32,1792]{2,1,0:T(8,128)(2,1)S(1)} %shard_map.105.factor, bf16[2,768,1792]{2,1,0:T(8,128)(2,1)S(1)} %bitcast.24), kind=kOutput, calls=%fused_computation.19 | convolution fusion | flops 176160768 | bytes 5931008 | tf_op jit(solution)/shard_map/slw,srw->srl/dot_general | solution.py:213
  45.1 1.0 %fusion.12 = f32[2,32,1792]{2,1,0:T(8,128)S(1)} fusion(bf16[2,32,768]{2,1,0:T(8,128)(2,1)S(1)} %add_convert_fusion.1.coeff, bf16[2,768,1792]{2,1,0:T(8,128)(2,1)S(1)} %bitcast.25), kind=kOutput, calls=%fused_computation.21 | convolution fusion | flops 176160768 | bytes 6062080 | tf_op jit(solution)/shard_map/srl,slw->srw/dot_general | solution.py:217
  46.2 1.5 %collective-permute-start.21 = (bf16[2,32,1024]{2,1,0:T(8,128)(2,1)S(1)}, bf16[2,32,1024]{2,1,0:T(8,128)(2,1)S(1)}, u32[]{:S(2)}, u32[]{:S(2)}) collective-permute-start(bf16[2,32,1024]{2,1,0:T(8,128)(2,1)S(1)} %slice.51), channel_id=1, source_target_pairs={{0,6},{2,4},{4,2},{6,0},{8,14},{10,12},{12,10},{14,8},{16,22},{18,... | collective-permute-start | bytes 393224 | tf_op jit(solution)/shard_map/ppermute | solution.py:54
  47.7 1.5 %collective-permute-start.20 = (bf16[2,32,1024]{2,1,0:T(8,128)(2,1)S(1)}, bf16[2,32,1024]{2,1,0:T(8,128)(2,1)S(1)}, u32[]{:S(2)}, u32[]{:S(2)}) collective-permute-start(bf16[2,32,1024]{2,1,0:T(8,128)(2,1)S(1)} %slice.51), channel_id=1, source_target_pairs={{0,4},{2,6},{4,0},{6,2},{8,12},{10,14},{12,8},{14,10},{16,20},{18,... | collective-permute-start | bytes 393224 | tf_op jit(solution)/shard_map/ppermute | solution.py:54
  49.2 0.5 collective-permute-start.19
  50.3 3.3 %collective-permute-done.21.refs_10_ = bf16[2,32,1024]{2,1,0:T(8,128)(2,1)S(1)} collective-permute-done((bf16[2,32,1024]{2,1,0:T(8,128)(2,1)S(1)}, bf16[2,32,1024]{2,1,0:T(8,128)(2,1)S(1)}, u32[]{:S(2)}, u32[]{:S(2)}) %collective-permute-start.21) | collective-permute-done | bytes 131104 | tf_op jit(solution)/shard_map/ppermute | solution.py:54
  53.6 1.4 %collective-permute-start.24 = (bf16[2,32,1024]{2,1,0:T(8,128)(2,1)S(1)}, bf16[2,32,1024]{2,1,0:T(8,128)(2,1)S(1)}, u32[]{:S(2)}, u32[]{:S(2)}) collective-permute-start(bf16[2,32,1024]{2,1,0:T(8,128)(2,1)S(1)} %fusion.9), channel_id=1, source_target_pairs={{0,6},{2,4},{4,2},{6,0},{8,14},{10,12},{12,10},{14,8},{16,22},{18,... | collective-permute-start | bytes 393224 | tf_op jit(solution)/shard_map/ppermute | solution.py:54
  55.0 0.9 %collective-permute-done.20.refs_9_ = bf16[2,32,1024]{2,1,0:T(8,128)(2,1)S(1)} collective-permute-done((bf16[2,32,1024]{2,1,0:T(8,128)(2,1)S(1)}, bf16[2,32,1024]{2,1,0:T(8,128)(2,1)S(1)}, u32[]{:S(2)}, u32[]{:S(2)}) %collective-permute-start.20) | collective-permute-done | bytes 131104 | tf_op jit(solution)/shard_map/ppermute | solution.py:54
  55.9 1.2 %collective-permute-start.23 = (bf16[2,32,1024]{2,1,0:T(8,128)(2,1)S(1)}, bf16[2,32,1024]{2,1,0:T(8,128)(2,1)S(1)}, u32[]{:S(2)}, u32[]{:S(2)}) collective-permute-start(bf16[2,32,1024]{2,1,0:T(8,128)(2,1)S(1)} %fusion.9), channel_id=1, source_target_pairs={{0,4},{2,6},{4,0},{6,2},{8,12},{10,14},{12,8},{14,10},{16,20},{18,... | collective-permute-start | bytes 393224 | tf_op jit(solution)/shard_map/ppermute | solution.py:54
  57.1 0.8 %collective-permute-start.22 = (bf16[2,32,1024]{2,1,0:T(8,128)(2,1)S(1)}, bf16[2,32,1024]{2,1,0:T(8,128)(2,1)S(1)}, u32[]{:S(2)}, u32[]{:S(2)}) collective-permute-start(bf16[2,32,1024]{2,1,0:T(8,128)(2,1)S(1)} %fusion.9), channel_id=1, source_target_pairs={{0,2},{2,0},{4,6},{6,4},{8,10},{10,8},{12,14},{14,12},{16,18},{18,... | collective-permute-start | bytes 393224 | tf_op jit(solution)/shard_map/ppermute | solution.py:54
  57.9 0.8 %fusion.7 = f32[2,768,256]{2,1,0:T(8,128)S(1)} fusion(bf16[2,32,256]{2,1,0:T(8,128)(2,1)S(1)} %get-tuple-element.48, f32[2,32,768]{2,1,0:T(8,128)S(1)} %fusion.10, f32[2,32,768]{2,1,0:T(8,128)S(1)} %collective-permute-done.16), kind=kOutput, calls=%fused_computation.15 | convolution fusion | flops 151044096 | bytes 1998848 | tf_op jit(solution)/shard_map/srl,srk->slk/dot_general | solution.py:215
  58.8 0.8 collective-permute-done.24.refs_13_
  59.6 2.7 %collective-permute-done.23.refs_12_ = bf16[2,32,1024]{2,1,0:T(8,128)(2,1)S(1)} collective-permute-done((bf16[2,32,1024]{2,1,0:T(8,128)(2,1)S(1)}, bf16[2,32,1024]{2,1,0:T(8,128)(2,1)S(1)}, u32[]{:S(2)}, u32[]{:S(2)}) %collective-permute-start.23) | collective-permute-done | bytes 131104 | tf_op jit(solution)/shard_map/ppermute | solution.py:54
  62.3 1.0 %shard_map.106 = (f32[32,2048]{1,0:T(8,128)S(1)}, bf16[32,2048]{1,0:T(8,128)(2,1)S(1)}, bf16[32,2048]{1,0:T(8,128)(2,1)S(1)}, bf16[32,2048]{1,0:T(8,128)(2,1)S(1)}) custom-call(s32[1]{0:T(128)} %bitcast.refs_0_, s32[16]{0:T(128)} %refs_1_.9, s32[2]{0:T(128)} %refs_2_.4, s32[2]{0:T(128)S(1)} %collective-permute-done.1.refs_3_, ...), custom_call_target="tpu_custom_call" | custom-call | tf_op jit(solution)/shard_map/pallas_call | solution.py:39
  63.2 1.0 %collective-permute-start.25 = (bf16[32,2048]{1,0:T(8,128)(2,1)S(1)}, bf16[32,2048]{1,0:T(8,128)(2,1)S(1)}, u32[]{:S(2)}, u32[]{:S(2)}) collective-permute-start(bf16[32,2048]{1,0:T(8,128)(2,1)S(1)} %get-tuple-element.51), channel_id=1, source_target_pairs={{0,8},{2,10},{4,12},{6,14},{8,0},{10,2},{12,4},{14,6},{16,24},{18,... | collective-permute-start | bytes 393224 | tf_op jit(solution)/shard_map/ppermute | solution.py:57
  64.3 2.9 %collective-permute-start.26 = (bf16[32,2048]{1,0:T(8,128)(2,1)S(1)}, bf16[32,2048]{1,0:T(8,128)(2,1)S(1)}, u32[]{:S(2)}, u32[]{:S(2)}) collective-permute-start(bf16[32,2048]{1,0:T(8,128)(2,1)S(1)} %get-tuple-element.52), channel_id=1, source_target_pairs={{0,16},{2,18},{4,20},{6,22},{8,24},{10,26},{12,28},{14,30},{16,0},... | collective-permute-start | bytes 393224 | tf_op jit(solution)/shard_map/ppermute | solution.py:57
  67.2 0.5 collective-permute-start.27
  67.7 6.3 %widen.1 = bf16[1536,1792]{1,0:T(8,128)(2,1)} custom-call(s32[1]{0:T(128)} %bitcast.1.core_ref, bf16[1536,256]{1,0:T(8,128)(2,1)S(1)} %get-tuple-element.50.own, bf16[1536,256]{1,0:T(8,128)(2,1)S(1)} %collective-permute-done.17.mate, bf16[1792,512]{1,0:T(8,128)(2,1)S(1)} %copy-done, bf16[2,32,768]{2,1,0:T(8,128)(2,1)S(1)} %add_convert_fusion.1.coeff, ...), custom_call_target="tpu_custom_call" | custom-call | tf_op jit(solution)/shard_map/widen/pallas_call | solution.py:235
  74.3 1.0 %add_convert_fusion = bf16[2,768,256]{2,1,0:T(8,128)(2,1)} fusion(f32[2,768,256]{2,1,0:T(8,128)S(1)} %bitcast.28, f32[2,768,256]{2,1,0:T(8,128)S(1)} %fusion.7), kind=kLoop, calls=%fused_computation.8 | loop fusion | flops 786432 | bytes 3932160 | tf_op jit(solution)/shard_map/convert_element_type | solution.py:215
  75.3 1.9 %collective-permute-done.26.refs_2_ = bf16[32,2048]{1,0:T(8,128)(2,1)S(1)} collective-permute-done((bf16[32,2048]{1,0:T(8,128)(2,1)S(1)}, bf16[32,2048]{1,0:T(8,128)(2,1)S(1)}, u32[]{:S(2)}, u32[]{:S(2)}) %collective-permute-start.26) | collective-permute-done | bytes 131104 | tf_op jit(solution)/shard_map/ppermute | solution.py:57
  77.2 0.7 shard_map.107
  (37 shorter events, 1.6 us)
Async XLA Ops:
  1.6 25.2 %collective-permute-start.12 = (bf16[32,1024]{1,0:T(8,128)(2,1)S(1)}, bf16[32,1024]{1,0:T(8,128)(2,1)S(1)}, u32[]{:S(2)}, u32[]{:S(2)}) collective-permute-start(bf16[32,1024]{1,0:T(8,128)(2,1)S(1)} %get-tuple-element.43.refs_6_), channel_id=1, source_target_pairs={{0,24},{2,26},{4,28},{6,30},{8,16},{10,18},{12,20},{14,22},{16,8},... | collective-permute-start | bytes 196616 | tf_op jit(solution)/shard_map/ppermute | solution.py:57
  6.7 21.1 %collective-permute-start.11 = (bf16[32,1024]{1,0:T(8,128)(2,1)S(1)}, bf16[32,1024]{1,0:T(8,128)(2,1)S(1)}, u32[]{:S(2)}, u32[]{:S(2)}) collective-permute-start(bf16[32,1024]{1,0:T(8,128)(2,1)S(1)} %get-tuple-element.43.refs_6_), channel_id=1, source_target_pairs={{0,16},{2,18},{4,20},{6,22},{8,24},{10,26},{12,28},{14,30},{16,0},... | collective-permute-start | bytes 196616 | tf_op jit(solution)/shard_map/ppermute | solution.py:57
  6.7 21.1 %collective-permute-start.10 = (bf16[32,1024]{1,0:T(8,128)(2,1)S(1)}, bf16[32,1024]{1,0:T(8,128)(2,1)S(1)}, u32[]{:S(2)}, u32[]{:S(2)}) collective-permute-start(bf16[32,1024]{1,0:T(8,128)(2,1)S(1)} %get-tuple-element.43.refs_6_), channel_id=1, source_target_pairs={{0,8},{2,10},{4,12},{6,14},{8,0},{10,2},{12,4},{14,6},{16,24},{18,... | collective-permute-start | bytes 196616 | tf_op jit(solution)/shard_map/ppermute | solution.py:57
  7.3 12.2 %collective-permute-start.3 = (s32[2]{0:T(128)}, s32[2]{0:T(128)S(1)}, u32[]{:S(2)}, u32[]{:S(2)}) collective-permute-start(s32[2]{0:T(128)} %refs_2_.4), channel_id=1, source_target_pairs={{0,6},{2,4},{4,2},{6,0},{8,14},{10,12},{12,10},{14,8},{16,22},{18,... | collective-permute-start | bytes 32 | tf_op jit(solution)/shard_map/ppermute | solution.py:54
  9.9 6.4 %copy-start = (bf16[1792,512]{1,0:T(8,128)(2,1)S(1)}, bf16[1792,512]{1,0:T(8,128)(2,1)}, u32[]{:S(2)}) copy-start(bf16[1792,512]{1,0:T(8,128)(2,1)} %w.1) | copy-start | bytes 5505028
  9.9 19.9 %collective-permute-start.6 = (bf16[32,1024]{1,0:T(8,128)(2,1)S(1)}, bf16[32,1024]{1,0:T(8,128)(2,1)S(1)}, u32[]{:S(2)}, u32[]{:S(2)}) collective-permute-start(bf16[32,1024]{1,0:T(8,128)(2,1)S(1)} %get-tuple-element.39.refs_6_), channel_id=1, source_target_pairs={{0,24},{2,26},{4,28},{6,30},{8,16},{10,18},{12,20},{14,22},{16,8},... | collective-permute-start | bytes 196616 | tf_op jit(solution)/shard_map/ppermute | solution.py:57
  17.9 1.6 %copy-start.1 = (s32[2]{0:T(128)S(1)}, s32[2]{0:T(128)}, u32[]{:S(2)}) copy-start(s32[2]{0:T(128)} %refs_2_.4) | copy-start | bytes 28
  19.5 3.6 %collective-permute-start.2 = (s32[2]{0:T(128)S(1)}, s32[2]{0:T(128)S(1)}, u32[]{:S(2)}, u32[]{:S(2)}) collective-permute-start(s32[2]{0:T(128)S(1)} %copy-done.1), channel_id=1, source_target_pairs={{0,4},{2,6},{4,0},{6,2},{8,12},{10,14},{12,8},{14,10},{16,20},{18,... | collective-permute-start | bytes 32 | tf_op jit(solution)/shard_map/ppermute | solution.py:54
  23.1 3.6 %collective-permute-start.1 = (s32[2]{0:T(128)S(1)}, s32[2]{0:T(128)S(1)}, u32[]{:S(2)}, u32[]{:S(2)}) collective-permute-start(s32[2]{0:T(128)S(1)} %copy-done.1), channel_id=1, source_target_pairs={{0,2},{2,0},{4,6},{6,4},{8,10},{10,8},{12,14},{14,12},{16,18},{18,... | collective-permute-start | bytes 32 | tf_op jit(solution)/shard_map/ppermute | solution.py:54
  26.7 5.8 %collective-permute-start.5 = (bf16[32,1024]{1,0:T(8,128)(2,1)S(1)}, bf16[32,1024]{1,0:T(8,128)(2,1)S(1)}, u32[]{:S(2)}, u32[]{:S(2)}) collective-permute-start(bf16[32,1024]{1,0:T(8,128)(2,1)S(1)} %get-tuple-element.39.refs_6_), channel_id=1, source_target_pairs={{0,16},{2,18},{4,20},{6,22},{8,24},{10,26},{12,28},{14,30},{16,0},... | collective-permute-start | bytes 196616 | tf_op jit(solution)/shard_map/ppermute | solution.py:57
  26.7 5.9 %collective-permute-start.4 = (bf16[32,1024]{1,0:T(8,128)(2,1)S(1)}, bf16[32,1024]{1,0:T(8,128)(2,1)S(1)}, u32[]{:S(2)}, u32[]{:S(2)}) collective-permute-start(bf16[32,1024]{1,0:T(8,128)(2,1)S(1)} %get-tuple-element.39.refs_6_), channel_id=1, source_target_pairs={{0,8},{2,10},{4,12},{6,14},{8,0},{10,2},{12,4},{14,6},{16,24},{18,... | collective-permute-start | bytes 196616 | tf_op jit(solution)/shard_map/ppermute | solution.py:57
  28.7 5.2 %collective-permute-start.13 = (bf16[2,32,1024]{2,1,0:T(8,128)(2,1)S(1)}, bf16[2,32,1024]{2,1,0:T(8,128)(2,1)S(1)}, u32[]{:S(2)}, u32[]{:S(2)}) collective-permute-start(bf16[2,32,1024]{2,1,0:T(8,128)(2,1)S(1)} %get-tuple-element.44), channel_id=1, source_target_pairs={{0,2},{2,0},{4,6},{6,4},{8,10},{10,8},{12,14},{14,12},{16,18},{18,... | collective-permute-start | bytes 393224 | tf_op jit(solution)/shard_map/ppermute | solution.py:54
  29.3 5.3 %collective-permute-start.14 = (bf16[2,32,1024]{2,1,0:T(8,128)(2,1)S(1)}, bf16[2,32,1024]{2,1,0:T(8,128)(2,1)S(1)}, u32[]{:S(2)}, u32[]{:S(2)}) collective-permute-start(bf16[2,32,1024]{2,1,0:T(8,128)(2,1)S(1)} %get-tuple-element.45), channel_id=1, source_target_pairs={{0,4},{2,6},{4,0},{6,2},{8,12},{10,14},{12,8},{14,10},{16,20},{18,... | collective-permute-start | bytes 393224 | tf_op jit(solution)/shard_map/ppermute | solution.py:54
  29.8 5.9 %collective-permute-start.15 = (bf16[2,32,1024]{2,1,0:T(8,128)(2,1)S(1)}, bf16[2,32,1024]{2,1,0:T(8,128)(2,1)S(1)}, u32[]{:S(2)}, u32[]{:S(2)}) collective-permute-start(bf16[2,32,1024]{2,1,0:T(8,128)(2,1)S(1)} %get-tuple-element.46), channel_id=1, source_target_pairs={{0,6},{2,4},{4,2},{6,0},{8,14},{10,12},{12,10},{14,8},{16,22},{18,... | collective-permute-start | bytes 393224 | tf_op jit(solution)/shard_map/ppermute | solution.py:54
  32.5 35.2 %collective-permute-start.17 = (bf16[1536,256]{1,0:T(8,128)(2,1)S(1)}, bf16[1536,256]{1,0:T(8,128)(2,1)S(1)}, u32[]{:S(2)}, u32[]{:S(2)}) collective-permute-start(bf16[1536,256]{1,0:T(8,128)(2,1)S(1)} %get-tuple-element.50.own), channel_id=1, source_target_pairs={{0,1},{1,0},{2,3},{3,2},{4,5},{5,4},{6,7},{7,6},{8,9},{9,8},{10,11... | collective-permute-start | bytes 2359304 | tf_op jit(solution)/shard_map/ppermute | solution.py:60
  32.6 41.4 %collective-permute-start = (f32[1536,256]{1,0:T(8,128)S(1)}, f32[1536,256]{1,0:T(8,128)S(1)}, u32[]{:S(2)}, u32[]{:S(2)}) collective-permute-start(f32[1536,256]{1,0:T(8,128)S(1)} %broadcast_select_fusion), channel_id=1, source_target_pairs={{0,1},{1,0},{2,3},{3,2},{4,5},{5,4},{6,7},{7,6},{8,9},{9,8},{10,11... | collective-permute-start | bytes 4718600 | tf_op jit(solution)/shard_map/ppermute | solution.py:60
  34.0 6.4 %collective-permute-start.7 = (bf16[2,32,1024]{2,1,0:T(8,128)(2,1)S(1)}, bf16[2,32,1024]{2,1,0:T(8,128)(2,1)S(1)}, u32[]{:S(2)}, u32[]{:S(2)}) collective-permute-start(bf16[2,32,1024]{2,1,0:T(8,128)(2,1)S(1)} %get-tuple-element.40), channel_id=1, source_target_pairs={{0,2},{2,0},{4,6},{6,4},{8,10},{10,8},{12,14},{14,12},{16,18},{18,... | collective-permute-start | bytes 393224 | tf_op jit(solution)/shard_map/ppermute | solution.py:54
  34.6 8.0 %collective-permute-start.8 = (bf16[2,32,1024]{2,1,0:T(8,128)(2,1)S(1)}, bf16[2,32,1024]{2,1,0:T(8,128)(2,1)S(1)}, u32[]{:S(2)}, u32[]{:S(2)}) collective-permute-start(bf16[2,32,1024]{2,1,0:T(8,128)(2,1)S(1)} %get-tuple-element.41), channel_id=1, source_target_pairs={{0,4},{2,6},{4,0},{6,2},{8,12},{10,14},{12,8},{14,10},{16,20},{18,... | collective-permute-start | bytes 393224 | tf_op jit(solution)/shard_map/ppermute | solution.py:54
  35.7 6.9 %collective-permute-start.9 = (bf16[2,32,1024]{2,1,0:T(8,128)(2,1)S(1)}, bf16[2,32,1024]{2,1,0:T(8,128)(2,1)S(1)}, u32[]{:S(2)}, u32[]{:S(2)}) collective-permute-start(bf16[2,32,1024]{2,1,0:T(8,128)(2,1)S(1)} %get-tuple-element.42), channel_id=1, source_target_pairs={{0,6},{2,4},{4,2},{6,0},{8,14},{10,12},{12,10},{14,8},{16,22},{18,... | collective-permute-start | bytes 393224 | tf_op jit(solution)/shard_map/ppermute | solution.py:54
  40.4 4.7 %collective-permute-start.18 = (f32[2,32,768]{2,1,0:T(8,128)S(1)}, f32[2,32,768]{2,1,0:T(8,128)S(1)}, u32[]{:S(2)}, u32[]{:S(2)}) collective-permute-start(f32[2,32,768]{2,1,0:T(8,128)S(1)} %fusion.11), channel_id=1, source_target_pairs={{0,1},{1,0},{2,3},{3,2},{4,5},{5,4},{6,7},{7,6},{8,9},{9,8},{10,11... | collective-permute-start | bytes 589832 | tf_op jit(solution)/shard_map/ppermute | solution.py:60
  45.1 4.1 %collective-permute-start.16 = (f32[2,32,768]{2,1,0:T(8,128)S(1)}, f32[2,32,768]{2,1,0:T(8,128)S(1)}, u32[]{:S(2)}, u32[]{:S(2)}) collective-permute-start(f32[2,32,768]{2,1,0:T(8,128)S(1)} %fusion.10), channel_id=1, source_target_pairs={{0,1},{1,0},{2,3},{3,2},{4,5},{5,4},{6,7},{7,6},{8,9},{9,8},{10,11... | collective-permute-start | bytes 589832 | tf_op jit(solution)/shard_map/ppermute | solution.py:60
  46.2 7.4 %collective-permute-start.21 = (bf16[2,32,1024]{2,1,0:T(8,128)(2,1)S(1)}, bf16[2,32,1024]{2,1,0:T(8,128)(2,1)S(1)}, u32[]{:S(2)}, u32[]{:S(2)}) collective-permute-start(bf16[2,32,1024]{2,1,0:T(8,128)(2,1)S(1)} %slice.51), channel_id=1, source_target_pairs={{0,6},{2,4},{4,2},{6,0},{8,14},{10,12},{12,10},{14,8},{16,22},{18,... | collective-permute-start | bytes 393224 | tf_op jit(solution)/shard_map/ppermute | solution.py:54
  47.7 8.2 %collective-permute-start.20 = (bf16[2,32,1024]{2,1,0:T(8,128)(2,1)S(1)}, bf16[2,32,1024]{2,1,0:T(8,128)(2,1)S(1)}, u32[]{:S(2)}, u32[]{:S(2)}) collective-permute-start(bf16[2,32,1024]{2,1,0:T(8,128)(2,1)S(1)} %slice.51), channel_id=1, source_target_pairs={{0,4},{2,6},{4,0},{6,2},{8,12},{10,14},{12,8},{14,10},{16,20},{18,... | collective-permute-start | bytes 393224 | tf_op jit(solution)/shard_map/ppermute | solution.py:54
  49.2 7.8 %collective-permute-start.19 = (bf16[2,32,1024]{2,1,0:T(8,128)(2,1)S(1)}, bf16[2,32,1024]{2,1,0:T(8,128)(2,1)S(1)}, u32[]{:S(2)}, u32[]{:S(2)}) collective-permute-start(bf16[2,32,1024]{2,1,0:T(8,128)(2,1)S(1)} %slice.51), channel_id=1, source_target_pairs={{0,2},{2,0},{4,6},{6,4},{8,10},{10,8},{12,14},{14,12},{16,18},{18,... | collective-permute-start | bytes 393224 | tf_op jit(solution)/shard_map/ppermute | solution.py:54
  53.6 6.0 %collective-permute-start.24 = (bf16[2,32,1024]{2,1,0:T(8,128)(2,1)S(1)}, bf16[2,32,1024]{2,1,0:T(8,128)(2,1)S(1)}, u32[]{:S(2)}, u32[]{:S(2)}) collective-permute-start(bf16[2,32,1024]{2,1,0:T(8,128)(2,1)S(1)} %fusion.9), channel_id=1, source_target_pairs={{0,6},{2,4},{4,2},{6,0},{8,14},{10,12},{12,10},{14,8},{16,22},{18,... | collective-permute-start | bytes 393224 | tf_op jit(solution)/shard_map/ppermute | solution.py:54
  55.9 6.4 %collective-permute-start.23 = (bf16[2,32,1024]{2,1,0:T(8,128)(2,1)S(1)}, bf16[2,32,1024]{2,1,0:T(8,128)(2,1)S(1)}, u32[]{:S(2)}, u32[]{:S(2)}) collective-permute-start(bf16[2,32,1024]{2,1,0:T(8,128)(2,1)S(1)} %fusion.9), channel_id=1, source_target_pairs={{0,4},{2,6},{4,0},{6,2},{8,12},{10,14},{12,8},{14,10},{16,20},{18,... | collective-permute-start | bytes 393224 | tf_op jit(solution)/shard_map/ppermute | solution.py:54
  57.1 5.2 %collective-permute-start.22 = (bf16[2,32,1024]{2,1,0:T(8,128)(2,1)S(1)}, bf16[2,32,1024]{2,1,0:T(8,128)(2,1)S(1)}, u32[]{:S(2)}, u32[]{:S(2)}) collective-permute-start(bf16[2,32,1024]{2,1,0:T(8,128)(2,1)S(1)} %fusion.9), channel_id=1, source_target_pairs={{0,2},{2,0},{4,6},{6,4},{8,10},{10,8},{12,14},{14,12},{16,18},{18,... | collective-permute-start | bytes 393224 | tf_op jit(solution)/shard_map/ppermute | solution.py:54
  63.2 12.1 %collective-permute-start.25 = (bf16[32,2048]{1,0:T(8,128)(2,1)S(1)}, bf16[32,2048]{1,0:T(8,128)(2,1)S(1)}, u32[]{:S(2)}, u32[]{:S(2)}) collective-permute-start(bf16[32,2048]{1,0:T(8,128)(2,1)S(1)} %get-tuple-element.51), channel_id=1, source_target_pairs={{0,8},{2,10},{4,12},{6,14},{8,0},{10,2},{12,4},{14,6},{16,24},{18,... | collective-permute-start | bytes 393224 | tf_op jit(solution)/shard_map/ppermute | solution.py:57
  64.3 12.9 %collective-permute-start.26 = (bf16[32,2048]{1,0:T(8,128)(2,1)S(1)}, bf16[32,2048]{1,0:T(8,128)(2,1)S(1)}, u32[]{:S(2)}, u32[]{:S(2)}) collective-permute-start(bf16[32,2048]{1,0:T(8,128)(2,1)S(1)} %get-tuple-element.52), channel_id=1, source_target_pairs={{0,16},{2,18},{4,20},{6,22},{8,24},{10,26},{12,28},{14,30},{16,0},... | collective-permute-start | bytes 393224 | tf_op jit(solution)/shard_map/ppermute | solution.py:57
  67.2 10.0 %collective-permute-start.27 = (bf16[32,2048]{1,0:T(8,128)(2,1)S(1)}, bf16[32,2048]{1,0:T(8,128)(2,1)S(1)}, u32[]{:S(2)}, u32[]{:S(2)}) collective-permute-start(bf16[32,2048]{1,0:T(8,128)(2,1)S(1)} %get-tuple-element.53), channel_id=1, source_target_pairs={{0,24},{2,26},{4,28},{6,30},{8,16},{10,18},{12,20},{14,22},{16,8},... | collective-permute-start | bytes 393224 | tf_op jit(solution)/shard_map/ppermute | solution.py:57

commit v4 on v3

--- a/solution.py
+++ b/solution.py
@@ -77,7 +77,7 @@
         low_core = lax.axis_index("mp") == 0
         me, core, low_core, down, up, tenant = lax.optimization_barrier((me, core, low_core, down, up, tenant))
 
-        first = max(width - cols, 256) // 256 * 128
+        first = max(width * 768 // 1792 // 128 * 128, 128)
         rest = width - first
 
         def join(down_ref, up_ref, out0, out1):
@@ -200,61 +200,83 @@
         base = []
         for j in range(seqs):
             base.append(jnp.dot(h3[j], weight, preferred_element_type=F32))
-        base = jnp.concatenate(base)
         if m == 2:
-            theirs = jnp.where(low_core, base[:, cols:], base[:, :cols])
-            ours = jnp.where(low_core, base[:, :cols], base[:, cols:])
+            theirs = jnp.concatenate([jnp.where(low_core, x[:, cols:], x[:, :cols]) for x in base])
             base_got = swap(theirs)
-            base_own = ours + base_got
         else:
-            base_own = lax.psum_scatter(base, "mp", scatter_dimension=1, tiled=True)
+            base_own = lax.psum_scatter(jnp.concatenate(base), "mp", scatter_dimension=1, tiled=True)
 
         back_low = mp_sum(jnp.einsum("slk,srk->srl", g3, up_s, preferred_element_type=F32)).astype(BF16)
         low = mp_sum(jnp.einsum("slw,srw->srl", h3, down_s, preferred_element_type=F32))
-        up_f = up_s.astype(F32)
-        values = (base_own.reshape(seqs, length, cols) + jnp.einsum("srl,srk->slk", low, up_f, precision=HIGH)).astype(BF16)
         up_seq = jnp.einsum("srl,slk->srk", low, g3.astype(F32), precision=HIGH)
         down_seq = jnp.einsum("srl,slw->srw", back_low, h3, preferred_element_type=F32)
         if m == 2:
             per = length // block
 
-            def widen(core_ref, own, mate, w, coeff, factor, out):
-                def part(x, half):
-                    at = pl.multiple_of(half * cols, math.gcd(cols, 128))
-                    return lax.dot_general(
-                        x[...], w[:, pl.ds(at, cols)], (((1,), (1,)), ((), ())), preferred_element_type=F32
-                    )
-
-                total = part(own, core_ref[0]) + part(mate, 1 - core_ref[0])
-                total += lax.dot_general(
+            def outputs(core_ref, own, mate, w, coeff, factor, low_ref, up_ref, got_ref, *rest_refs):
+                bases, (out, values_out, lhs) = rest_refs[:seqs], rest_refs[seqs:]
+                step = pl.program_id(0)
+                here = pl.multiple_of(core_ref[0] * cols, math.gcd(cols, 128))
+                there = pl.multiple_of((1 - core_ref[0]) * cols, math.gcd(cols, 128))
+                lhs[:, pl.ds(here, cols)] = own[...]
+                lhs[:, pl.ds(there, cols)] = mate[...]
+                total = lax.dot_general(
+                    lhs[...], w[...], (((1,), (1,)), ((), ())), preferred_element_type=F32
+                ) + lax.dot_general(
                     coeff[0], factor[0], (((0,), (0,)), ((), ())), preferred_element_type=F32
                 )
                 out[...] = total.astype(BF16)
+                term = got_ref[...] + lax.dot_general(
+                    low_ref[0],
+                    up_ref[0].astype(F32),
+                    (((0,), (0,)), ((), ())),
+                    precision=HIGH,
+                    preferred_element_type=F32,
+                )
+                for j in range(seqs):
+
+                    @pl.when(step // per == j)
+                    def _(j=j):
+                        at = pl.multiple_of(step % per * block, block)
+                        values_out[...] = (term + bases[j][pl.ds(at, block), pl.ds(here, cols)]).astype(BF16)
 
             rows_of = pl.BlockSpec((block, cols), lambda i: (i, 0))
-            hidden_grad = pl.pallas_call(
-                widen,
+            coeff_of = pl.BlockSpec((1, rank, block), lambda i: (i // per, 0, i % per))
+            values, hidden_grad = pl.pallas_call(
+                outputs,
                 grid=(rows // block,),
-                out_shape=jax.ShapeDtypeStruct((rows, width), BF16),
+                out_shape=[
+                    jax.ShapeDtypeStruct((rows, width), BF16),
+                    jax.ShapeDtypeStruct((rows, cols), BF16),
+                ],
                 in_specs=[
                     SMEM,
                     rows_of,
                     rows_of,
-                    pl.BlockSpec((width, m * cols), lambda i: (0, 0)),
-                    pl.BlockSpec((1, rank, block), lambda i: (i // per, 0, i % per)),
+                    VMEM,
+                    coeff_of,
                     pl.BlockSpec((1, rank, width), lambda i: (i // per, 0, 0)),
-                ],
-                out_specs=pl.BlockSpec((block, width), lambda i: (i, 0)),
+                    coeff_of,
+                    pl.BlockSpec((1, rank, cols), lambda i: (i // per, 0, 0)),
+                    rows_of,
+                ]
+                + [VMEM] * seqs,
+                out_specs=[pl.BlockSpec((block, width), lambda i: (i, 0)), rows_of],
+                scratch_shapes=[pltpu.VMEM((block, m * cols), BF16)],
                 compiler_params=pltpu.CompilerParams(vmem_limit_bytes=24 << 20),
-                name="widen",
-            )(core, grad_in, other, weight, back_low, down_s)
+                name="outputs",
+            )(core, grad_in, other, weight, back_low, down_s, low, up_s, base_got, *base)[::-1]
         else:
+            values = (
+                base_own.reshape(seqs, length, cols)
+                + jnp.einsum("srl,srk->slk", low, up_s.astype(F32), precision=HIGH)
+            ).astype(BF16)
             hidden_grad = (
                 lax.dot_general(grad_full, weight, (((1,), (1,)), ((), ())), preferred_element_type=F32)
                 + jnp.einsum("srl,srw->slw", back_low, down_s, preferred_element_type=F32).reshape(rows, width)
             ).astype(BF16)
 
-        items = [down_seq[:, :, :rest], jnp.concatenate([down_seq[:, :, rest:], up_seq], axis=2)]
+        items = [down_seq, up_seq]
         near = [[], []]
         for p in range(2):
             small = items[p].astype(BF16)
@@ -273,7 +295,7 @@
                     @pl.when(holder % q == inner)
                     def _(d=d, j=j, holder=holder):
                         k = offset(outer, holder // q, r)
-                        for p, at in ((0, slice(0, rest)), (1, slice(rest, None))):
+                        for p, at in ((0, slice(0, width)), (1, slice(width, None))):
                             piece = own[p] if d == 0 else others[p * (q - 1) + d - 1]
                             acc[k, :, at] += piece[j].astype(F32)
 

time: 78.2 us -> 78.8 us (level)
  starting transfers between devices: 33.3 us -> 35.6 us
  Pallas kernels: 15 us -> 16.6 us
  other arithmetic: 1.6 us -> 0.35 us
  waiting for transfers between devices: 19.6 us -> 18.4 us
  matrix products: 7.5 us -> 6.68 us
    ppermute x15, waiting for transfers between devices: 17.7 us -> 15.6 us  [send_inner(): lax.ppermute(x, 'dp', [(i, i // q * q + peer(i % q, d, q)) for i in range...]
    pallas_call x1, Pallas kernels: 6.29 us -> 7.93 us  [local(): pl.pallas_call(outputs, grid=(rows // block,), out_shape=[jax.ShapeDtypeS...]
    ppermute x9, starting transfers between devices: 14.9 us -> 16.2 us  [send_outer(): lax.ppermute(x, 'dp', [(i, peer(i // q, d, r) * q + i % q) for i in range...]
    convert_element_type x2 -> x0, other arithmetic: 1.05 us -> none  [the longest x1 1.04 us: local(): (base_own.reshape(seqs, length, cols) + jnp.einsum('srl,srk->slk', low, u...]
    dot_general x1 -> x0, matrix products: 0.83 us -> none  [local(): jnp.einsum('srl,srk->slk', low, up_f, precision=HIGH)]
  transfers between devices with their start and end apart: 28 -> 28, of which waited for: 10 -> 8; matrix products, arithmetic and copies ran while one was open for 12% -> 9% of each run, Pallas kernels for 17% -> 20%
where the time goes in v4:
time: 78.8 us; the launch traced here: 78.5 us
  starting transfers between devices  35.6 us (45%)
  waiting for transfers between devices  18.4 us (23%)
  Pallas kernels  16.6 us (21%)
  matrix products  6.68 us (8%)
  between operations  0.82 us (1%)
    ppermute x15, starting transfers between devices, send_inner(): lax.ppermute(x, 'dp', [(i, i // q * q + peer(i % q, d, q)) for i in range...  18.3 us
    ppermute x9, starting transfers between devices, send_outer(): lax.ppermute(x, 'dp', [(i, peer(i // q, d, r) * q + i % q) for i in range...  16.2 us
    ppermute x15, waiting for transfers between devices, send_inner(): lax.ppermute(x, 'dp', [(i, i // q * q + peer(i % q, d, q)) for i in range...  15.6 us
    pallas_call x1, Pallas kernels, local(): pl.pallas_call(outputs, grid=(rows // block,), out_shape=[jax.ShapeDtypeS...  7.93 us
    pallas_call x6, Pallas kernels, kernel_call(): pl.pallas_call(body, out_shape=[pltpu.VMEM(o.shape, o.dtype) if inside el...  5.02 us
    dot_general x2, matrix products, local(): base.append(jnp.dot(h3[j], weight, preferred_element_type=F32))  3.15 us
    pallas_call x1, Pallas kernels, local(): pl.pallas_call(load, out_shape=[pltpu.VMEM(hidden.shape, BF16), pltpu.VME...  2.77 us
    ppermute x9, waiting for transfers between devices, send_outer(): lax.ppermute(x, 'dp', [(i, peer(i // q, d, r) * q + i % q) for i in range...  2.22 us
  transfers between devices with their start and end apart: 28, of which 8 were waited for; matrix products, arithmetic and copies ran while one was open for 9% of the time, Pallas kernels for 20%

profile of v4, /device:TPU:0, one launch (start us, length us, event | category | flops | bytes accessed | tf_op | source)
XLA Modules:
  0.0 78.5 jit_solution(5097469684461189724)
XLA Ops:
  0.6 4.0 %collective-permute-start.3 = (s32[2]{0:T(128)}, s32[2]{0:T(128)S(1)}, u32[]{:S(2)}, u32[]{:S(2)}) collective-permute-start(s32[2]{0:T(128)} %refs_2_.4), channel_id=1, source_target_pairs={{0,6},{2,4},{4,2},{6,0},{8,14},{10,12},{12,10},{14,8},{16,22},{18,... | collective-permute-start | bytes 32 | tf_op jit(solution)/shard_map/ppermute | solution.py:54
  4.6 0.5 collective-permute-start.2
  5.1 0.9 %join.1 = (bf16[32,1024]{1,0:T(8,128)(2,1)S(1)}, bf16[32,1024]{1,0:T(8,128)(2,1)S(1)}) custom-call(bf16[32,1792]{1,0:T(8,128)(2,1)} %bitcast.26, bf16[32,256]{1,0:T(8,128)(2,1)} %bitcast.27), custom_call_target="tpu_custom_call" | custom-call | tf_op jit(solution)/shard_map/join/pallas_call | solution.py:88
  6.1 3.7 %collective-permute-start.6 = (bf16[32,1024]{1,0:T(8,128)(2,1)S(1)}, bf16[32,1024]{1,0:T(8,128)(2,1)S(1)}, u32[]{:S(2)}, u32[]{:S(2)}) collective-permute-start(bf16[32,1024]{1,0:T(8,128)(2,1)S(1)} %get-tuple-element.41.refs_6_), channel_id=1, source_target_pairs={{0,24},{2,26},{4,28},{6,30},{8,16},{10,18},{12,20},{14,22},{16,8},... | collective-permute-start | bytes 196616 | tf_op jit(solution)/shard_map/ppermute | solution.py:57
  9.7 0.8 collective-permute-start.4
  10.5 2.8 %load.1 = (bf16[1536,1792]{1,0:T(8,128)(2,1)S(1)}, bf16[1536,256]{1,0:T(8,128)(2,1)S(1)}) custom-call(bf16[1536,1792]{1,0:T(8,128)(2,1)} %x_ref.1, bf16[1536,256]{1,0:T(8,128)(2,1)} %g_ref.1), custom_call_target="tpu_custom_call" | custom-call | tf_op jit(solution)/shard_map/load/pallas_call | solution.py:115
  13.3 1.6 %fusion.rest_refs_1_ = f32[768,512]{1,0:T(8,128)S(1)} fusion(bf16[1792,512]{1,0:T(8,128)(2,1)S(1)} %copy-done, bf16[1536,1792]{1,0:T(8,128)(2,1)S(1)} %get-tuple-element.51), kind=kOutput, calls=%fused_computation | convolution fusion | flops 1409286144 | bytes 6160384 | tf_op jit(solution)/shard_map/dot_general | solution.py:202
  14.9 1.6 %fusion.2.rest_refs_0_ = f32[768,512]{1,0:T(8,128)S(1)} fusion(bf16[1792,512]{1,0:T(8,128)(2,1)S(1)} %copy-done, bf16[1536,1792]{1,0:T(8,128)(2,1)S(1)} %get-tuple-element.51), kind=kOutput, calls=%fused_computation.2 | convolution fusion | flops 1409286144 | bytes 6160384 | tf_op jit(solution)/shard_map/dot_general | solution.py:202
  16.5 0.5 collective-permute-start.1
  17.0 3.7 %collective-permute-start.13 = (bf16[32,1024]{1,0:T(8,128)(2,1)S(1)}, bf16[32,1024]{1,0:T(8,128)(2,1)S(1)}, u32[]{:S(2)}, u32[]{:S(2)}) collective-permute-start(bf16[32,1024]{1,0:T(8,128)(2,1)S(1)} %get-tuple-element.46.refs_6_), channel_id=1, source_target_pairs={{0,24},{2,26},{4,28},{6,30},{8,16},{10,18},{12,20},{14,22},{16,8},... | collective-permute-start | bytes 196616 | tf_op jit(solution)/shard_map/ppermute | solution.py:57
  20.7 1.6 %collective-permute-start.12 = (bf16[32,1024]{1,0:T(8,128)(2,1)S(1)}, bf16[32,1024]{1,0:T(8,128)(2,1)S(1)}, u32[]{:S(2)}, u32[]{:S(2)}) collective-permute-start(bf16[32,1024]{1,0:T(8,128)(2,1)S(1)} %get-tuple-element.46.refs_6_), channel_id=1, source_target_pairs={{0,16},{2,18},{4,20},{6,22},{8,24},{10,26},{12,28},{14,30},{16,0},... | collective-permute-start | bytes 196616 | tf_op jit(solution)/shard_map/ppermute | solution.py:57
  22.3 2.0 %collective-permute-start.11 = (bf16[32,1024]{1,0:T(8,128)(2,1)S(1)}, bf16[32,1024]{1,0:T(8,128)(2,1)S(1)}, u32[]{:S(2)}, u32[]{:S(2)}) collective-permute-start(bf16[32,1024]{1,0:T(8,128)(2,1)S(1)} %get-tuple-element.46.refs_6_), channel_id=1, source_target_pairs={{0,8},{2,10},{4,12},{6,14},{8,0},{10,2},{12,4},{14,6},{16,24},{18,... | collective-permute-start | bytes 196616 | tf_op jit(solution)/shard_map/ppermute | solution.py:57
  24.3 0.9 %shard_map.102 = (bf16[2,32,1024]{2,1,0:T(8,128)(2,1)S(1)}, bf16[2,32,1024]{2,1,0:T(8,128)(2,1)S(1)}, bf16[2,32,1024]{2,1,0:T(8,128)(2,1)S(1)}) custom-call(s32[1]{0:T(128)} %bitcast.refs_0_, s32[16]{0:T(128)} %refs_1_.9, s32[2]{0:T(128)} %refs_2_.4, s32[2]{0:T(128)S(1)} %collective-permute-done.1.refs_3_, s32[2]{0:T(128)S(1)} %collective-permute-done.2.refs_4_, ...), custom_call_target="tpu_custom_call" | custom-call | tf_op jit(solution)/shard_map/pallas_call | solution.py:39
  25.2 0.6 collective-permute-start.7
  26.0 0.7 collective-permute-done.12.refs_8_
  26.7 0.4 collective-permute-done.11.refs_7_
  27.0 0.9 %shard_map.104 = (bf16[2,32,1024]{2,1,0:T(8,128)(2,1)S(1)}, bf16[2,32,1024]{2,1,0:T(8,128)(2,1)S(1)}, bf16[2,32,1024]{2,1,0:T(8,128)(2,1)S(1)}) custom-call(s32[1]{0:T(128)} %bitcast.refs_0_, s32[16]{0:T(128)} %refs_1_.9, s32[2]{0:T(128)} %refs_2_.4, s32[2]{0:T(128)S(1)} %collective-permute-done.1.refs_3_, s32[2]{0:T(128)S(1)} %collective-permute-done.2.refs_4_, ...), custom_call_target="tpu_custom_call" | custom-call | tf_op jit(solution)/shard_map/pallas_call | solution.py:39
  27.9 0.8 %collective-permute-start.14 = (bf16[2,32,1024]{2,1,0:T(8,128)(2,1)S(1)}, bf16[2,32,1024]{2,1,0:T(8,128)(2,1)S(1)}, u32[]{:S(2)}, u32[]{:S(2)}) collective-permute-start(bf16[2,32,1024]{2,1,0:T(8,128)(2,1)S(1)} %get-tuple-element.47), channel_id=1, source_target_pairs={{0,2},{2,0},{4,6},{6,4},{8,10},{10,8},{12,14},{14,12},{16,18},{18,... | collective-permute-start | bytes 393224 | tf_op jit(solution)/shard_map/ppermute | solution.py:54
  28.7 1.5 %collective-permute-start.15 = (bf16[2,32,1024]{2,1,0:T(8,128)(2,1)S(1)}, bf16[2,32,1024]{2,1,0:T(8,128)(2,1)S(1)}, u32[]{:S(2)}, u32[]{:S(2)}) collective-permute-start(bf16[2,32,1024]{2,1,0:T(8,128)(2,1)S(1)} %get-tuple-element.48), channel_id=1, source_target_pairs={{0,4},{2,6},{4,0},{6,2},{8,12},{10,14},{12,8},{14,10},{16,20},{18,... | collective-permute-start | bytes 393224 | tf_op jit(solution)/shard_map/ppermute | solution.py:54
  30.2 1.2 %collective-permute-start.16 = (bf16[2,32,1024]{2,1,0:T(8,128)(2,1)S(1)}, bf16[2,32,1024]{2,1,0:T(8,128)(2,1)S(1)}, u32[]{:S(2)}, u32[]{:S(2)}) collective-permute-start(bf16[2,32,1024]{2,1,0:T(8,128)(2,1)S(1)} %get-tuple-element.49), channel_id=1, source_target_pairs={{0,6},{2,4},{4,2},{6,0},{8,14},{10,12},{12,10},{14,8},{16,22},{18,... | collective-permute-start | bytes 393224 | tf_op jit(solution)/shard_map/ppermute | solution.py:54
  31.5 1.5 %collective-permute-start.8 = (bf16[2,32,1024]{2,1,0:T(8,128)(2,1)S(1)}, bf16[2,32,1024]{2,1,0:T(8,128)(2,1)S(1)}, u32[]{:S(2)}, u32[]{:S(2)}) collective-permute-start(bf16[2,32,1024]{2,1,0:T(8,128)(2,1)S(1)} %get-tuple-element.43), channel_id=1, source_target_pairs={{0,4},{2,6},{4,0},{6,2},{8,12},{10,14},{12,8},{14,10},{16,20},{18,... | collective-permute-start | bytes 393224 | tf_op jit(solution)/shard_map/ppermute | solution.py:54
  33.0 0.7 collective-permute-start.9
  33.8 6.3 %collective-permute-done.8.refs_11_ = bf16[2,32,1024]{2,1,0:T(8,128)(2,1)S(1)} collective-permute-done((bf16[2,32,1024]{2,1,0:T(8,128)(2,1)S(1)}, bf16[2,32,1024]{2,1,0:T(8,128)(2,1)S(1)}, u32[]{:S(2)}, u32[]{:S(2)}) %collective-permute-start.8) | collective-permute-done | bytes 131104 | tf_op jit(solution)/shard_map/ppermute | solution.py:54
  40.1 0.5 collective-permute-start.18
  40.6 0.8 shard_map.103
  41.4 0.8 %shard_map.105.factor = bf16[2,32,1792]{2,1,0:T(8,128)(2,1)S(1)} custom-call(s32[1]{0:T(128)} %bitcast.refs_0_, s32[16]{0:T(128)} %refs_1_.9, s32[2]{0:T(128)} %refs_2_.4, s32[2]{0:T(128)S(1)} %collective-permute-done.1.refs_3_, s32[2]{0:T(128)S(1)} %collective-permute-done.2.refs_4_, s32[2]{0:T(128)S(1)} %collective-permute-done.3.refs_5_, ...), custom_call_target="tpu_custom_call" | custom-call | tf_op jit(solution)/shard_map/pallas_call | solution.py:39
  42.2 1.7 %fusion.7 = f32[2,32,768]{2,1,0:T(8,128)S(1)} fusion(bf16[2,32,1792]{2,1,0:T(8,128)(2,1)S(1)} %shard_map.105.factor, bf16[2,768,1792]{2,1,0:T(8,128)(2,1)S(1)} %bitcast.22), kind=kOutput, calls=%fused_computation.11 | convolution fusion | flops 176160768 | bytes 5931008 | tf_op jit(solution)/shard_map/slw,srw->srl/dot_general | solution.py:210
  43.9 0.3 fusion.6
  44.3 0.5 collective-permute-start.10
  44.8 0.6 collective-permute-done.17
  45.4 0.5 fusion.5
  45.9 1.6 %collective-permute-start.24 = (bf16[2,32,256]{2,1,0:T(8,128)(2,1)S(1)}, bf16[2,32,256]{2,1,0:T(8,128)(2,1)S(1)}, u32[]{:S(2)}, u32[]{:S(2)}) collective-permute-start(bf16[2,32,256]{2,1,0:T(8,128)(2,1)S(1)} %get-tuple-element.68), channel_id=1, source_target_pairs={{0,6},{2,4},{4,2},{6,0},{8,14},{10,12},{12,10},{14,8},{16,22},{18,... | collective-permute-start | bytes 98312 | tf_op jit(solution)/shard_map/ppermute | solution.py:54
  47.5 0.8 %collective-permute-start.23 = (bf16[2,32,256]{2,1,0:T(8,128)(2,1)S(1)}, bf16[2,32,256]{2,1,0:T(8,128)(2,1)S(1)}, u32[]{:S(2)}, u32[]{:S(2)}) collective-permute-start(bf16[2,32,256]{2,1,0:T(8,128)(2,1)S(1)} %get-tuple-element.68), channel_id=1, source_target_pairs={{0,4},{2,6},{4,0},{6,2},{8,12},{10,14},{12,8},{14,10},{16,20},{18,... | collective-permute-start | bytes 98312 | tf_op jit(solution)/shard_map/ppermute | solution.py:54
  48.4 1.1 %collective-permute-start.22 = (bf16[2,32,256]{2,1,0:T(8,128)(2,1)S(1)}, bf16[2,32,256]{2,1,0:T(8,128)(2,1)S(1)}, u32[]{:S(2)}, u32[]{:S(2)}) collective-permute-start(bf16[2,32,256]{2,1,0:T(8,128)(2,1)S(1)} %get-tuple-element.68), channel_id=1, source_target_pairs={{0,2},{2,0},{4,6},{6,4},{8,10},{10,8},{12,14},{14,12},{16,18},{18,... | collective-permute-start | bytes 98312 | tf_op jit(solution)/shard_map/ppermute | solution.py:54
  49.5 1.0 %fusion.4 = (bf16[2,32,1792]{2,1,0:T(8,128)(2,1)S(1)}, f32[2,32,1792]{2,1,0:T(8,128)S(1)}) fusion(bf16[2,32,768]{2,1,0:T(8,128)(2,1)S(1)} %add_convert_fusion.coeff, bf16[2,768,1792]{2,1,0:T(8,128)(2,1)S(1)} %bitcast.23), kind=kOutput, calls=%fused_computation.8 | convolution fusion | flops 176275456 | bytes 6291456 | tf_op jit(solution)/shard_map/srl,slw->srw/dot_general | solution.py:212
  50.5 0.3 collective-permute-done.24.refs_13_
  50.8 1.6 %collective-permute-start.21 = (bf16[2,32,1792]{2,1,0:T(8,128)(2,1)S(1)}, bf16[2,32,1792]{2,1,0:T(8,128)(2,1)S(1)}, u32[]{:S(2)}, u32[]{:S(2)}) collective-permute-start(bf16[2,32,1792]{2,1,0:T(8,128)(2,1)S(1)} %get-tuple-element.66), channel_id=1, source_target_pairs={{0,6},{2,4},{4,2},{6,0},{8,14},{10,12},{12,10},{14,8},{16,22},{18,... | collective-permute-start | bytes 688136 | tf_op jit(solution)/shard_map/ppermute | solution.py:54
  52.4 0.8 %collective-permute-start.20 = (bf16[2,32,1792]{2,1,0:T(8,128)(2,1)S(1)}, bf16[2,32,1792]{2,1,0:T(8,128)(2,1)S(1)}, u32[]{:S(2)}, u32[]{:S(2)}) collective-permute-start(bf16[2,32,1792]{2,1,0:T(8,128)(2,1)S(1)} %get-tuple-element.66), channel_id=1, source_target_pairs={{0,4},{2,6},{4,0},{6,2},{8,12},{10,14},{12,8},{14,10},{16,20},{18,... | collective-permute-start | bytes 688136 | tf_op jit(solution)/shard_map/ppermute | solution.py:54
  53.2 1.1 %collective-permute-start.19 = (bf16[2,32,1792]{2,1,0:T(8,128)(2,1)S(1)}, bf16[2,32,1792]{2,1,0:T(8,128)(2,1)S(1)}, u32[]{:S(2)}, u32[]{:S(2)}) collective-permute-start(bf16[2,32,1792]{2,1,0:T(8,128)(2,1)S(1)} %get-tuple-element.66), channel_id=1, source_target_pairs={{0,2},{2,0},{4,6},{6,4},{8,10},{10,8},{12,14},{14,12},{16,18},{18,... | collective-permute-start | bytes 688136 | tf_op jit(solution)/shard_map/ppermute | solution.py:54
  54.3 5.9 %collective-permute-done.21.refs_10_ = bf16[2,32,1792]{2,1,0:T(8,128)(2,1)S(1)} collective-permute-done((bf16[2,32,1792]{2,1,0:T(8,128)(2,1)S(1)}, bf16[2,32,1792]{2,1,0:T(8,128)(2,1)S(1)}, u32[]{:S(2)}, u32[]{:S(2)}) %collective-permute-start.21) | collective-permute-done | bytes 229408 | tf_op jit(solution)/shard_map/ppermute | solution.py:54
  60.2 3.0 %collective-permute-done.20.refs_9_ = bf16[2,32,1792]{2,1,0:T(8,128)(2,1)S(1)} collective-permute-done((bf16[2,32,1792]{2,1,0:T(8,128)(2,1)S(1)}, bf16[2,32,1792]{2,1,0:T(8,128)(2,1)S(1)}, u32[]{:S(2)}, u32[]{:S(2)}) %collective-permute-start.20) | collective-permute-done | bytes 229408 | tf_op jit(solution)/shard_map/ppermute | solution.py:54
  63.2 1.0 %shard_map.106 = (f32[32,2048]{1,0:T(8,128)S(1)}, bf16[32,2048]{1,0:T(8,128)(2,1)S(1)}, bf16[32,2048]{1,0:T(8,128)(2,1)S(1)}, bf16[32,2048]{1,0:T(8,128)(2,1)S(1)}) custom-call(s32[1]{0:T(128)} %bitcast.refs_0_, s32[16]{0:T(128)} %refs_1_.9, s32[2]{0:T(128)} %refs_2_.4, s32[2]{0:T(128)S(1)} %collective-permute-done.1.refs_3_, ...), custom_call_target="tpu_custom_call" | custom-call | tf_op jit(solution)/shard_map/pallas_call | solution.py:39
  64.2 0.8 %collective-permute-start.25 = (bf16[32,2048]{1,0:T(8,128)(2,1)S(1)}, bf16[32,2048]{1,0:T(8,128)(2,1)S(1)}, u32[]{:S(2)}, u32[]{:S(2)}) collective-permute-start(bf16[32,2048]{1,0:T(8,128)(2,1)S(1)} %get-tuple-element.55), channel_id=1, source_target_pairs={{0,8},{2,10},{4,12},{6,14},{8,0},{10,2},{12,4},{14,6},{16,24},{18,... | collective-permute-start | bytes 393224 | tf_op jit(solution)/shard_map/ppermute | solution.py:57
  65.0 2.0 %collective-permute-start.26 = (bf16[32,2048]{1,0:T(8,128)(2,1)S(1)}, bf16[32,2048]{1,0:T(8,128)(2,1)S(1)}, u32[]{:S(2)}, u32[]{:S(2)}) collective-permute-start(bf16[32,2048]{1,0:T(8,128)(2,1)S(1)} %get-tuple-element.56), channel_id=1, source_target_pairs={{0,16},{2,18},{4,20},{6,22},{8,24},{10,26},{12,28},{14,30},{16,0},... | collective-permute-start | bytes 393224 | tf_op jit(solution)/shard_map/ppermute | solution.py:57
  67.0 1.7 %collective-permute-start.27 = (bf16[32,2048]{1,0:T(8,128)(2,1)S(1)}, bf16[32,2048]{1,0:T(8,128)(2,1)S(1)}, u32[]{:S(2)}, u32[]{:S(2)}) collective-permute-start(bf16[32,2048]{1,0:T(8,128)(2,1)S(1)} %get-tuple-element.57), channel_id=1, source_target_pairs={{0,24},{2,26},{4,28},{6,30},{8,16},{10,18},{12,20},{14,22},{16,8},... | collective-permute-start | bytes 393224 | tf_op jit(solution)/shard_map/ppermute | solution.py:57
  68.7 7.9 %outputs.1 = (bf16[1536,1792]{1,0:T(8,128)(2,1)}, bf16[1536,256]{1,0:T(8,128)(2,1)}) custom-call(s32[1]{0:T(128)} %bitcast.1.core_ref, bf16[1536,256]{1,0:T(8,128)(2,1)S(1)} %get-tuple-element.36.own, bf16[1536,256]{1,0:T(8,128)(2,1)S(1)} %collective-permute-done.mate, bf16[1792,512]{1,0:T(8,128)(2,1)S(1)} %copy-done, ...), custom_call_target="tpu_custom_call" | custom-call | tf_op jit(solution)/shard_map/outputs/pallas_call | solution.py:245
  76.6 1.2 %collective-permute-done.26.refs_2_ = bf16[32,2048]{1,0:T(8,128)(2,1)S(1)} collective-permute-done((bf16[32,2048]{1,0:T(8,128)(2,1)S(1)}, bf16[32,2048]{1,0:T(8,128)(2,1)S(1)}, u32[]{:S(2)}, u32[]{:S(2)}) %collective-permute-start.26) | collective-permute-done | bytes 131104 | tf_op jit(solution)/shard_map/ppermute | solution.py:57
  77.8 0.7 shard_map.107
  (31 shorter events, 0.4 us)
Async XLA Ops:
  0.6 15.8 %collective-permute-start.3 = (s32[2]{0:T(128)}, s32[2]{0:T(128)S(1)}, u32[]{:S(2)}, u32[]{:S(2)}) collective-permute-start(s32[2]{0:T(128)} %refs_2_.4), channel_id=1, source_target_pairs={{0,6},{2,4},{4,2},{6,0},{8,14},{10,12},{12,10},{14,8},{16,22},{18,... | collective-permute-start | bytes 32 | tf_op jit(solution)/shard_map/ppermute | solution.py:54
  4.6 12.3 %collective-permute-start.2 = (s32[2]{0:T(128)}, s32[2]{0:T(128)S(1)}, u32[]{:S(2)}, u32[]{:S(2)}) collective-permute-start(s32[2]{0:T(128)} %refs_2_.4), channel_id=1, source_target_pairs={{0,4},{2,6},{4,0},{6,2},{8,12},{10,14},{12,8},{14,10},{16,20},{18,... | collective-permute-start | bytes 32 | tf_op jit(solution)/shard_map/ppermute | solution.py:54
  6.0 7.2 %copy-start = (bf16[1792,512]{1,0:T(8,128)(2,1)S(1)}, bf16[1792,512]{1,0:T(8,128)(2,1)}, u32[]{:S(2)}) copy-start(bf16[1792,512]{1,0:T(8,128)(2,1)} %w.1) | copy-start | bytes 5505028
  6.1 16.2 %collective-permute-start.6 = (bf16[32,1024]{1,0:T(8,128)(2,1)S(1)}, bf16[32,1024]{1,0:T(8,128)(2,1)S(1)}, u32[]{:S(2)}, u32[]{:S(2)}) collective-permute-start(bf16[32,1024]{1,0:T(8,128)(2,1)S(1)} %get-tuple-element.41.refs_6_), channel_id=1, source_target_pairs={{0,24},{2,26},{4,28},{6,30},{8,16},{10,18},{12,20},{14,22},{16,8},... | collective-permute-start | bytes 196616 | tf_op jit(solution)/shard_map/ppermute | solution.py:57
  9.7 14.6 %collective-permute-start.5 = (bf16[32,1024]{1,0:T(8,128)(2,1)S(1)}, bf16[32,1024]{1,0:T(8,128)(2,1)S(1)}, u32[]{:S(2)}, u32[]{:S(2)}) collective-permute-start(bf16[32,1024]{1,0:T(8,128)(2,1)S(1)} %get-tuple-element.41.refs_6_), channel_id=1, source_target_pairs={{0,16},{2,18},{4,20},{6,22},{8,24},{10,26},{12,28},{14,30},{16,0},... | collective-permute-start | bytes 196616 | tf_op jit(solution)/shard_map/ppermute | solution.py:57
  9.7 14.6 %collective-permute-start.4 = (bf16[32,1024]{1,0:T(8,128)(2,1)S(1)}, bf16[32,1024]{1,0:T(8,128)(2,1)S(1)}, u32[]{:S(2)}, u32[]{:S(2)}) collective-permute-start(bf16[32,1024]{1,0:T(8,128)(2,1)S(1)} %get-tuple-element.41.refs_6_), channel_id=1, source_target_pairs={{0,8},{2,10},{4,12},{6,14},{8,0},{10,2},{12,4},{14,6},{16,24},{18,... | collective-permute-start | bytes 196616 | tf_op jit(solution)/shard_map/ppermute | solution.py:57
  14.9 1.6 %copy-start.1 = (s32[2]{0:T(128)S(1)}, s32[2]{0:T(128)}, u32[]{:S(2)}) copy-start(s32[2]{0:T(128)} %refs_2_.4) | copy-start | bytes 28
  16.5 4.2 %collective-permute-start.1 = (s32[2]{0:T(128)S(1)}, s32[2]{0:T(128)S(1)}, u32[]{:S(2)}, u32[]{:S(2)}) collective-permute-start(s32[2]{0:T(128)S(1)} %copy-done.1), channel_id=1, source_target_pairs={{0,2},{2,0},{4,6},{6,4},{8,10},{10,8},{12,14},{14,12},{16,18},{18,... | collective-permute-start | bytes 32 | tf_op jit(solution)/shard_map/ppermute | solution.py:54
  17.0 9.0 %collective-permute-start.13 = (bf16[32,1024]{1,0:T(8,128)(2,1)S(1)}, bf16[32,1024]{1,0:T(8,128)(2,1)S(1)}, u32[]{:S(2)}, u32[]{:S(2)}) collective-permute-start(bf16[32,1024]{1,0:T(8,128)(2,1)S(1)} %get-tuple-element.46.refs_6_), channel_id=1, source_target_pairs={{0,24},{2,26},{4,28},{6,30},{8,16},{10,18},{12,20},{14,22},{16,8},... | collective-permute-start | bytes 196616 | tf_op jit(solution)/shard_map/ppermute | solution.py:57
  20.7 6.0 %collective-permute-start.12 = (bf16[32,1024]{1,0:T(8,128)(2,1)S(1)}, bf16[32,1024]{1,0:T(8,128)(2,1)S(1)}, u32[]{:S(2)}, u32[]{:S(2)}) collective-permute-start(bf16[32,1024]{1,0:T(8,128)(2,1)S(1)} %get-tuple-element.46.refs_6_), channel_id=1, source_target_pairs={{0,16},{2,18},{4,20},{6,22},{8,24},{10,26},{12,28},{14,30},{16,0},... | collective-permute-start | bytes 196616 | tf_op jit(solution)/shard_map/ppermute | solution.py:57
  22.3 4.8 %collective-permute-start.11 = (bf16[32,1024]{1,0:T(8,128)(2,1)S(1)}, bf16[32,1024]{1,0:T(8,128)(2,1)S(1)}, u32[]{:S(2)}, u32[]{:S(2)}) collective-permute-start(bf16[32,1024]{1,0:T(8,128)(2,1)S(1)} %get-tuple-element.46.refs_6_), channel_id=1, source_target_pairs={{0,8},{2,10},{4,12},{6,14},{8,0},{10,2},{12,4},{14,6},{16,24},{18,... | collective-permute-start | bytes 196616 | tf_op jit(solution)/shard_map/ppermute | solution.py:57
  25.2 7.8 %collective-permute-start.7 = (bf16[2,32,1024]{2,1,0:T(8,128)(2,1)S(1)}, bf16[2,32,1024]{2,1,0:T(8,128)(2,1)S(1)}, u32[]{:S(2)}, u32[]{:S(2)}) collective-permute-start(bf16[2,32,1024]{2,1,0:T(8,128)(2,1)S(1)} %get-tuple-element.42), channel_id=1, source_target_pairs={{0,2},{2,0},{4,6},{6,4},{8,10},{10,8},{12,14},{14,12},{16,18},{18,... | collective-permute-start | bytes 393224 | tf_op jit(solution)/shard_map/ppermute | solution.py:54
  27.9 13.5 %collective-permute-start.14 = (bf16[2,32,1024]{2,1,0:T(8,128)(2,1)S(1)}, bf16[2,32,1024]{2,1,0:T(8,128)(2,1)S(1)}, u32[]{:S(2)}, u32[]{:S(2)}) collective-permute-start(bf16[2,32,1024]{2,1,0:T(8,128)(2,1)S(1)} %get-tuple-element.47), channel_id=1, source_target_pairs={{0,2},{2,0},{4,6},{6,4},{8,10},{10,8},{12,14},{14,12},{16,18},{18,... | collective-permute-start | bytes 393224 | tf_op jit(solution)/shard_map/ppermute | solution.py:54
  28.7 12.7 %collective-permute-start.15 = (bf16[2,32,1024]{2,1,0:T(8,128)(2,1)S(1)}, bf16[2,32,1024]{2,1,0:T(8,128)(2,1)S(1)}, u32[]{:S(2)}, u32[]{:S(2)}) collective-permute-start(bf16[2,32,1024]{2,1,0:T(8,128)(2,1)S(1)} %get-tuple-element.48), channel_id=1, source_target_pairs={{0,4},{2,6},{4,0},{6,2},{8,12},{10,14},{12,8},{14,10},{16,20},{18,... | collective-permute-start | bytes 393224 | tf_op jit(solution)/shard_map/ppermute | solution.py:54
  30.2 11.2 %collective-permute-start.16 = (bf16[2,32,1024]{2,1,0:T(8,128)(2,1)S(1)}, bf16[2,32,1024]{2,1,0:T(8,128)(2,1)S(1)}, u32[]{:S(2)}, u32[]{:S(2)}) collective-permute-start(bf16[2,32,1024]{2,1,0:T(8,128)(2,1)S(1)} %get-tuple-element.49), channel_id=1, source_target_pairs={{0,6},{2,4},{4,2},{6,0},{8,14},{10,12},{12,10},{14,8},{16,22},{18,... | collective-permute-start | bytes 393224 | tf_op jit(solution)/shard_map/ppermute | solution.py:54
  31.5 8.6 %collective-permute-start.8 = (bf16[2,32,1024]{2,1,0:T(8,128)(2,1)S(1)}, bf16[2,32,1024]{2,1,0:T(8,128)(2,1)S(1)}, u32[]{:S(2)}, u32[]{:S(2)}) collective-permute-start(bf16[2,32,1024]{2,1,0:T(8,128)(2,1)S(1)} %get-tuple-element.43), channel_id=1, source_target_pairs={{0,4},{2,6},{4,0},{6,2},{8,12},{10,14},{12,8},{14,10},{16,20},{18,... | collective-permute-start | bytes 393224 | tf_op jit(solution)/shard_map/ppermute | solution.py:54
  33.0 7.1 %collective-permute-start.9 = (bf16[2,32,1024]{2,1,0:T(8,128)(2,1)S(1)}, bf16[2,32,1024]{2,1,0:T(8,128)(2,1)S(1)}, u32[]{:S(2)}, u32[]{:S(2)}) collective-permute-start(bf16[2,32,1024]{2,1,0:T(8,128)(2,1)S(1)} %get-tuple-element.44), channel_id=1, source_target_pairs={{0,6},{2,4},{4,2},{6,0},{8,14},{10,12},{12,10},{14,8},{16,22},{18,... | collective-permute-start | bytes 393224 | tf_op jit(solution)/shard_map/ppermute | solution.py:54
  40.1 28.6 %collective-permute-start = (bf16[1536,256]{1,0:T(8,128)(2,1)S(1)}, bf16[1536,256]{1,0:T(8,128)(2,1)S(1)}, u32[]{:S(2)}, u32[]{:S(2)}) collective-permute-start(bf16[1536,256]{1,0:T(8,128)(2,1)S(1)} %get-tuple-element.36.own), channel_id=1, source_target_pairs={{0,1},{1,0},{2,3},{3,2},{4,5},{5,4},{6,7},{7,6},{8,9},{9,8},{10,11... | collective-permute-start | bytes 2359304 | tf_op jit(solution)/shard_map/ppermute | solution.py:60
  40.1 28.5 %collective-permute-start.18 = (f32[1536,256]{1,0:T(8,128)S(1)}, f32[1536,256]{1,0:T(8,128)S(1)}, u32[]{:S(2)}, u32[]{:S(2)}) collective-permute-start(f32[1536,256]{1,0:T(8,128)S(1)} %pad_maximum_fusion), channel_id=1, source_target_pairs={{0,1},{1,0},{2,3},{3,2},{4,5},{5,4},{6,7},{7,6},{8,9},{9,8},{10,11... | collective-permute-start | bytes 4718600 | tf_op jit(solution)/shard_map/ppermute | solution.py:60
  43.9 1.5 %collective-permute-start.17 = (f32[2,32,768]{2,1,0:T(8,128)S(1)}, f32[2,32,768]{2,1,0:T(8,128)S(1)}, u32[]{:S(2)}, u32[]{:S(2)}) collective-permute-start(f32[2,32,768]{2,1,0:T(8,128)S(1)} %fusion.7), channel_id=1, source_target_pairs={{0,1},{1,0},{2,3},{3,2},{4,5},{5,4},{6,7},{7,6},{8,9},{9,8},{10,11... | collective-permute-start | bytes 589832 | tf_op jit(solution)/shard_map/ppermute | solution.py:60
  44.3 4.1 %collective-permute-start.10 = (f32[2,32,768]{2,1,0:T(8,128)S(1)}, f32[2,32,768]{2,1,0:T(8,128)S(1)}, u32[]{:S(2)}, u32[]{:S(2)}) collective-permute-start(f32[2,32,768]{2,1,0:T(8,128)S(1)} %fusion.6), channel_id=1, source_target_pairs={{0,1},{1,0},{2,3},{3,2},{4,5},{5,4},{6,7},{7,6},{8,9},{9,8},{10,11... | collective-permute-start | bytes 589832 | tf_op jit(solution)/shard_map/ppermute | solution.py:60
  45.9 4.9 %collective-permute-start.24 = (bf16[2,32,256]{2,1,0:T(8,128)(2,1)S(1)}, bf16[2,32,256]{2,1,0:T(8,128)(2,1)S(1)}, u32[]{:S(2)}, u32[]{:S(2)}) collective-permute-start(bf16[2,32,256]{2,1,0:T(8,128)(2,1)S(1)} %get-tuple-element.68), channel_id=1, source_target_pairs={{0,6},{2,4},{4,2},{6,0},{8,14},{10,12},{12,10},{14,8},{16,22},{18,... | collective-permute-start | bytes 98312 | tf_op jit(solution)/shard_map/ppermute | solution.py:54
  47.5 4.8 %collective-permute-start.23 = (bf16[2,32,256]{2,1,0:T(8,128)(2,1)S(1)}, bf16[2,32,256]{2,1,0:T(8,128)(2,1)S(1)}, u32[]{:S(2)}, u32[]{:S(2)}) collective-permute-start(bf16[2,32,256]{2,1,0:T(8,128)(2,1)S(1)} %get-tuple-element.68), channel_id=1, source_target_pairs={{0,4},{2,6},{4,0},{6,2},{8,12},{10,14},{12,8},{14,10},{16,20},{18,... | collective-permute-start | bytes 98312 | tf_op jit(solution)/shard_map/ppermute | solution.py:54
  48.4 4.8 %collective-permute-start.22 = (bf16[2,32,256]{2,1,0:T(8,128)(2,1)S(1)}, bf16[2,32,256]{2,1,0:T(8,128)(2,1)S(1)}, u32[]{:S(2)}, u32[]{:S(2)}) collective-permute-start(bf16[2,32,256]{2,1,0:T(8,128)(2,1)S(1)} %get-tuple-element.68), channel_id=1, source_target_pairs={{0,2},{2,0},{4,6},{6,4},{8,10},{10,8},{12,14},{14,12},{16,18},{18,... | collective-permute-start | bytes 98312 | tf_op jit(solution)/shard_map/ppermute | solution.py:54
  50.8 9.4 %collective-permute-start.21 = (bf16[2,32,1792]{2,1,0:T(8,128)(2,1)S(1)}, bf16[2,32,1792]{2,1,0:T(8,128)(2,1)S(1)}, u32[]{:S(2)}, u32[]{:S(2)}) collective-permute-start(bf16[2,32,1792]{2,1,0:T(8,128)(2,1)S(1)} %get-tuple-element.66), channel_id=1, source_target_pairs={{0,6},{2,4},{4,2},{6,0},{8,14},{10,12},{12,10},{14,8},{16,22},{18,... | collective-permute-start | bytes 688136 | tf_op jit(solution)/shard_map/ppermute | solution.py:54
  52.4 10.9 %collective-permute-start.20 = (bf16[2,32,1792]{2,1,0:T(8,128)(2,1)S(1)}, bf16[2,32,1792]{2,1,0:T(8,128)(2,1)S(1)}, u32[]{:S(2)}, u32[]{:S(2)}) collective-permute-start(bf16[2,32,1792]{2,1,0:T(8,128)(2,1)S(1)} %get-tuple-element.66), channel_id=1, source_target_pairs={{0,4},{2,6},{4,0},{6,2},{8,12},{10,14},{12,8},{14,10},{16,20},{18,... | collective-permute-start | bytes 688136 | tf_op jit(solution)/shard_map/ppermute | solution.py:54
  53.2 10.0 %collective-permute-start.19 = (bf16[2,32,1792]{2,1,0:T(8,128)(2,1)S(1)}, bf16[2,32,1792]{2,1,0:T(8,128)(2,1)S(1)}, u32[]{:S(2)}, u32[]{:S(2)}) collective-permute-start(bf16[2,32,1792]{2,1,0:T(8,128)(2,1)S(1)} %get-tuple-element.66), channel_id=1, source_target_pairs={{0,2},{2,0},{4,6},{6,4},{8,10},{10,8},{12,14},{14,12},{16,18},{18,... | collective-permute-start | bytes 688136 | tf_op jit(solution)/shard_map/ppermute | solution.py:54
  64.2 12.4 %collective-permute-start.25 = (bf16[32,2048]{1,0:T(8,128)(2,1)S(1)}, bf16[32,2048]{1,0:T(8,128)(2,1)S(1)}, u32[]{:S(2)}, u32[]{:S(2)}) collective-permute-start(bf16[32,2048]{1,0:T(8,128)(2,1)S(1)} %get-tuple-element.55), channel_id=1, source_target_pairs={{0,8},{2,10},{4,12},{6,14},{8,0},{10,2},{12,4},{14,6},{16,24},{18,... | collective-permute-start | bytes 393224 | tf_op jit(solution)/shard_map/ppermute | solution.py:57
  65.0 12.8 %collective-permute-start.26 = (bf16[32,2048]{1,0:T(8,128)(2,1)S(1)}, bf16[32,2048]{1,0:T(8,128)(2,1)S(1)}, u32[]{:S(2)}, u32[]{:S(2)}) collective-permute-start(bf16[32,2048]{1,0:T(8,128)(2,1)S(1)} %get-tuple-element.56), channel_id=1, source_target_pairs={{0,16},{2,18},{4,20},{6,22},{8,24},{10,26},{12,28},{14,30},{16,0},... | collective-permute-start | bytes 393224 | tf_op jit(solution)/shard_map/ppermute | solution.py:57
  67.0 10.8 %collective-permute-start.27 = (bf16[32,2048]{1,0:T(8,128)(2,1)S(1)}, bf16[32,2048]{1,0:T(8,128)(2,1)S(1)}, u32[]{:S(2)}, u32[]{:S(2)}) collective-permute-start(bf16[32,2048]{1,0:T(8,128)(2,1)S(1)} %get-tuple-element.57), channel_id=1, source_target_pairs={{0,24},{2,26},{4,28},{6,30},{8,16},{10,18},{12,20},{14,22},{16,8},... | collective-permute-start | bytes 393224 | tf_op jit(solution)/shard_map/ppermute | solution.py:57

commit v5 on v4

--- a/solution.py
+++ b/solution.py
@@ -71,33 +71,28 @@
         rank = down.shape[2]
         cols = grad.shape[1]
         length = rows // seqs
-        block = math.gcd(length, 384)
+        block = math.gcd(length, 768)
         me = lax.axis_index("dp").astype(jnp.int32)[None]
         core = lax.axis_index("mp").astype(jnp.int32)[None]
         low_core = lax.axis_index("mp") == 0
         me, core, low_core, down, up, tenant = lax.optimization_barrier((me, core, low_core, down, up, tenant))
 
-        first = max(width * 768 // 1792 // 128 * 128, 128)
+        first = max(width * 512 // 1792 // 128 * 128, 128)
         rest = width - first
 
-        def join(down_ref, up_ref, out0, out1):
-            out0[:, :first] = down_ref[:, :first]
-            out0[:, first:] = up_ref[...]
-            out1[...] = down_ref[:, first:]
+        def join(down_ref, up_ref, out):
+            out[:, :width] = down_ref[...]
+            out[:, width:] = up_ref[...]
 
         mine = pl.pallas_call(
             join,
-            out_shape=[pltpu.VMEM((rank, first + cols), BF16), pltpu.VMEM((rank, rest), BF16)],
+            out_shape=pltpu.VMEM((rank, width + cols), BF16),
             compiler_params=SMALL,
             name="join",
-        )(
-            fixed(jnp.swapaxes(down[0], 0, 1)),
-            fixed(up[0]),
-        )
-        held, tenants = [[mine[0]], [mine[1]]], [tenant]
-        for p in range(2):
-            for d in range(1, r):
-                held[p].append(send_outer(mine[p], d))
+        )(fixed(jnp.swapaxes(down[0], 0, 1)), fixed(up[0]))
+        held, tenants = [mine], [tenant]
+        for d in range(1, r):
+            held.append(send_outer(mine, d))
         for d in range(1, q):
             tenants.append(send_inner(tenant, d))
         ints = [me, fixed(table), fixed(tenant)] + tenants[1:]
@@ -135,16 +130,23 @@
 
                         @pl.when(have == k)
                         def _(d=d, j=j, k=k):
-                            outs[d - 1][j] = parts[k][...]
-
-        got = []
+                            outs[d - 1][j, :, :first] = parts[k][:, :first]
+                            outs[d - 1][j, :, first:] = parts[k][:, width:]
+                            outs[q + d - 2][j] = parts[k][:, first:width]
+
+        sent = kernel_call(
+            pick,
+            ints,
+            held,
+            [jax.ShapeDtypeStruct((seqs, rank, first + cols), BF16)] * (q - 1)
+            + [jax.ShapeDtypeStruct((seqs, rank, rest), BF16)] * (q - 1),
+        )
+        got = [[], []]
         for p in range(2):
-            sent = kernel_call(pick, ints, held[p], [jax.ShapeDtypeStruct((seqs,) + held[p][0].shape, BF16)] * (q - 1))
-            got.append([])
             for d in range(1, q):
-                got[p].append(send_inner(sent[d - 1], d))
-
-        def chosen(refs, store):
+                got[p].append(send_inner(sent[p * (q - 1) + d - 1], d))
+
+        def chosen(refs, from_peer, from_held):
             ins, parts, gots = refs[: 2 + q], refs[2 + q : 2 + q + r], refs[2 + q + r : 1 + 2 * q + r]
             inner, outer = ins[0][0] % q, ins[0][0] // q
             for j in range(seqs):
@@ -155,40 +157,47 @@
 
                     @pl.when(way == d)
                     def _(d=d, j=j):
-                        store(j, gots[d - 1].at[j])
+                        from_peer(j, gots[d - 1].at[j])
 
                 for k in range(r):
 
                     @pl.when((way == 0) & (have == k))
                     def _(j=j, k=k):
-                        store(j, parts[k])
+                        from_held(j, parts[k])
 
         def choose0(*refs):
             down_out, up_out = refs[-2:]
 
-            def store(j, ref):
+            def from_peer(j, ref):
                 down_out[j] = ref[:, :first]
                 up_out[j] = ref[:, first:]
 
-            chosen(refs, store)
+            def from_held(j, ref):
+                down_out[j] = ref[:, :first]
+                up_out[j] = ref[:, width:]
+
+            chosen(refs, from_peer, from_held)
 
         def choose1(*refs):
             down_in, down_out = refs[-2:]
             down_out[:, :, :first] = down_in[...]
 
-            def store(j, ref):
+            def from_peer(j, ref):
                 down_out[j, :, first:] = ref[...]
 
-            chosen(refs, store)
+            def from_held(j, ref):
+                down_out[j, :, first:] = ref[:, first:width]
+
+            chosen(refs, from_peer, from_held)
 
         down_first, up_s = kernel_call(
             choose0,
             ints,
-            held[0] + got[0],
+            held + got[0],
             [jax.ShapeDtypeStruct((seqs, rank, first), BF16), jax.ShapeDtypeStruct((seqs, rank, cols), BF16)],
         )
         (down_s,) = kernel_call(
-            choose1, ints, held[1] + got[1] + [down_first], [jax.ShapeDtypeStruct((seqs, rank, width), BF16)]
+            choose1, ints, held + got[1] + [down_first], [jax.ShapeDtypeStruct((seqs, rank, width), BF16)]
         )
 
         h3 = hidden.reshape(seqs, length, width)
@@ -197,6 +206,12 @@
             other = swap(grad_in)
         else:
             grad_full = lax.all_gather(grad, "mp", axis=1, tiled=True)
+        if m == 2:
+            both = jnp.where(
+                low_core, jnp.concatenate([grad_in, other], axis=1), jnp.concatenate([other, grad_in], axis=1)
+            )
+            pre = lax.dot_general(both, weight, (((1,), (1,)), ((), ())), preferred_element_type=F32)
+            pre = pltpu.with_memory_space_constraint(pre, pltpu.VMEM)
         base = []
         for j in range(seqs):
             base.append(jnp.dot(h3[j], weight, preferred_element_type=F32))
@@ -213,19 +228,16 @@
         if m == 2:
             per = length // block
 
-            def outputs(core_ref, own, mate, w, coeff, factor, low_ref, up_ref, got_ref, *rest_refs):
-                bases, (out, values_out, lhs) = rest_refs[:seqs], rest_refs[seqs:]
+            def outputs(core_ref, pre_ref, coeff, factor, low_ref, up_ref, got_ref, *rest_refs):
+                bases, (out, values_out) = rest_refs[:seqs], rest_refs[seqs:]
                 step = pl.program_id(0)
                 here = pl.multiple_of(core_ref[0] * cols, math.gcd(cols, 128))
-                there = pl.multiple_of((1 - core_ref[0]) * cols, math.gcd(cols, 128))
-                lhs[:, pl.ds(here, cols)] = own[...]
-                lhs[:, pl.ds(there, cols)] = mate[...]
-                total = lax.dot_general(
-                    lhs[...], w[...], (((1,), (1,)), ((), ())), preferred_element_type=F32
-                ) + lax.dot_general(
-                    coeff[0], factor[0], (((0,), (0,)), ((), ())), preferred_element_type=F32
-                )
-                out[...] = total.astype(BF16)
+                out[...] = (
+                    pre_ref[pl.ds(pl.multiple_of(step * block, block), block), :]
+                    + lax.dot_general(
+                        coeff[0], factor[0], (((0,), (0,)), ((), ())), preferred_element_type=F32
+                    )
+                ).astype(BF16)
                 term = got_ref[...] + lax.dot_general(
                     low_ref[0],
                     up_ref[0].astype(F32),
@@ -251,8 +263,6 @@
                 ],
                 in_specs=[
                     SMEM,
-                    rows_of,
-                    rows_of,
                     VMEM,
                     coeff_of,
                     pl.BlockSpec((1, rank, width), lambda i: (i // per, 0, 0)),
@@ -262,10 +272,9 @@
                 ]
                 + [VMEM] * seqs,
                 out_specs=[pl.BlockSpec((block, width), lambda i: (i, 0)), rows_of],
-                scratch_shapes=[pltpu.VMEM((block, m * cols), BF16)],
-                compiler_params=pltpu.CompilerParams(vmem_limit_bytes=24 << 20),
+                compiler_params=pltpu.CompilerParams(vmem_limit_bytes=32 << 20),
                 name="outputs",
-            )(core, grad_in, other, weight, back_low, down_s, low, up_s, base_got, *base)[::-1]
+            )(core, pre, back_low, down_s, low, up_s, base_got, *base)[::-1]
         else:
             values = (
                 base_own.reshape(seqs, length, cols)
@@ -276,7 +285,8 @@
                 + jnp.einsum("srl,srw->slw", back_low, down_s, preferred_element_type=F32).reshape(rows, width)
             ).astype(BF16)
 
-        items = [down_seq, up_seq]
+        early = (width + cols) * 5 // 1024 * 128
+        items = [down_seq[:, :, :early], jnp.concatenate([down_seq[:, :, early:], up_seq], axis=2)]
         near = [[], []]
         for p in range(2):
             small = items[p].astype(BF16)
@@ -284,8 +294,8 @@
                 near[p].append(send_inner(small, d))
 
         def gather_items(*refs):
-            ins, own, others = refs[: 2 + q], refs[2 + q : 4 + q], refs[4 + q : 2 + 3 * q]
-            outs, acc = refs[2 + 3 * q : -1], refs[-1]
+            ins, own, others = refs[: 2 + q], refs[2 + q], refs[3 + q : 2 + 2 * q]
+            outs, acc = refs[2 + 2 * q : -1], refs[-1]
             inner, outer = ins[0][0] % q, ins[0][0] // q
             acc[...] = jnp.zeros_like(acc)
             for d in range(q):
@@ -295,39 +305,42 @@
                     @pl.when(holder % q == inner)
                     def _(d=d, j=j, holder=holder):
                         k = offset(outer, holder // q, r)
-                        for p, at in ((0, slice(0, width)), (1, slice(width, None))):
-                            piece = own[p] if d == 0 else others[p * (q - 1) + d - 1]
-                            acc[k, :, at] += piece[j].astype(F32)
+                        item = own[j] if d == 0 else others[d - 1][j].astype(F32)
+                        acc[k] += item
 
             outs[0][...] = acc[0]
             for k in range(1, r):
                 outs[k][...] = acc[k].astype(BF16)
 
-        shape = (rank, width + cols)
-        parts = kernel_call(
-            gather_items,
-            ints,
-            items + near[0] + near[1],
-            [jax.ShapeDtypeStruct(shape, F32)] + [jax.ShapeDtypeStruct(shape, BF16)] * (r - 1),
-            [pltpu.VMEM((r,) + shape, F32)],
-        )
-        arrived = []
-        for k in range(1, r):
-            arrived.append(send_outer(parts[k], opposite(k, r)))
+        totals, arrived = [], []
+        for p in range(2):
+            shape = items[p].shape[1:]
+            parts = kernel_call(
+                gather_items,
+                ints,
+                [items[p]] + near[p],
+                [jax.ShapeDtypeStruct(shape, F32)] + [jax.ShapeDtypeStruct(shape, BF16)] * (r - 1),
+                [pltpu.VMEM((r,) + shape, F32)],
+            )
+            totals.append(parts[0])
+            for k in range(1, r):
+                arrived.append(send_outer(parts[k], opposite(k, r)))
         values, hidden_grad, arrived = lax.optimization_barrier((values, hidden_grad, arrived))
 
         def finish(*refs):
-            others, down_out, up_out = refs[:r], refs[r], refs[r + 1]
-            total = others[0][...]
-            for other in others[1:]:
-                total = total + other[...].astype(F32)
-            down_out[...] = total[:, :width]
-            up_out[...] = total[:, width:]
+            own, others, down_out, up_out = refs[:2], refs[2 : 2 * r], refs[2 * r], refs[2 * r + 1]
+            total = [own[0][...], own[1][...]]
+            for p in range(2):
+                for other in others[p * (r - 1) : (p + 1) * (r - 1)]:
+                    total[p] = total[p] + other[...].astype(F32)
+            down_out[:, :early] = total[0]
+            down_out[:, early:] = total[1][:, : width - early]
+            up_out[...] = total[1][:, width - early :]
 
         down_grad, up_grad = kernel_call(
             finish,
             [],
-            [parts[0]] + arrived,
+            totals + arrived,
             [jax.ShapeDtypeStruct((rank, width), F32), jax.ShapeDtypeStruct((rank, cols), F32)],
             inside=False,
         )

time: 78.8 us -> 74.8 us (0.949)
  waiting for transfers between devices: 18.4 us -> 14.3 us
  matrix products: 6.68 us -> 9.75 us
  Pallas kernels: 16.6 us -> 13.7 us
    dot_general x0 -> x1, matrix products: none -> 3.08 us  [local(): lax.dot_general(both, weight, (((1,), (1,)), ((), ())), preferred_element...]
    ppermute x15, starting transfers between devices: 18.3 us -> 21.3 us  [send_inner(): lax.ppermute(x, 'dp', [(i, i // q * q + peer(i % q, d, q)) for i in range...]
    pallas_call x1, Pallas kernels: 7.93 us -> 5.06 us  [local(): pl.pallas_call(outputs, grid=(rows // block,), out_shape=[jax.ShapeDtypeS...]
    ppermute x9, starting transfers between devices: 16.2 us -> 13.6 us  [send_outer(): lax.ppermute(x, 'dp', [(i, peer(i // q, d, r) * q + i % q) for i in range...]
    ppermute x9, waiting for transfers between devices: 2.22 us -> 0.02 us  [send_outer(): lax.ppermute(x, 'dp', [(i, peer(i // q, d, r) * q + i % q) for i in range...]
    ppermute x15, waiting for transfers between devices: 15.6 us -> 13.9 us  [send_inner(): lax.ppermute(x, 'dp', [(i, i // q * q + peer(i % q, d, q)) for i in range...]
    ppermute x4, starting transfers between devices: 1.06 us -> 0.08 us  [swap(): return lax.ppermute(x, 'mp', [(0, 1), (1, 0)])]
  transfers between devices with their start and end apart: 28 -> 28, of which waited for: 8 -> 9; matrix products, arithmetic and copies ran while one was open for 9% -> 14% of each run, Pallas kernels for 20% -> 17%
where the time goes in v5:
time: 74.8 us; the launch traced here: 74.6 us
  starting transfers between devices  35 us (47%)
  waiting for transfers between devices  14.3 us (19%)
  Pallas kernels  13.7 us (18%)
  matrix products  9.75 us (13%)
  between operations  0.87 us (1%)
    ppermute x15, starting transfers between devices, send_inner(): lax.ppermute(x, 'dp', [(i, i // q * q + peer(i % q, d, q)) for i in range...  21.3 us
    ppermute x15, waiting for transfers between devices, send_inner(): lax.ppermute(x, 'dp', [(i, i // q * q + peer(i % q, d, q)) for i in range...  13.9 us
    ppermute x9, starting transfers between devices, send_outer(): lax.ppermute(x, 'dp', [(i, peer(i // q, d, r) * q + i % q) for i in range...  13.6 us
    pallas_call x1, Pallas kernels, local(): pl.pallas_call(outputs, grid=(rows // block,), out_shape=[jax.ShapeDtypeS...  5.06 us
    pallas_call x6, Pallas kernels, kernel_call(): pl.pallas_call(body, out_shape=[pltpu.VMEM(o.shape, o.dtype) if inside el...  4.97 us
    dot_general x2, matrix products, local(): base.append(jnp.dot(h3[j], weight, preferred_element_type=F32))  3.15 us
    dot_general x1, matrix products, local(): lax.dot_general(both, weight, (((1,), (1,)), ((), ())), preferred_element...  3.08 us
    pallas_call x1, Pallas kernels, local(): pl.pallas_call(load, out_shape=[pltpu.VMEM(hidden.shape, BF16), pltpu.VME...  2.77 us
  transfers between devices with their start and end apart: 28, of which 9 were waited for; matrix products, arithmetic and copies ran while one was open for 14% of the time, Pallas kernels for 17%

profile of v5, /device:TPU:0, one launch (start us, length us, event | category | flops | bytes accessed | tf_op | source)
XLA Modules:
  0.0 74.6 jit_solution(5072037344332631070)
XLA Ops:
  0.7 4.0 %collective-permute-start.3 = (s32[2]{0:T(128)}, s32[2]{0:T(128)S(1)}, u32[]{:S(2)}, u32[]{:S(2)}) collective-permute-start(s32[2]{0:T(128)} %refs_2_.4), channel_id=1, source_target_pairs={{0,6},{2,4},{4,2},{6,0},{8,14},{10,12},{12,10},{14,8},{16,22},{18,... | collective-permute-start | bytes 32 | tf_op jit(solution)/shard_map/ppermute | solution.py:54
  4.6 0.5 collective-permute-start.2
  5.2 0.9 %join.1.refs_6_ = bf16[32,2048]{1,0:T(8,128)(2,1)S(1)} custom-call(bf16[32,1792]{1,0:T(8,128)(2,1)} %bitcast.27, bf16[32,256]{1,0:T(8,128)(2,1)} %bitcast.28), custom_call_target="tpu_custom_call" | custom-call | tf_op jit(solution)/shard_map/join/pallas_call | solution.py:87
  6.1 3.7 %collective-permute-start.6 = (bf16[32,2048]{1,0:T(8,128)(2,1)S(1)}, bf16[32,2048]{1,0:T(8,128)(2,1)S(1)}, u32[]{:S(2)}, u32[]{:S(2)}) collective-permute-start(bf16[32,2048]{1,0:T(8,128)(2,1)S(1)} %join.1.refs_6_), channel_id=1, source_target_pairs={{0,24},{2,26},{4,28},{6,30},{8,16},{10,18},{12,20},{14,22},{16,8},... | collective-permute-start | bytes 393224 | tf_op jit(solution)/shard_map/ppermute | solution.py:57
  9.7 0.8 %collective-permute-start.4 = (bf16[32,2048]{1,0:T(8,128)(2,1)S(1)}, bf16[32,2048]{1,0:T(8,128)(2,1)S(1)}, u32[]{:S(2)}, u32[]{:S(2)}) collective-permute-start(bf16[32,2048]{1,0:T(8,128)(2,1)S(1)} %join.1.refs_6_), channel_id=1, source_target_pairs={{0,8},{2,10},{4,12},{6,14},{8,0},{10,2},{12,4},{14,6},{16,24},{18,... | collective-permute-start | bytes 393224 | tf_op jit(solution)/shard_map/ppermute | solution.py:57
  10.5 2.8 %load.1 = (bf16[1536,1792]{1,0:T(8,128)(2,1)S(1)}, bf16[1536,256]{1,0:T(8,128)(2,1)S(1)}) custom-call(bf16[1536,1792]{1,0:T(8,128)(2,1)} %x_ref.1, bf16[1536,256]{1,0:T(8,128)(2,1)} %g_ref.1), custom_call_target="tpu_custom_call" | custom-call | tf_op jit(solution)/shard_map/load/pallas_call | solution.py:110
  13.3 1.6 %fusion.rest_refs_1_ = f32[768,512]{1,0:T(8,128)S(1)} fusion(bf16[1792,512]{1,0:T(8,128)(2,1)S(1)} %copy-done, bf16[1536,1792]{1,0:T(8,128)(2,1)S(1)} %get-tuple-element.55), kind=kOutput, calls=%fused_computation | convolution fusion | flops 1409286144 | bytes 6160384 | tf_op jit(solution)/shard_map/dot_general | solution.py:217
  14.9 1.6 %fusion.2.rest_refs_0_ = f32[768,512]{1,0:T(8,128)S(1)} fusion(bf16[1792,512]{1,0:T(8,128)(2,1)S(1)} %copy-done, bf16[1536,1792]{1,0:T(8,128)(2,1)S(1)} %get-tuple-element.55), kind=kOutput, calls=%fused_computation.2 | convolution fusion | flops 1409286144 | bytes 6160384 | tf_op jit(solution)/shard_map/dot_general | solution.py:217
  16.7 0.4 copy-done.1
  17.1 0.4 collective-permute-start.1
  17.5 3.2 %collective-permute-done.1.refs_3_ = s32[2]{0:T(128)S(1)} collective-permute-done((s32[2]{0:T(128)S(1)}, s32[2]{0:T(128)S(1)}, u32[]{:S(2)}, u32[]{:S(2)}) %collective-permute-start.1) | collective-permute-done | bytes 40 | tf_op jit(solution)/shard_map/ppermute | solution.py:54
  20.7 0.9 %shard_map.102 = (bf16[2,32,768]{2,1,0:T(8,128)(2,1)S(1)}, bf16[2,32,768]{2,1,0:T(8,128)(2,1)S(1)}, bf16[2,32,768]{2,1,0:T(8,128)(2,1)S(1)}, bf16[2,32,1280]{2,1...) custom-call(s32[1]{0:T(128)} %bitcast.refs_0_, s32[16]{0:T(128)} %refs_1_.9, ...), custom_call_target="tpu_custom_call" | custom-call | tf_op jit(solution)/shard_map/pallas_call | solution.py:39
  21.6 0.5 collective-permute-start.7
  22.1 1.7 %collective-permute-start.8 = (bf16[2,32,768]{2,1,0:T(8,128)(2,1)S(1)}, bf16[2,32,768]{2,1,0:T(8,128)(2,1)S(1)}, u32[]{:S(2)}, u32[]{:S(2)}) collective-permute-start(bf16[2,32,768]{2,1,0:T(8,128)(2,1)S(1)} %get-tuple-element.48), channel_id=1, source_target_pairs={{0,4},{2,6},{4,0},{6,2},{8,12},{10,14},{12,8},{14,10},{16,20},{18,... | collective-permute-start | bytes 294920 | tf_op jit(solution)/shard_map/ppermute | solution.py:54
  23.7 1.4 %collective-permute-start.9 = (bf16[2,32,768]{2,1,0:T(8,128)(2,1)S(1)}, bf16[2,32,768]{2,1,0:T(8,128)(2,1)S(1)}, u32[]{:S(2)}, u32[]{:S(2)}) collective-permute-start(bf16[2,32,768]{2,1,0:T(8,128)(2,1)S(1)} %get-tuple-element.49), channel_id=1, source_target_pairs={{0,6},{2,4},{4,2},{6,0},{8,14},{10,12},{12,10},{14,8},{16,22},{18,... | collective-permute-start | bytes 294920 | tf_op jit(solution)/shard_map/ppermute | solution.py:54
  25.4 1.2 %collective-permute-done.7.refs_10_ = bf16[2,32,768]{2,1,0:T(8,128)(2,1)S(1)} collective-permute-done((bf16[2,32,768]{2,1,0:T(8,128)(2,1)S(1)}, bf16[2,32,768]{2,1,0:T(8,128)(2,1)S(1)}, u32[]{:S(2)}, u32[]{:S(2)}) %collective-permute-start.7) | collective-permute-done | bytes 98336 | tf_op jit(solution)/shard_map/ppermute | solution.py:54
  26.5 0.9 %collective-permute-start.11 = (bf16[2,32,1280]{2,1,0:T(8,128)(2,1)S(1)}, bf16[2,32,1280]{2,1,0:T(8,128)(2,1)S(1)}, u32[]{:S(2)}, u32[]{:S(2)}) collective-permute-start(bf16[2,32,1280]{2,1,0:T(8,128)(2,1)S(1)} %get-tuple-element.51), channel_id=1, source_target_pairs={{0,2},{2,0},{4,6},{6,4},{8,10},{10,8},{12,14},{14,12},{16,18},{18,... | collective-permute-start | bytes 491528 | tf_op jit(solution)/shard_map/ppermute | solution.py:54
  27.5 1.8 %collective-permute-start.12 = (bf16[2,32,1280]{2,1,0:T(8,128)(2,1)S(1)}, bf16[2,32,1280]{2,1,0:T(8,128)(2,1)S(1)}, u32[]{:S(2)}, u32[]{:S(2)}) collective-permute-start(bf16[2,32,1280]{2,1,0:T(8,128)(2,1)S(1)} %get-tuple-element.52), channel_id=1, source_target_pairs={{0,4},{2,6},{4,0},{6,2},{8,12},{10,14},{12,8},{14,10},{16,20},{18,... | collective-permute-start | bytes 491528 | tf_op jit(solution)/shard_map/ppermute | solution.py:54
  29.3 2.3 %collective-permute-start.13 = (bf16[2,32,1280]{2,1,0:T(8,128)(2,1)S(1)}, bf16[2,32,1280]{2,1,0:T(8,128)(2,1)S(1)}, u32[]{:S(2)}, u32[]{:S(2)}) collective-permute-start(bf16[2,32,1280]{2,1,0:T(8,128)(2,1)S(1)} %get-tuple-element.53), channel_id=1, source_target_pairs={{0,6},{2,4},{4,2},{6,0},{8,14},{10,12},{12,10},{14,8},{16,22},{18,... | collective-permute-start | bytes 491528 | tf_op jit(solution)/shard_map/ppermute | solution.py:54
  31.6 0.8 %shard_map.103 = (bf16[2,32,512]{2,1,0:T(8,128)(2,1)S(1)}, bf16[2,32,256]{2,1,0:T(8,128)(2,1)S(1)}) custom-call(s32[1]{0:T(128)} %bitcast.refs_0_, s32[16]{0:T(128)} %refs_1_.9, s32[2]{0:T(128)} %refs_2_.4, s32[2]{0:T(128)S(1)} %collective-permute-done.1.refs_3_, s32[2]{0:T(128)S(1)} %collective-permute-done.2.refs_4_, s32[2]{0:T(128)S(1)} %collective-permute-done.3.refs_5_, ...), custom_call_target="tpu_custom_call" | custom-call | tf_op jit(solution)/shard_map/pallas_call | solution.py:39
  32.8 0.8 %collective-permute-done.11.refs_10_ = bf16[2,32,1280]{2,1,0:T(8,128)(2,1)S(1)} collective-permute-done((bf16[2,32,1280]{2,1,0:T(8,128)(2,1)S(1)}, bf16[2,32,1280]{2,1,0:T(8,128)(2,1)S(1)}, u32[]{:S(2)}, u32[]{:S(2)}) %collective-permute-start.11) | collective-permute-done | bytes 163872 | tf_op jit(solution)/shard_map/ppermute | solution.py:54
  33.6 1.5 %collective-permute-done.12.refs_11_ = bf16[2,32,1280]{2,1,0:T(8,128)(2,1)S(1)} collective-permute-done((bf16[2,32,1280]{2,1,0:T(8,128)(2,1)S(1)}, bf16[2,32,1280]{2,1,0:T(8,128)(2,1)S(1)}, u32[]{:S(2)}, u32[]{:S(2)}) %collective-permute-start.12) | collective-permute-done | bytes 163872 | tf_op jit(solution)/shard_map/ppermute | solution.py:54
  35.1 1.3 %collective-permute-done.13.refs_12_ = bf16[2,32,1280]{2,1,0:T(8,128)(2,1)S(1)} collective-permute-done((bf16[2,32,1280]{2,1,0:T(8,128)(2,1)S(1)}, bf16[2,32,1280]{2,1,0:T(8,128)(2,1)S(1)}, u32[]{:S(2)}, u32[]{:S(2)}) %collective-permute-start.13) | collective-permute-done | bytes 163872 | tf_op jit(solution)/shard_map/ppermute | solution.py:54
  36.4 0.8 %shard_map.104.factor = bf16[2,32,1792]{2,1,0:T(8,128)(2,1)S(1)} custom-call(s32[1]{0:T(128)} %bitcast.refs_0_, s32[16]{0:T(128)} %refs_1_.9, s32[2]{0:T(128)} %refs_2_.4, s32[2]{0:T(128)S(1)} %collective-permute-done.1.refs_3_, s32[2]{0:T(128)S(1)} %collective-permute-done.2.refs_4_, s32[2]{0:T(128)S(1)} %collective-permute-done.3.refs_5_, ...), custom_call_target="tpu_custom_call" | custom-call | tf_op jit(solution)/shard_map/pallas_call | solution.py:39
  37.2 1.7 %fusion.14 = f32[2,32,768]{2,1,0:T(8,128)S(1)} fusion(bf16[2,32,1792]{2,1,0:T(8,128)(2,1)S(1)} %shard_map.104.factor, bf16[2,768,1792]{2,1,0:T(8,128)(2,1)S(1)} %bitcast.23), kind=kOutput, calls=%fused_computation.21 | convolution fusion | flops 176160768 | bytes 5931008 | tf_op jit(solution)/shard_map/slw,srw->srl/dot_general | solution.py:225
  39.0 1.0 %fusion.15 = f32[2,32,1792]{2,1,0:T(8,128)S(1)} fusion(bf16[2,32,768]{2,1,0:T(8,128)(2,1)S(1)} %add_convert_fusion.coeff, bf16[2,768,1792]{2,1,0:T(8,128)(2,1)S(1)} %bitcast.24), kind=kOutput, calls=%fused_computation.22 | convolution fusion | flops 176160768 | bytes 6062080 | tf_op jit(solution)/shard_map/srl,slw->srw/dot_general | solution.py:227
  40.0 0.3 collective-permute-done.14
  40.4 0.5 fusion.16
  40.9 2.1 %collective-permute-start.24 = (bf16[2,32,768]{2,1,0:T(8,128)(2,1)S(1)}, bf16[2,32,768]{2,1,0:T(8,128)(2,1)S(1)}, u32[]{:S(2)}, u32[]{:S(2)}) collective-permute-start(bf16[2,32,768]{2,1,0:T(8,128)(2,1)S(1)} %fusion.12), channel_id=1, source_target_pairs={{0,6},{2,4},{4,2},{6,0},{8,14},{10,12},{12,10},{14,8},{16,22},{18,... | collective-permute-start | bytes 294920 | tf_op jit(solution)/shard_map/ppermute | solution.py:54
  43.0 1.0 %collective-permute-start.23 = (bf16[2,32,768]{2,1,0:T(8,128)(2,1)S(1)}, bf16[2,32,768]{2,1,0:T(8,128)(2,1)S(1)}, u32[]{:S(2)}, u32[]{:S(2)}) collective-permute-start(bf16[2,32,768]{2,1,0:T(8,128)(2,1)S(1)} %fusion.12), channel_id=1, source_target_pairs={{0,4},{2,6},{4,0},{6,2},{8,12},{10,14},{12,8},{14,10},{16,20},{18,... | collective-permute-start | bytes 294920 | tf_op jit(solution)/shard_map/ppermute | solution.py:54
  44.0 0.4 collective-permute-start.22
  44.5 2.4 %collective-permute-done.24.refs_9_ = bf16[2,32,768]{2,1,0:T(8,128)(2,1)S(1)} collective-permute-done((bf16[2,32,768]{2,1,0:T(8,128)(2,1)S(1)}, bf16[2,32,768]{2,1,0:T(8,128)(2,1)S(1)}, u32[]{:S(2)}, u32[]{:S(2)}) %collective-permute-start.24) | collective-permute-done | bytes 98336 | tf_op jit(solution)/shard_map/ppermute | solution.py:54
  46.9 2.7 %collective-permute-start.18 = (bf16[2,32,1280]{2,1,0:T(8,128)(2,1)S(1)}, bf16[2,32,1280]{2,1,0:T(8,128)(2,1)S(1)}, u32[]{:S(2)}, u32[]{:S(2)}) collective-permute-start(bf16[2,32,1280]{2,1,0:T(8,128)(2,1)S(1)} %slice.49), channel_id=1, source_target_pairs={{0,6},{2,4},{4,2},{6,0},{8,14},{10,12},{12,10},{14,8},{16,22},{18,... | collective-permute-start | bytes 491528 | tf_op jit(solution)/shard_map/ppermute | solution.py:54
  49.6 1.0 %collective-permute-start.17 = (bf16[2,32,1280]{2,1,0:T(8,128)(2,1)S(1)}, bf16[2,32,1280]{2,1,0:T(8,128)(2,1)S(1)}, u32[]{:S(2)}, u32[]{:S(2)}) collective-permute-start(bf16[2,32,1280]{2,1,0:T(8,128)(2,1)S(1)} %slice.49), channel_id=1, source_target_pairs={{0,4},{2,6},{4,0},{6,2},{8,12},{10,14},{12,8},{14,10},{16,20},{18,... | collective-permute-start | bytes 491528 | tf_op jit(solution)/shard_map/ppermute | solution.py:54
  50.6 0.5 collective-permute-start.16
  51.2 0.9 %shard_map.106 = (f32[32,768]{1,0:T(8,128)S(1)}, bf16[32,768]{1,0:T(8,128)(2,1)S(1)}, bf16[32,768]{1,0:T(8,128)(2,1)S(1)}, bf16[32,768]{1,0:T(8,128)(2,1)S(1)}) custom-call(s32[1]{0:T(128)} %bitcast.refs_0_, s32[16]{0:T(128)} %refs_1_.9, s32[2]{0:T(128)} %refs_2_.4, s32[2]{0:T(128)S(1)} %collective-permute-done.1.refs_3_, ...), custom_call_target="tpu_custom_call" | custom-call | tf_op jit(solution)/shard_map/pallas_call | solution.py:39
  52.1 2.0 %collective-permute-done.18.refs_9_ = bf16[2,32,1280]{2,1,0:T(8,128)(2,1)S(1)} collective-permute-done((bf16[2,32,1280]{2,1,0:T(8,128)(2,1)S(1)}, bf16[2,32,1280]{2,1,0:T(8,128)(2,1)S(1)}, u32[]{:S(2)}, u32[]{:S(2)}) %collective-permute-start.18) | collective-permute-done | bytes 163872 | tf_op jit(solution)/shard_map/ppermute | solution.py:54
  54.1 1.0 %collective-permute-start.25 = (bf16[32,768]{1,0:T(8,128)(2,1)S(1)}, bf16[32,768]{1,0:T(8,128)(2,1)S(1)}, u32[]{:S(2)}, u32[]{:S(2)}) collective-permute-start(bf16[32,768]{1,0:T(8,128)(2,1)S(1)} %get-tuple-element.61), channel_id=1, source_target_pairs={{0,8},{2,10},{4,12},{6,14},{8,0},{10,2},{12,4},{14,6},{16,24},{18,... | collective-permute-start | bytes 147464 | tf_op jit(solution)/shard_map/ppermute | solution.py:57
  55.1 1.5 %collective-permute-done.17.refs_8_ = bf16[2,32,1280]{2,1,0:T(8,128)(2,1)S(1)} collective-permute-done((bf16[2,32,1280]{2,1,0:T(8,128)(2,1)S(1)}, bf16[2,32,1280]{2,1,0:T(8,128)(2,1)S(1)}, u32[]{:S(2)}, u32[]{:S(2)}) %collective-permute-start.17) | collective-permute-done | bytes 163872 | tf_op jit(solution)/shard_map/ppermute | solution.py:54
  56.6 2.2 %collective-permute-start.26 = (bf16[32,768]{1,0:T(8,128)(2,1)S(1)}, bf16[32,768]{1,0:T(8,128)(2,1)S(1)}, u32[]{:S(2)}, u32[]{:S(2)}) collective-permute-start(bf16[32,768]{1,0:T(8,128)(2,1)S(1)} %get-tuple-element.62), channel_id=1, source_target_pairs={{0,16},{2,18},{4,20},{6,22},{8,24},{10,26},{12,28},{14,30},{16,0},... | collective-permute-start | bytes 147464 | tf_op jit(solution)/shard_map/ppermute | solution.py:57
  58.8 1.5 %collective-permute-start.27 = (bf16[32,768]{1,0:T(8,128)(2,1)S(1)}, bf16[32,768]{1,0:T(8,128)(2,1)S(1)}, u32[]{:S(2)}, u32[]{:S(2)}) collective-permute-start(bf16[32,768]{1,0:T(8,128)(2,1)S(1)} %get-tuple-element.63), channel_id=1, source_target_pairs={{0,24},{2,26},{4,28},{6,30},{8,16},{10,18},{12,20},{14,22},{16,8},... | collective-permute-start | bytes 147464 | tf_op jit(solution)/shard_map/ppermute | solution.py:57
  60.3 0.9 %shard_map.105 = (f32[32,1280]{1,0:T(8,128)S(1)}, bf16[32,1280]{1,0:T(8,128)(2,1)S(1)}, bf16[32,1280]{1,0:T(8,128)(2,1)S(1)}, bf16[32,1280]{1,0:T(8,128)(2,1)S(1)}) custom-call(s32[1]{0:T(128)} %bitcast.refs_0_, s32[16]{0:T(128)} %refs_1_.9, s32[2]{0:T(128)} %refs_2_.4, s32[2]{0:T(128)S(1)} %collective-permute-done.1.refs_3_, ...), custom_call_target="tpu_custom_call" | custom-call | tf_op jit(solution)/shard_map/pallas_call | solution.py:39
  61.2 0.7 collective-permute-start.19
  61.9 2.3 %collective-permute-start.20 = (bf16[32,1280]{1,0:T(8,128)(2,1)S(1)}, bf16[32,1280]{1,0:T(8,128)(2,1)S(1)}, u32[]{:S(2)}, u32[]{:S(2)}) collective-permute-start(bf16[32,1280]{1,0:T(8,128)(2,1)S(1)} %get-tuple-element.59), channel_id=1, source_target_pairs={{0,16},{2,18},{4,20},{6,22},{8,24},{10,26},{12,28},{14,30},{16,0},... | collective-permute-start | bytes 245768 | tf_op jit(solution)/shard_map/ppermute | solution.py:57
  64.2 1.5 %collective-permute-start.21 = (bf16[32,1280]{1,0:T(8,128)(2,1)S(1)}, bf16[32,1280]{1,0:T(8,128)(2,1)S(1)}, u32[]{:S(2)}, u32[]{:S(2)}) collective-permute-start(bf16[32,1280]{1,0:T(8,128)(2,1)S(1)} %get-tuple-element.60), channel_id=1, source_target_pairs={{0,24},{2,26},{4,28},{6,30},{8,16},{10,18},{12,20},{14,22},{16,8},... | collective-permute-start | bytes 245768 | tf_op jit(solution)/shard_map/ppermute | solution.py:57
  65.6 3.1 %fusion.4.pre_ref = f32[1536,1792]{1,0:T(8,128)S(1)} fusion(bf16[1792,512]{1,0:T(8,128)(2,1)S(1)} %copy-done, bf16[1536,256]{1,0:T(8,128)(2,1)S(1)} %collective-permute-done, bf16[1536,256]{1,0:T(8,128)(2,1)S(1)} %get-tuple-element.42, pred[]{:T(512)S(6)} %eq.3), kind=kOutput, calls=%fused_computation.5 | convolution fusion | flops 2825650176 | bytes 14417921 | tf_op jit(solution)/shard_map/dot_general | solution.py:213
  68.7 5.1 %outputs.1 = (bf16[1536,1792]{1,0:T(8,128)(2,1)}, bf16[1536,256]{1,0:T(8,128)(2,1)}) custom-call(s32[1]{0:T(128)} %bitcast.1.core_ref, f32[1536,1792]{1,0:T(8,128)S(1)} %fusion.4.pre_ref, bf16[2,32,768]{2,1,0:T(8,128)(2,1)S(1)} %add_convert_fusion.coeff, bf16[2,32,1792]{2,1,0:T(8,128)(2,1)S(1)} %shard_map.104.factor, f32[2,32,768]{2,1,0:T(8,128)S(1)} %add.7.low_ref, ...), custom_call_target="tpu_custom_call" | custom-call | tf_op jit(solution)/shard_map/outputs/pallas_call | solution.py:257
  73.8 0.7 shard_map.107
  (37 shorter events, 1.0 us)
Async XLA Ops:
  0.6 12.7 %copy-start = (bf16[1792,512]{1,0:T(8,128)(2,1)S(1)}, bf16[1792,512]{1,0:T(8,128)(2,1)}, u32[]{:S(2)}) copy-start(bf16[1792,512]{1,0:T(8,128)(2,1)} %param.8) | copy-start | bytes 5505028
  0.7 16.0 %collective-permute-start.3 = (s32[2]{0:T(128)}, s32[2]{0:T(128)S(1)}, u32[]{:S(2)}, u32[]{:S(2)}) collective-permute-start(s32[2]{0:T(128)} %refs_2_.4), channel_id=1, source_target_pairs={{0,6},{2,4},{4,2},{6,0},{8,14},{10,12},{12,10},{14,8},{16,22},{18,... | collective-permute-start | bytes 32 | tf_op jit(solution)/shard_map/ppermute | solution.py:54
  4.6 12.9 %collective-permute-start.2 = (s32[2]{0:T(128)}, s32[2]{0:T(128)S(1)}, u32[]{:S(2)}, u32[]{:S(2)}) collective-permute-start(s32[2]{0:T(128)} %refs_2_.4), channel_id=1, source_target_pairs={{0,4},{2,6},{4,0},{6,2},{8,12},{10,14},{12,8},{14,10},{16,20},{18,... | collective-permute-start | bytes 32 | tf_op jit(solution)/shard_map/ppermute | solution.py:54
  6.1 14.6 %collective-permute-start.6 = (bf16[32,2048]{1,0:T(8,128)(2,1)S(1)}, bf16[32,2048]{1,0:T(8,128)(2,1)S(1)}, u32[]{:S(2)}, u32[]{:S(2)}) collective-permute-start(bf16[32,2048]{1,0:T(8,128)(2,1)S(1)} %join.1.refs_6_), channel_id=1, source_target_pairs={{0,24},{2,26},{4,28},{6,30},{8,16},{10,18},{12,20},{14,22},{16,8},... | collective-permute-start | bytes 393224 | tf_op jit(solution)/shard_map/ppermute | solution.py:57
  9.7 11.0 %collective-permute-start.5 = (bf16[32,2048]{1,0:T(8,128)(2,1)S(1)}, bf16[32,2048]{1,0:T(8,128)(2,1)S(1)}, u32[]{:S(2)}, u32[]{:S(2)}) collective-permute-start(bf16[32,2048]{1,0:T(8,128)(2,1)S(1)} %join.1.refs_6_), channel_id=1, source_target_pairs={{0,16},{2,18},{4,20},{6,22},{8,24},{10,26},{12,28},{14,30},{16,0},... | collective-permute-start | bytes 393224 | tf_op jit(solution)/shard_map/ppermute | solution.py:57
  9.7 11.0 %collective-permute-start.4 = (bf16[32,2048]{1,0:T(8,128)(2,1)S(1)}, bf16[32,2048]{1,0:T(8,128)(2,1)S(1)}, u32[]{:S(2)}, u32[]{:S(2)}) collective-permute-start(bf16[32,2048]{1,0:T(8,128)(2,1)S(1)} %join.1.refs_6_), channel_id=1, source_target_pairs={{0,8},{2,10},{4,12},{6,14},{8,0},{10,2},{12,4},{14,6},{16,24},{18,... | collective-permute-start | bytes 393224 | tf_op jit(solution)/shard_map/ppermute | solution.py:57
  16.5 0.7 copy-start.1
  17.1 3.6 %collective-permute-start.1 = (s32[2]{0:T(128)S(1)}, s32[2]{0:T(128)S(1)}, u32[]{:S(2)}, u32[]{:S(2)}) collective-permute-start(s32[2]{0:T(128)S(1)} %copy-done.1), channel_id=1, source_target_pairs={{0,2},{2,0},{4,6},{6,4},{8,10},{10,8},{12,14},{14,12},{16,18},{18,... | collective-permute-start | bytes 32 | tf_op jit(solution)/shard_map/ppermute | solution.py:54
  17.5 44.3 %collective-permute-start = (bf16[1536,256]{1,0:T(8,128)(2,1)S(1)}, bf16[1536,256]{1,0:T(8,128)(2,1)S(1)}, u32[]{:S(2)}, u32[]{:S(2)}) collective-permute-start(bf16[1536,256]{1,0:T(8,128)(2,1)S(1)} %get-tuple-element.42), channel_id=1, source_target_pairs={{0,1},{1,0},{2,3},{3,2},{4,5},{5,4},{6,7},{7,6},{8,9},{9,8},{10,11... | collective-permute-start | bytes 2359304 | tf_op jit(solution)/shard_map/ppermute | solution.py:60
  21.6 4.9 %collective-permute-start.7 = (bf16[2,32,768]{2,1,0:T(8,128)(2,1)S(1)}, bf16[2,32,768]{2,1,0:T(8,128)(2,1)S(1)}, u32[]{:S(2)}, u32[]{:S(2)}) collective-permute-start(bf16[2,32,768]{2,1,0:T(8,128)(2,1)S(1)} %get-tuple-element.47), channel_id=1, source_target_pairs={{0,2},{2,0},{4,6},{6,4},{8,10},{10,8},{12,14},{14,12},{16,18},{18,... | collective-permute-start | bytes 294920 | tf_op jit(solution)/shard_map/ppermute | solution.py:54
  22.1 5.4 %collective-permute-start.8 = (bf16[2,32,768]{2,1,0:T(8,128)(2,1)S(1)}, bf16[2,32,768]{2,1,0:T(8,128)(2,1)S(1)}, u32[]{:S(2)}, u32[]{:S(2)}) collective-permute-start(bf16[2,32,768]{2,1,0:T(8,128)(2,1)S(1)} %get-tuple-element.48), channel_id=1, source_target_pairs={{0,4},{2,6},{4,0},{6,2},{8,12},{10,14},{12,8},{14,10},{16,20},{18,... | collective-permute-start | bytes 294920 | tf_op jit(solution)/shard_map/ppermute | solution.py:54
  23.7 5.6 %collective-permute-start.9 = (bf16[2,32,768]{2,1,0:T(8,128)(2,1)S(1)}, bf16[2,32,768]{2,1,0:T(8,128)(2,1)S(1)}, u32[]{:S(2)}, u32[]{:S(2)}) collective-permute-start(bf16[2,32,768]{2,1,0:T(8,128)(2,1)S(1)} %get-tuple-element.49), channel_id=1, source_target_pairs={{0,6},{2,4},{4,2},{6,0},{8,14},{10,12},{12,10},{14,8},{16,22},{18,... | collective-permute-start | bytes 294920 | tf_op jit(solution)/shard_map/ppermute | solution.py:54
  25.3 38.9 %collective-permute-start.15 = (f32[1536,256]{1,0:T(8,128)S(1)}, f32[1536,256]{1,0:T(8,128)S(1)}, u32[]{:S(2)}, u32[]{:S(2)}) collective-permute-start(f32[1536,256]{1,0:T(8,128)S(1)} %pad_maximum_fusion), channel_id=1, source_target_pairs={{0,1},{1,0},{2,3},{3,2},{4,5},{5,4},{6,7},{7,6},{8,9},{9,8},{10,11... | collective-permute-start | bytes 4718600 | tf_op jit(solution)/shard_map/ppermute | solution.py:60
  26.5 7.1 %collective-permute-start.11 = (bf16[2,32,1280]{2,1,0:T(8,128)(2,1)S(1)}, bf16[2,32,1280]{2,1,0:T(8,128)(2,1)S(1)}, u32[]{:S(2)}, u32[]{:S(2)}) collective-permute-start(bf16[2,32,1280]{2,1,0:T(8,128)(2,1)S(1)} %get-tuple-element.51), channel_id=1, source_target_pairs={{0,2},{2,0},{4,6},{6,4},{8,10},{10,8},{12,14},{14,12},{16,18},{18,... | collective-permute-start | bytes 491528 | tf_op jit(solution)/shard_map/ppermute | solution.py:54
  27.5 7.6 %collective-permute-start.12 = (bf16[2,32,1280]{2,1,0:T(8,128)(2,1)S(1)}, bf16[2,32,1280]{2,1,0:T(8,128)(2,1)S(1)}, u32[]{:S(2)}, u32[]{:S(2)}) collective-permute-start(bf16[2,32,1280]{2,1,0:T(8,128)(2,1)S(1)} %get-tuple-element.52), channel_id=1, source_target_pairs={{0,4},{2,6},{4,0},{6,2},{8,12},{10,14},{12,8},{14,10},{16,20},{18,... | collective-permute-start | bytes 491528 | tf_op jit(solution)/shard_map/ppermute | solution.py:54
  29.3 7.1 %collective-permute-start.13 = (bf16[2,32,1280]{2,1,0:T(8,128)(2,1)S(1)}, bf16[2,32,1280]{2,1,0:T(8,128)(2,1)S(1)}, u32[]{:S(2)}, u32[]{:S(2)}) collective-permute-start(bf16[2,32,1280]{2,1,0:T(8,128)(2,1)S(1)} %get-tuple-element.53), channel_id=1, source_target_pairs={{0,6},{2,4},{4,2},{6,0},{8,14},{10,12},{12,10},{14,8},{16,22},{18,... | collective-permute-start | bytes 491528 | tf_op jit(solution)/shard_map/ppermute | solution.py:54
  33.6 5.3 %collective-permute-start.10 = (f32[2,32,768]{2,1,0:T(8,128)S(1)}, f32[2,32,768]{2,1,0:T(8,128)S(1)}, u32[]{:S(2)}, u32[]{:S(2)}) collective-permute-start(f32[2,32,768]{2,1,0:T(8,128)S(1)} %fusion.13), channel_id=1, source_target_pairs={{0,1},{1,0},{2,3},{3,2},{4,5},{5,4},{6,7},{7,6},{8,9},{9,8},{10,11... | collective-permute-start | bytes 589832 | tf_op jit(solution)/shard_map/ppermute | solution.py:60
  38.9 1.5 %collective-permute-start.14 = (f32[2,32,768]{2,1,0:T(8,128)S(1)}, f32[2,32,768]{2,1,0:T(8,128)S(1)}, u32[]{:S(2)}, u32[]{:S(2)}) collective-permute-start(f32[2,32,768]{2,1,0:T(8,128)S(1)} %fusion.14), channel_id=1, source_target_pairs={{0,1},{1,0},{2,3},{3,2},{4,5},{5,4},{6,7},{7,6},{8,9},{9,8},{10,11... | collective-permute-start | bytes 589832 | tf_op jit(solution)/shard_map/ppermute | solution.py:60
  40.9 5.9 %collective-permute-start.24 = (bf16[2,32,768]{2,1,0:T(8,128)(2,1)S(1)}, bf16[2,32,768]{2,1,0:T(8,128)(2,1)S(1)}, u32[]{:S(2)}, u32[]{:S(2)}) collective-permute-start(bf16[2,32,768]{2,1,0:T(8,128)(2,1)S(1)} %fusion.12), channel_id=1, source_target_pairs={{0,6},{2,4},{4,2},{6,0},{8,14},{10,12},{12,10},{14,8},{16,22},{18,... | collective-permute-start | bytes 294920 | tf_op jit(solution)/shard_map/ppermute | solution.py:54
  43.0 6.6 %collective-permute-start.23 = (bf16[2,32,768]{2,1,0:T(8,128)(2,1)S(1)}, bf16[2,32,768]{2,1,0:T(8,128)(2,1)S(1)}, u32[]{:S(2)}, u32[]{:S(2)}) collective-permute-start(bf16[2,32,768]{2,1,0:T(8,128)(2,1)S(1)} %fusion.12), channel_id=1, source_target_pairs={{0,4},{2,6},{4,0},{6,2},{8,12},{10,14},{12,8},{14,10},{16,20},{18,... | collective-permute-start | bytes 294920 | tf_op jit(solution)/shard_map/ppermute | solution.py:54
  44.0 6.6 %collective-permute-start.22 = (bf16[2,32,768]{2,1,0:T(8,128)(2,1)S(1)}, bf16[2,32,768]{2,1,0:T(8,128)(2,1)S(1)}, u32[]{:S(2)}, u32[]{:S(2)}) collective-permute-start(bf16[2,32,768]{2,1,0:T(8,128)(2,1)S(1)} %fusion.12), channel_id=1, source_target_pairs={{0,2},{2,0},{4,6},{6,4},{8,10},{10,8},{12,14},{14,12},{16,18},{18,... | collective-permute-start | bytes 294920 | tf_op jit(solution)/shard_map/ppermute | solution.py:54
  46.9 7.2 %collective-permute-start.18 = (bf16[2,32,1280]{2,1,0:T(8,128)(2,1)S(1)}, bf16[2,32,1280]{2,1,0:T(8,128)(2,1)S(1)}, u32[]{:S(2)}, u32[]{:S(2)}) collective-permute-start(bf16[2,32,1280]{2,1,0:T(8,128)(2,1)S(1)} %slice.49), channel_id=1, source_target_pairs={{0,6},{2,4},{4,2},{6,0},{8,14},{10,12},{12,10},{14,8},{16,22},{18,... | collective-permute-start | bytes 491528 | tf_op jit(solution)/shard_map/ppermute | solution.py:54
  49.6 7.0 %collective-permute-start.17 = (bf16[2,32,1280]{2,1,0:T(8,128)(2,1)S(1)}, bf16[2,32,1280]{2,1,0:T(8,128)(2,1)S(1)}, u32[]{:S(2)}, u32[]{:S(2)}) collective-permute-start(bf16[2,32,1280]{2,1,0:T(8,128)(2,1)S(1)} %slice.49), channel_id=1, source_target_pairs={{0,4},{2,6},{4,0},{6,2},{8,12},{10,14},{12,8},{14,10},{16,20},{18,... | collective-permute-start | bytes 491528 | tf_op jit(solution)/shard_map/ppermute | solution.py:54
  50.6 8.2 %collective-permute-start.16 = (bf16[2,32,1280]{2,1,0:T(8,128)(2,1)S(1)}, bf16[2,32,1280]{2,1,0:T(8,128)(2,1)S(1)}, u32[]{:S(2)}, u32[]{:S(2)}) collective-permute-start(bf16[2,32,1280]{2,1,0:T(8,128)(2,1)S(1)} %slice.49), channel_id=1, source_target_pairs={{0,2},{2,0},{4,6},{6,4},{8,10},{10,8},{12,14},{14,12},{16,18},{18,... | collective-permute-start | bytes 491528 | tf_op jit(solution)/shard_map/ppermute | solution.py:54
  54.1 7.1 %collective-permute-start.25 = (bf16[32,768]{1,0:T(8,128)(2,1)S(1)}, bf16[32,768]{1,0:T(8,128)(2,1)S(1)}, u32[]{:S(2)}, u32[]{:S(2)}) collective-permute-start(bf16[32,768]{1,0:T(8,128)(2,1)S(1)} %get-tuple-element.61), channel_id=1, source_target_pairs={{0,8},{2,10},{4,12},{6,14},{8,0},{10,2},{12,4},{14,6},{16,24},{18,... | collective-permute-start | bytes 147464 | tf_op jit(solution)/shard_map/ppermute | solution.py:57
  56.6 17.2 %collective-permute-start.26 = (bf16[32,768]{1,0:T(8,128)(2,1)S(1)}, bf16[32,768]{1,0:T(8,128)(2,1)S(1)}, u32[]{:S(2)}, u32[]{:S(2)}) collective-permute-start(bf16[32,768]{1,0:T(8,128)(2,1)S(1)} %get-tuple-element.62), channel_id=1, source_target_pairs={{0,16},{2,18},{4,20},{6,22},{8,24},{10,26},{12,28},{14,30},{16,0},... | collective-permute-start | bytes 147464 | tf_op jit(solution)/shard_map/ppermute | solution.py:57
  58.8 15.0 %collective-permute-start.27 = (bf16[32,768]{1,0:T(8,128)(2,1)S(1)}, bf16[32,768]{1,0:T(8,128)(2,1)S(1)}, u32[]{:S(2)}, u32[]{:S(2)}) collective-permute-start(bf16[32,768]{1,0:T(8,128)(2,1)S(1)} %get-tuple-element.63), channel_id=1, source_target_pairs={{0,24},{2,26},{4,28},{6,30},{8,16},{10,18},{12,20},{14,22},{16,8},... | collective-permute-start | bytes 147464 | tf_op jit(solution)/shard_map/ppermute | solution.py:57
  61.2 12.6 %collective-permute-start.19 = (bf16[32,1280]{1,0:T(8,128)(2,1)S(1)}, bf16[32,1280]{1,0:T(8,128)(2,1)S(1)}, u32[]{:S(2)}, u32[]{:S(2)}) collective-permute-start(bf16[32,1280]{1,0:T(8,128)(2,1)S(1)} %get-tuple-element.58), channel_id=1, source_target_pairs={{0,8},{2,10},{4,12},{6,14},{8,0},{10,2},{12,4},{14,6},{16,24},{18,... | collective-permute-start | bytes 245768 | tf_op jit(solution)/shard_map/ppermute | solution.py:57
  61.9 11.9 %collective-permute-start.20 = (bf16[32,1280]{1,0:T(8,128)(2,1)S(1)}, bf16[32,1280]{1,0:T(8,128)(2,1)S(1)}, u32[]{:S(2)}, u32[]{:S(2)}) collective-permute-start(bf16[32,1280]{1,0:T(8,128)(2,1)S(1)} %get-tuple-element.59), channel_id=1, source_target_pairs={{0,16},{2,18},{4,20},{6,22},{8,24},{10,26},{12,28},{14,30},{16,0},... | collective-permute-start | bytes 245768 | tf_op jit(solution)/shard_map/ppermute | solution.py:57
  64.2 9.6 %collective-permute-start.21 = (bf16[32,1280]{1,0:T(8,128)(2,1)S(1)}, bf16[32,1280]{1,0:T(8,128)(2,1)S(1)}, u32[]{:S(2)}, u32[]{:S(2)}) collective-permute-start(bf16[32,1280]{1,0:T(8,128)(2,1)S(1)} %get-tuple-element.60), channel_id=1, source_target_pairs={{0,24},{2,26},{4,28},{6,30},{8,16},{10,18},{12,20},{14,22},{16,8},... | collective-permute-start | bytes 245768 | tf_op jit(solution)/shard_map/ppermute | solution.py:57

commit v6 on v5

--- a/solution.py
+++ b/solution.py
@@ -95,7 +95,7 @@
             held.append(send_outer(mine, d))
         for d in range(1, q):
             tenants.append(send_inner(tenant, d))
-        ints = [me, fixed(table), fixed(tenant)] + tenants[1:]
+        ints = [me, table, tenant] + tenants[1:]
 
         def load(x_ref, g_ref, x_out, g_out, sems):
             copies = [
@@ -210,8 +210,11 @@
             both = jnp.where(
                 low_core, jnp.concatenate([grad_in, other], axis=1), jnp.concatenate([other, grad_in], axis=1)
             )
-            pre = lax.dot_general(both, weight, (((1,), (1,)), ((), ())), preferred_element_type=F32)
-            pre = pltpu.with_memory_space_constraint(pre, pltpu.VMEM)
+            both = both.reshape(seqs, length, m * cols)
+            pre = []
+            for j in range(seqs):
+                pre.append(lax.dot_general(both[j], weight, (((1,), (1,)), ((), ())), preferred_element_type=F32))
+            pre = [pltpu.with_memory_space_constraint(x, pltpu.VMEM) for x in pre]
         base = []
         for j in range(seqs):
             base.append(jnp.dot(h3[j], weight, preferred_element_type=F32))
@@ -228,28 +231,29 @@
         if m == 2:
             per = length // block
 
-            def outputs(core_ref, pre_ref, coeff, factor, low_ref, up_ref, got_ref, *rest_refs):
-                bases, (out, values_out) = rest_refs[:seqs], rest_refs[seqs:]
+            def outputs(core_ref, coeff, factor, low_ref, up_ref, got_ref, *rest_refs):
+                pres, bases, (out, values_out) = rest_refs[:seqs], rest_refs[seqs : 2 * seqs], rest_refs[2 * seqs :]
                 step = pl.program_id(0)
+                at = pl.multiple_of(step % per * block, block)
                 here = pl.multiple_of(core_ref[0] * cols, math.gcd(cols, 128))
-                out[...] = (
-                    pre_ref[pl.ds(pl.multiple_of(step * block, block), block), :]
-                    + lax.dot_general(
-                        coeff[0], factor[0], (((0,), (0,)), ((), ())), preferred_element_type=F32
-                    )
-                ).astype(BF16)
+                piece, parts = low_ref[0], []
+                for _ in range(3):
+                    parts.append(piece.astype(BF16))
+                    piece = piece - parts[-1].astype(F32)
                 term = got_ref[...] + lax.dot_general(
-                    low_ref[0],
-                    up_ref[0].astype(F32),
+                    jnp.concatenate(parts, axis=0),
+                    jnp.concatenate([up_ref[0]] * 3, axis=0),
                     (((0,), (0,)), ((), ())),
-                    precision=HIGH,
                     preferred_element_type=F32,
                 )
                 for j in range(seqs):
 
                     @pl.when(step // per == j)
                     def _(j=j):
-                        at = pl.multiple_of(step % per * block, block)
+                        adapter = lax.dot_general(
+                            coeff[0], factor[0], (((0,), (0,)), ((), ())), preferred_element_type=F32
+                        )
+                        out[...] = (adapter + pres[j][pl.ds(at, block), :]).astype(BF16)
                         values_out[...] = (term + bases[j][pl.ds(at, block), pl.ds(here, cols)]).astype(BF16)
 
             rows_of = pl.BlockSpec((block, cols), lambda i: (i, 0))
@@ -263,18 +267,17 @@
                 ],
                 in_specs=[
                     SMEM,
-                    VMEM,
                     coeff_of,
                     pl.BlockSpec((1, rank, width), lambda i: (i // per, 0, 0)),
                     coeff_of,
                     pl.BlockSpec((1, rank, cols), lambda i: (i // per, 0, 0)),
                     rows_of,
                 ]
-                + [VMEM] * seqs,
+                + [VMEM] * (2 * seqs),
                 out_specs=[pl.BlockSpec((block, width), lambda i: (i, 0)), rows_of],
                 compiler_params=pltpu.CompilerParams(vmem_limit_bytes=32 << 20),
                 name="outputs",
-            )(core, pre, back_low, down_s, low, up_s, base_got, *base)[::-1]
+            )(core, back_low, down_s, low, up_s, base_got, *pre, *base)[::-1]
         else:
             values = (
                 base_own.reshape(seqs, length, cols)
@@ -285,7 +288,7 @@
                 + jnp.einsum("srl,srw->slw", back_low, down_s, preferred_element_type=F32).reshape(rows, width)
             ).astype(BF16)
 
-        early = (width + cols) * 5 // 1024 * 128
+        early = (width + cols) * 9 // 2048 * 128
         items = [down_seq[:, :, :early], jnp.concatenate([down_seq[:, :, early:], up_seq], axis=2)]
         near = [[], []]
         for p in range(2):

time: 74.8 us -> 73.7 us (0.985)
  Pallas kernels: 13.7 us -> 12.4 us
  waiting for transfers between devices: 14.3 us -> 13.4 us
    dot_general x1 -> x2, matrix products: 3.08 us -> 3.26 us  [local(): lax.dot_general(both[j], weight, (((1,), (1,)), ((), ())), preferred_elem...]
  transfers between devices with their start and end apart: 28 -> 28, of which waited for: 9 -> 8; matrix products, arithmetic and copies ran while one was open for 14% -> 15% of each run, Pallas kernels for 17% -> 16%
where the time goes in v6:
time: 73.7 us; the launch traced here: 73.5 us
  starting transfers between devices  35.6 us (48%)
  waiting for transfers between devices  13.4 us (18%)
  Pallas kernels  12.4 us (17%)
  matrix products  9.93 us (13%)
  between operations  0.92 us (1%)
  other arithmetic  0.81 us (1%)
    ppermute x15, starting transfers between devices, send_inner(): lax.ppermute(x, 'dp', [(i, i // q * q + peer(i % q, d, q)) for i in range...  21.4 us
    ppermute x9, starting transfers between devices, send_outer(): lax.ppermute(x, 'dp', [(i, peer(i // q, d, r) * q + i % q) for i in range...  14.1 us
    ppermute x15, waiting for transfers between devices, send_inner(): lax.ppermute(x, 'dp', [(i, i // q * q + peer(i % q, d, q)) for i in range...  13.4 us
    pallas_call x6, Pallas kernels, kernel_call(): pl.pallas_call(body, out_shape=[pltpu.VMEM(o.shape, o.dtype) if inside el...  4.39 us
    pallas_call x1, Pallas kernels, local(): pl.pallas_call(outputs, grid=(rows // block,), out_shape=[jax.ShapeDtypeS...  4.32 us
    dot_general x2, matrix products, local(): lax.dot_general(both[j], weight, (((1,), (1,)), ((), ())), preferred_elem...  3.26 us
    dot_general x2, matrix products, local(): base.append(jnp.dot(h3[j], weight, preferred_element_type=F32))  3.15 us
    pallas_call x1, Pallas kernels, local(): pl.pallas_call(load, out_shape=[pltpu.VMEM(hidden.shape, BF16), pltpu.VME...  2.77 us
  transfers between devices with their start and end apart: 28, of which 8 were waited for; matrix products, arithmetic and copies ran while one was open for 15% of the time, Pallas kernels for 16%

profile of v6, /device:TPU:0, one launch (start us, length us, event | category | flops | bytes accessed | tf_op | source)
XLA Modules:
  0.0 73.5 jit_solution(4483397119722483419)
XLA Ops:
  0.7 4.0 %collective-permute-start.2 = (s32[2]{0:T(128)}, s32[2]{0:T(128)S(1)}, u32[]{:S(2)}, u32[]{:S(2)}) collective-permute-start(s32[2]{0:T(128)} %refs_2_.4), channel_id=1, source_target_pairs={{0,6},{2,4},{4,2},{6,0},{8,14},{10,12},{12,10},{14,8},{16,22},{18,... | collective-permute-start | bytes 32 | tf_op jit(solution)/shard_map/ppermute | solution.py:54
  4.6 0.5 collective-permute-start.1
  5.2 0.9 %join.1.refs_6_ = bf16[32,2048]{1,0:T(8,128)(2,1)S(1)} custom-call(bf16[32,1792]{1,0:T(8,128)(2,1)} %bitcast.28, bf16[32,256]{1,0:T(8,128)(2,1)} %bitcast.29), custom_call_target="tpu_custom_call" | custom-call | tf_op jit(solution)/shard_map/join/pallas_call | solution.py:87
  6.1 3.7 %collective-permute-start.5 = (bf16[32,2048]{1,0:T(8,128)(2,1)S(1)}, bf16[32,2048]{1,0:T(8,128)(2,1)S(1)}, u32[]{:S(2)}, u32[]{:S(2)}) collective-permute-start(bf16[32,2048]{1,0:T(8,128)(2,1)S(1)} %join.1.refs_6_), channel_id=1, source_target_pairs={{0,24},{2,26},{4,28},{6,30},{8,16},{10,18},{12,20},{14,22},{16,8},... | collective-permute-start | bytes 393224 | tf_op jit(solution)/shard_map/ppermute | solution.py:57
  9.7 0.8 %collective-permute-start.3 = (bf16[32,2048]{1,0:T(8,128)(2,1)S(1)}, bf16[32,2048]{1,0:T(8,128)(2,1)S(1)}, u32[]{:S(2)}, u32[]{:S(2)}) collective-permute-start(bf16[32,2048]{1,0:T(8,128)(2,1)S(1)} %join.1.refs_6_), channel_id=1, source_target_pairs={{0,8},{2,10},{4,12},{6,14},{8,0},{10,2},{12,4},{14,6},{16,24},{18,... | collective-permute-start | bytes 393224 | tf_op jit(solution)/shard_map/ppermute | solution.py:57
  10.5 2.8 %load.1 = (bf16[1536,1792]{1,0:T(8,128)(2,1)S(1)}, bf16[1536,256]{1,0:T(8,128)(2,1)S(1)}) custom-call(bf16[1536,1792]{1,0:T(8,128)(2,1)} %x_ref.1, bf16[1536,256]{1,0:T(8,128)(2,1)} %g_ref.1), custom_call_target="tpu_custom_call" | custom-call | tf_op jit(solution)/shard_map/load/pallas_call | solution.py:110
  13.3 1.6 %fusion.rest_refs_3_ = f32[768,512]{1,0:T(8,128)S(1)} fusion(bf16[1792,512]{1,0:T(8,128)(2,1)S(1)} %copy-done, bf16[1536,1792]{1,0:T(8,128)(2,1)S(1)} %get-tuple-element.54), kind=kOutput, calls=%fused_computation | convolution fusion | flops 1409286144 | bytes 6160384 | tf_op jit(solution)/shard_map/dot_general | solution.py:220
  14.9 1.6 %fusion.2.rest_refs_2_ = f32[768,512]{1,0:T(8,128)S(1)} fusion(bf16[1792,512]{1,0:T(8,128)(2,1)S(1)} %copy-done, bf16[1536,1792]{1,0:T(8,128)(2,1)S(1)} %get-tuple-element.54), kind=kOutput, calls=%fused_computation.2 | convolution fusion | flops 1409286144 | bytes 6160384 | tf_op jit(solution)/shard_map/dot_general | solution.py:220
  16.7 0.4 copy-done.2
  17.5 3.2 %collective-permute-done.refs_3_ = s32[2]{0:T(128)S(1)} collective-permute-done((s32[2]{0:T(128)S(1)}, s32[2]{0:T(128)S(1)}, u32[]{:S(2)}, u32[]{:S(2)}) %collective-permute-start) | collective-permute-done | bytes 40 | tf_op jit(solution)/shard_map/ppermute | solution.py:54
  20.7 0.8 %shard_map.102 = (bf16[2,32,768]{2,1,0:T(8,128)(2,1)S(1)}, bf16[2,32,768]{2,1,0:T(8,128)(2,1)S(1)}, bf16[2,32,768]{2,1,0:T(8,128)(2,1)S(1)}, bf16[2,32,1280]{2,1...) custom-call(s32[1]{0:T(128)} %bitcast.refs_0_, s32[16]{0:T(128)S(1)} %copy-done.1, ...), custom_call_target="tpu_custom_call" | custom-call | tf_op jit(solution)/shard_map/pallas_call | solution.py:39
  21.5 0.5 collective-permute-start.6
  22.0 1.7 %collective-permute-start.7 = (bf16[2,32,768]{2,1,0:T(8,128)(2,1)S(1)}, bf16[2,32,768]{2,1,0:T(8,128)(2,1)S(1)}, u32[]{:S(2)}, u32[]{:S(2)}) collective-permute-start(bf16[2,32,768]{2,1,0:T(8,128)(2,1)S(1)} %get-tuple-element.46), channel_id=1, source_target_pairs={{0,4},{2,6},{4,0},{6,2},{8,12},{10,14},{12,8},{14,10},{16,20},{18,... | collective-permute-start | bytes 294920 | tf_op jit(solution)/shard_map/ppermute | solution.py:54
  23.6 1.4 %collective-permute-start.8 = (bf16[2,32,768]{2,1,0:T(8,128)(2,1)S(1)}, bf16[2,32,768]{2,1,0:T(8,128)(2,1)S(1)}, u32[]{:S(2)}, u32[]{:S(2)}) collective-permute-start(bf16[2,32,768]{2,1,0:T(8,128)(2,1)S(1)} %get-tuple-element.47), channel_id=1, source_target_pairs={{0,6},{2,4},{4,2},{6,0},{8,14},{10,12},{12,10},{14,8},{16,22},{18,... | collective-permute-start | bytes 294920 | tf_op jit(solution)/shard_map/ppermute | solution.py:54
  25.3 1.2 %collective-permute-done.6.refs_10_ = bf16[2,32,768]{2,1,0:T(8,128)(2,1)S(1)} collective-permute-done((bf16[2,32,768]{2,1,0:T(8,128)(2,1)S(1)}, bf16[2,32,768]{2,1,0:T(8,128)(2,1)S(1)}, u32[]{:S(2)}, u32[]{:S(2)}) %collective-permute-start.6) | collective-permute-done | bytes 98336 | tf_op jit(solution)/shard_map/ppermute | solution.py:54
  26.4 0.9 %collective-permute-start.10 = (bf16[2,32,1280]{2,1,0:T(8,128)(2,1)S(1)}, bf16[2,32,1280]{2,1,0:T(8,128)(2,1)S(1)}, u32[]{:S(2)}, u32[]{:S(2)}) collective-permute-start(bf16[2,32,1280]{2,1,0:T(8,128)(2,1)S(1)} %get-tuple-element.50), channel_id=1, source_target_pairs={{0,2},{2,0},{4,6},{6,4},{8,10},{10,8},{12,14},{14,12},{16,18},{18,... | collective-permute-start | bytes 491528 | tf_op jit(solution)/shard_map/ppermute | solution.py:54
  27.4 1.8 %collective-permute-start.11 = (bf16[2,32,1280]{2,1,0:T(8,128)(2,1)S(1)}, bf16[2,32,1280]{2,1,0:T(8,128)(2,1)S(1)}, u32[]{:S(2)}, u32[]{:S(2)}) collective-permute-start(bf16[2,32,1280]{2,1,0:T(8,128)(2,1)S(1)} %get-tuple-element.51), channel_id=1, source_target_pairs={{0,4},{2,6},{4,0},{6,2},{8,12},{10,14},{12,8},{14,10},{16,20},{18,... | collective-permute-start | bytes 491528 | tf_op jit(solution)/shard_map/ppermute | solution.py:54
  29.2 2.3 %collective-permute-start.12 = (bf16[2,32,1280]{2,1,0:T(8,128)(2,1)S(1)}, bf16[2,32,1280]{2,1,0:T(8,128)(2,1)S(1)}, u32[]{:S(2)}, u32[]{:S(2)}) collective-permute-start(bf16[2,32,1280]{2,1,0:T(8,128)(2,1)S(1)} %get-tuple-element.52), channel_id=1, source_target_pairs={{0,6},{2,4},{4,2},{6,0},{8,14},{10,12},{12,10},{14,8},{16,22},{18,... | collective-permute-start | bytes 491528 | tf_op jit(solution)/shard_map/ppermute | solution.py:54
  31.5 0.7 shard_map.103
  32.5 1.0 %collective-permute-done.10.refs_10_ = bf16[2,32,1280]{2,1,0:T(8,128)(2,1)S(1)} collective-permute-done((bf16[2,32,1280]{2,1,0:T(8,128)(2,1)S(1)}, bf16[2,32,1280]{2,1,0:T(8,128)(2,1)S(1)}, u32[]{:S(2)}, u32[]{:S(2)}) %collective-permute-start.10) | collective-permute-done | bytes 163872 | tf_op jit(solution)/shard_map/ppermute | solution.py:54
  33.5 1.5 %collective-permute-done.11.refs_11_ = bf16[2,32,1280]{2,1,0:T(8,128)(2,1)S(1)} collective-permute-done((bf16[2,32,1280]{2,1,0:T(8,128)(2,1)S(1)}, bf16[2,32,1280]{2,1,0:T(8,128)(2,1)S(1)}, u32[]{:S(2)}, u32[]{:S(2)}) %collective-permute-start.11) | collective-permute-done | bytes 163872 | tf_op jit(solution)/shard_map/ppermute | solution.py:54
  35.0 1.3 %collective-permute-done.12.refs_12_ = bf16[2,32,1280]{2,1,0:T(8,128)(2,1)S(1)} collective-permute-done((bf16[2,32,1280]{2,1,0:T(8,128)(2,1)S(1)}, bf16[2,32,1280]{2,1,0:T(8,128)(2,1)S(1)}, u32[]{:S(2)}, u32[]{:S(2)}) %collective-permute-start.12) | collective-permute-done | bytes 163872 | tf_op jit(solution)/shard_map/ppermute | solution.py:54
  36.3 0.7 shard_map.104.factor
  37.0 1.7 %fusion.10 = f32[2,32,768]{2,1,0:T(8,128)S(1)} fusion(bf16[2,32,1792]{2,1,0:T(8,128)(2,1)S(1)} %shard_map.104.factor, bf16[2,768,1792]{2,1,0:T(8,128)(2,1)S(1)} %bitcast.24), kind=kOutput, calls=%fused_computation.17 | convolution fusion | flops 176160768 | bytes 5931008 | tf_op jit(solution)/shard_map/slw,srw->srl/dot_general | solution.py:228
  38.7 1.0 %fusion.11 = f32[2,32,1792]{2,1,0:T(8,128)S(1)} fusion(bf16[2,32,768]{2,1,0:T(8,128)(2,1)S(1)} %add_convert_fusion.coeff, bf16[2,768,1792]{2,1,0:T(8,128)(2,1)S(1)} %bitcast.25), kind=kOutput, calls=%fused_computation.18 | convolution fusion | flops 176160768 | bytes 6062080 | tf_op jit(solution)/shard_map/srl,slw->srw/dot_general | solution.py:230
  39.8 2.1 %collective-permute-start.18 = (bf16[2,32,1152]{2,1,0:T(8,128)(2,1)S(1)}, bf16[2,32,1152]{2,1,0:T(8,128)(2,1)S(1)}, u32[]{:S(2)}, u32[]{:S(2)}) collective-permute-start(bf16[2,32,1152]{2,1,0:T(8,128)(2,1)S(1)} %slice.65), channel_id=1, source_target_pairs={{0,6},{2,4},{4,2},{6,0},{8,14},{10,12},{12,10},{14,8},{16,22},{18,... | collective-permute-start | bytes 442376 | tf_op jit(solution)/shard_map/ppermute | solution.py:54
  41.9 1.0 %collective-permute-start.17 = (bf16[2,32,1152]{2,1,0:T(8,128)(2,1)S(1)}, bf16[2,32,1152]{2,1,0:T(8,128)(2,1)S(1)}, u32[]{:S(2)}, u32[]{:S(2)}) collective-permute-start(bf16[2,32,1152]{2,1,0:T(8,128)(2,1)S(1)} %slice.65), channel_id=1, source_target_pairs={{0,4},{2,6},{4,0},{6,2},{8,12},{10,14},{12,8},{14,10},{16,20},{18,... | collective-permute-start | bytes 442376 | tf_op jit(solution)/shard_map/ppermute | solution.py:54
  43.0 0.5 collective-permute-start.16
  43.5 0.5 fusion.12
  44.0 3.5 %collective-permute-done.18.refs_9_ = bf16[2,32,1152]{2,1,0:T(8,128)(2,1)S(1)} collective-permute-done((bf16[2,32,1152]{2,1,0:T(8,128)(2,1)S(1)}, bf16[2,32,1152]{2,1,0:T(8,128)(2,1)S(1)}, u32[]{:S(2)}, u32[]{:S(2)}) %collective-permute-start.18) | collective-permute-done | bytes 147488 | tf_op jit(solution)/shard_map/ppermute | solution.py:54
  47.5 2.0 %collective-permute-start.24 = (bf16[2,32,896]{2,1,0:T(8,128)(2,1)S(1)}, bf16[2,32,896]{2,1,0:T(8,128)(2,1)S(1)}, u32[]{:S(2)}, u32[]{:S(2)}) collective-permute-start(bf16[2,32,896]{2,1,0:T(8,128)(2,1)S(1)} %fusion.8), channel_id=1, source_target_pairs={{0,6},{2,4},{4,2},{6,0},{8,14},{10,12},{12,10},{14,8},{16,22},{18,... | collective-permute-start | bytes 344072 | tf_op jit(solution)/shard_map/ppermute | solution.py:54
  49.5 0.7 collective-permute-done.17.refs_8_
  50.2 1.2 %collective-permute-start.23 = (bf16[2,32,896]{2,1,0:T(8,128)(2,1)S(1)}, bf16[2,32,896]{2,1,0:T(8,128)(2,1)S(1)}, u32[]{:S(2)}, u32[]{:S(2)}) collective-permute-start(bf16[2,32,896]{2,1,0:T(8,128)(2,1)S(1)} %fusion.8), channel_id=1, source_target_pairs={{0,4},{2,6},{4,0},{6,2},{8,12},{10,14},{12,8},{14,10},{16,20},{18,... | collective-permute-start | bytes 344072 | tf_op jit(solution)/shard_map/ppermute | solution.py:54
  51.4 1.1 %collective-permute-start.22 = (bf16[2,32,896]{2,1,0:T(8,128)(2,1)S(1)}, bf16[2,32,896]{2,1,0:T(8,128)(2,1)S(1)}, u32[]{:S(2)}, u32[]{:S(2)}) collective-permute-start(bf16[2,32,896]{2,1,0:T(8,128)(2,1)S(1)} %fusion.8), channel_id=1, source_target_pairs={{0,2},{2,0},{4,6},{6,4},{8,10},{10,8},{12,14},{14,12},{16,18},{18,... | collective-permute-start | bytes 344072 | tf_op jit(solution)/shard_map/ppermute | solution.py:54
  52.5 0.8 %shard_map.105 = (f32[32,1152]{1,0:T(8,128)S(1)}, bf16[32,1152]{1,0:T(8,128)(2,1)S(1)}, bf16[32,1152]{1,0:T(8,128)(2,1)S(1)}, bf16[32,1152]{1,0:T(8,128)(2,1)S(1)}) custom-call(s32[1]{0:T(128)} %bitcast.refs_0_, s32[16]{0:T(128)S(1)} %copy-done.1, s32[2]{0:T(128)S(1)} %copy-done.2, s32[2]{0:T(128)S(1)} %collective-permute-done.refs_3_, ...), custom_call_target="tpu_custom_call" | custom-call | tf_op jit(solution)/shard_map/pallas_call | solution.py:39
  53.3 1.4 %collective-permute-start.19 = (bf16[32,1152]{1,0:T(8,128)(2,1)S(1)}, bf16[32,1152]{1,0:T(8,128)(2,1)S(1)}, u32[]{:S(2)}, u32[]{:S(2)}) collective-permute-start(bf16[32,1152]{1,0:T(8,128)(2,1)S(1)} %get-tuple-element.58), channel_id=1, source_target_pairs={{0,8},{2,10},{4,12},{6,14},{8,0},{10,2},{12,4},{14,6},{16,24},{18,... | collective-permute-start | bytes 221192 | tf_op jit(solution)/shard_map/ppermute | solution.py:57
  54.7 1.0 %collective-permute-done.23.refs_8_ = bf16[2,32,896]{2,1,0:T(8,128)(2,1)S(1)} collective-permute-done((bf16[2,32,896]{2,1,0:T(8,128)(2,1)S(1)}, bf16[2,32,896]{2,1,0:T(8,128)(2,1)S(1)}, u32[]{:S(2)}, u32[]{:S(2)}) %collective-permute-start.23) | collective-permute-done | bytes 114720 | tf_op jit(solution)/shard_map/ppermute | solution.py:54
  55.7 2.1 %collective-permute-start.20 = (bf16[32,1152]{1,0:T(8,128)(2,1)S(1)}, bf16[32,1152]{1,0:T(8,128)(2,1)S(1)}, u32[]{:S(2)}, u32[]{:S(2)}) collective-permute-start(bf16[32,1152]{1,0:T(8,128)(2,1)S(1)} %get-tuple-element.59), channel_id=1, source_target_pairs={{0,16},{2,18},{4,20},{6,22},{8,24},{10,26},{12,28},{14,30},{16,0},... | collective-permute-start | bytes 221192 | tf_op jit(solution)/shard_map/ppermute | solution.py:57
  57.8 1.6 %collective-permute-start.21 = (bf16[32,1152]{1,0:T(8,128)(2,1)S(1)}, bf16[32,1152]{1,0:T(8,128)(2,1)S(1)}, u32[]{:S(2)}, u32[]{:S(2)}) collective-permute-start(bf16[32,1152]{1,0:T(8,128)(2,1)S(1)} %get-tuple-element.60), channel_id=1, source_target_pairs={{0,24},{2,26},{4,28},{6,30},{8,16},{10,18},{12,20},{14,22},{16,8},... | collective-permute-start | bytes 221192 | tf_op jit(solution)/shard_map/ppermute | solution.py:57
  59.4 0.7 %shard_map.106 = (f32[32,896]{1,0:T(8,128)S(1)}, bf16[32,896]{1,0:T(8,128)(2,1)S(1)}, bf16[32,896]{1,0:T(8,128)(2,1)S(1)}, bf16[32,896]{1,0:T(8,128)(2,1)S(1)}) custom-call(s32[1]{0:T(128)} %bitcast.refs_0_, s32[16]{0:T(128)S(1)} %copy-done.1, s32[2]{0:T(128)S(1)} %copy-done.2, s32[2]{0:T(128)S(1)} %collective-permute-done.refs_3_, ...), custom_call_target="tpu_custom_call" | custom-call | tf_op jit(solution)/shard_map/pallas_call | solution.py:39
  60.2 0.5 collective-permute-start.25
  60.7 0.4 maximum_select_fusion
  61.2 1.6 %fusion.4.rest_refs_1_ = f32[768,1792]{1,0:T(8,128)S(1)} fusion(bf16[1792,512]{1,0:T(8,128)(2,1)S(1)} %copy-done, bf16[1536,512]{1,0:T(8,128)(2,1)S(1)} %maximum_select_fusion), kind=kOutput, calls=%fused_computation.6 | convolution fusion | flops 1409286144 | bytes 8126464 | tf_op jit(solution)/shard_map/dot_general | solution.py:216
  62.8 2.4 %collective-permute-start.26 = (bf16[32,896]{1,0:T(8,128)(2,1)S(1)}, bf16[32,896]{1,0:T(8,128)(2,1)S(1)}, u32[]{:S(2)}, u32[]{:S(2)}) collective-permute-start(bf16[32,896]{1,0:T(8,128)(2,1)S(1)} %get-tuple-element.62), channel_id=1, source_target_pairs={{0,16},{2,18},{4,20},{6,22},{8,24},{10,26},{12,28},{14,30},{16,0},... | collective-permute-start | bytes 172040 | tf_op jit(solution)/shard_map/ppermute | solution.py:57
  65.2 1.6 %collective-permute-start.27 = (bf16[32,896]{1,0:T(8,128)(2,1)S(1)}, bf16[32,896]{1,0:T(8,128)(2,1)S(1)}, u32[]{:S(2)}, u32[]{:S(2)}) collective-permute-start(bf16[32,896]{1,0:T(8,128)(2,1)S(1)} %get-tuple-element.63), channel_id=1, source_target_pairs={{0,24},{2,26},{4,28},{6,30},{8,16},{10,18},{12,20},{14,22},{16,8},... | collective-permute-start | bytes 172040 | tf_op jit(solution)/shard_map/ppermute | solution.py:57
  66.8 1.6 %fusion.6.rest_refs_0_ = f32[768,1792]{1,0:T(8,128)S(1)} fusion(bf16[1792,512]{1,0:T(8,128)(2,1)S(1)} %copy-done, bf16[1536,512]{1,0:T(8,128)(2,1)S(1)} %maximum_select_fusion), kind=kOutput, calls=%fused_computation.8 | convolution fusion | flops 1409286144 | bytes 8126464 | tf_op jit(solution)/shard_map/dot_general | solution.py:216
  68.4 4.3 %outputs.1 = (bf16[1536,1792]{1,0:T(8,128)(2,1)}, bf16[1536,256]{1,0:T(8,128)(2,1)}) custom-call(s32[1]{0:T(128)} %bitcast.1.core_ref, bf16[2,32,768]{2,1,0:T(8,128)(2,1)S(1)} %add_convert_fusion.coeff, bf16[2,32,1792]{2,1,0:T(8,128)(2,1)S(1)} %shard_map.104.factor, f32[2,32,768]{2,1,0:T(8,128)S(1)} %add.7.low_ref, ...), custom_call_target="tpu_custom_call" | custom-call | tf_op jit(solution)/shard_map/outputs/pallas_call | solution.py:261
  72.8 0.7 %shard_map.107 = (f32[32,1792]{1,0:T(8,128)}, f32[32,256]{1,0:T(8,128)}) custom-call(f32[32,1152]{1,0:T(8,128)S(1)} %get-tuple-element.66.refs_0_, f32[32,896]{1,0:T(8,128)S(1)} %get-tuple-element.67.refs_1_, bf16[32,1152]{1,0:T(8,128)(2,1)S(1)} %collective-permute-done.19.refs_2_, bf16[32,1152]{1,0:T(8,128)(2,1)S(1)} %collective-permute-done.20.refs_3_, ...), custom_call_target="tpu_custom_call" | custom-call | tf_op jit(solution)/shard_map/pallas_call | solution.py:39
  (41 shorter events, 1.4 us)
Async XLA Ops:
  0.6 12.7 %copy-start = (bf16[1792,512]{1,0:T(8,128)(2,1)S(1)}, bf16[1792,512]{1,0:T(8,128)(2,1)}, u32[]{:S(2)}) copy-start(bf16[1792,512]{1,0:T(8,128)(2,1)} %param.8) | copy-start | bytes 5505028
  0.7 16.0 %collective-permute-start.2 = (s32[2]{0:T(128)}, s32[2]{0:T(128)S(1)}, u32[]{:S(2)}, u32[]{:S(2)}) collective-permute-start(s32[2]{0:T(128)} %refs_2_.4), channel_id=1, source_target_pairs={{0,6},{2,4},{4,2},{6,0},{8,14},{10,12},{12,10},{14,8},{16,22},{18,... | collective-permute-start | bytes 32 | tf_op jit(solution)/shard_map/ppermute | solution.py:54
  4.6 12.9 %collective-permute-start.1 = (s32[2]{0:T(128)}, s32[2]{0:T(128)S(1)}, u32[]{:S(2)}, u32[]{:S(2)}) collective-permute-start(s32[2]{0:T(128)} %refs_2_.4), channel_id=1, source_target_pairs={{0,4},{2,6},{4,0},{6,2},{8,12},{10,14},{12,8},{14,10},{16,20},{18,... | collective-permute-start | bytes 32 | tf_op jit(solution)/shard_map/ppermute | solution.py:54
  6.1 14.6 %collective-permute-start.5 = (bf16[32,2048]{1,0:T(8,128)(2,1)S(1)}, bf16[32,2048]{1,0:T(8,128)(2,1)S(1)}, u32[]{:S(2)}, u32[]{:S(2)}) collective-permute-start(bf16[32,2048]{1,0:T(8,128)(2,1)S(1)} %join.1.refs_6_), channel_id=1, source_target_pairs={{0,24},{2,26},{4,28},{6,30},{8,16},{10,18},{12,20},{14,22},{16,8},... | collective-permute-start | bytes 393224 | tf_op jit(solution)/shard_map/ppermute | solution.py:57
  9.7 11.0 %collective-permute-start.4 = (bf16[32,2048]{1,0:T(8,128)(2,1)S(1)}, bf16[32,2048]{1,0:T(8,128)(2,1)S(1)}, u32[]{:S(2)}, u32[]{:S(2)}) collective-permute-start(bf16[32,2048]{1,0:T(8,128)(2,1)S(1)} %join.1.refs_6_), channel_id=1, source_target_pairs={{0,16},{2,18},{4,20},{6,22},{8,24},{10,26},{12,28},{14,30},{16,0},... | collective-permute-start | bytes 393224 | tf_op jit(solution)/shard_map/ppermute | solution.py:57
  9.7 11.0 %collective-permute-start.3 = (bf16[32,2048]{1,0:T(8,128)(2,1)S(1)}, bf16[32,2048]{1,0:T(8,128)(2,1)S(1)}, u32[]{:S(2)}, u32[]{:S(2)}) collective-permute-start(bf16[32,2048]{1,0:T(8,128)(2,1)S(1)} %join.1.refs_6_), channel_id=1, source_target_pairs={{0,8},{2,10},{4,12},{6,14},{8,0},{10,2},{12,4},{14,6},{16,24},{18,... | collective-permute-start | bytes 393224 | tf_op jit(solution)/shard_map/ppermute | solution.py:57
  16.5 0.7 copy-start.2
  16.5 4.2 %copy-start.1 = (s32[16]{0:T(128)S(1)}, s32[16]{0:T(128)}, u32[]{:S(2)}) copy-start(s32[16]{0:T(128)} %refs_1_.9) | copy-start | bytes 196
  17.1 3.6 %collective-permute-start = (s32[2]{0:T(128)S(1)}, s32[2]{0:T(128)S(1)}, u32[]{:S(2)}, u32[]{:S(2)}) collective-permute-start(s32[2]{0:T(128)S(1)} %copy-done.2), channel_id=1, source_target_pairs={{0,2},{2,0},{4,6},{6,4},{8,10},{10,8},{12,14},{14,12},{16,18},{18,... | collective-permute-start | bytes 32 | tf_op jit(solution)/shard_map/ppermute | solution.py:54
  17.5 42.7 %collective-permute-start.15 = (bf16[1536,256]{1,0:T(8,128)(2,1)S(1)}, bf16[1536,256]{1,0:T(8,128)(2,1)S(1)}, u32[]{:S(2)}, u32[]{:S(2)}) collective-permute-start(bf16[1536,256]{1,0:T(8,128)(2,1)S(1)} %get-tuple-element.49), channel_id=1, source_target_pairs={{0,1},{1,0},{2,3},{3,2},{4,5},{5,4},{6,7},{7,6},{8,9},{9,8},{10,11... | collective-permute-start | bytes 2359304 | tf_op jit(solution)/shard_map/ppermute | solution.py:60
  21.5 4.9 %collective-permute-start.6 = (bf16[2,32,768]{2,1,0:T(8,128)(2,1)S(1)}, bf16[2,32,768]{2,1,0:T(8,128)(2,1)S(1)}, u32[]{:S(2)}, u32[]{:S(2)}) collective-permute-start(bf16[2,32,768]{2,1,0:T(8,128)(2,1)S(1)} %get-tuple-element.45), channel_id=1, source_target_pairs={{0,2},{2,0},{4,6},{6,4},{8,10},{10,8},{12,14},{14,12},{16,18},{18,... | collective-permute-start | bytes 294920 | tf_op jit(solution)/shard_map/ppermute | solution.py:54
  22.0 5.4 %collective-permute-start.7 = (bf16[2,32,768]{2,1,0:T(8,128)(2,1)S(1)}, bf16[2,32,768]{2,1,0:T(8,128)(2,1)S(1)}, u32[]{:S(2)}, u32[]{:S(2)}) collective-permute-start(bf16[2,32,768]{2,1,0:T(8,128)(2,1)S(1)} %get-tuple-element.46), channel_id=1, source_target_pairs={{0,4},{2,6},{4,0},{6,2},{8,12},{10,14},{12,8},{14,10},{16,20},{18,... | collective-permute-start | bytes 294920 | tf_op jit(solution)/shard_map/ppermute | solution.py:54
  23.6 5.6 %collective-permute-start.8 = (bf16[2,32,768]{2,1,0:T(8,128)(2,1)S(1)}, bf16[2,32,768]{2,1,0:T(8,128)(2,1)S(1)}, u32[]{:S(2)}, u32[]{:S(2)}) collective-permute-start(bf16[2,32,768]{2,1,0:T(8,128)(2,1)S(1)} %get-tuple-element.47), channel_id=1, source_target_pairs={{0,6},{2,4},{4,2},{6,0},{8,14},{10,12},{12,10},{14,8},{16,22},{18,... | collective-permute-start | bytes 294920 | tf_op jit(solution)/shard_map/ppermute | solution.py:54
  25.2 40.0 %collective-permute-start.14 = (f32[1536,256]{1,0:T(8,128)S(1)}, f32[1536,256]{1,0:T(8,128)S(1)}, u32[]{:S(2)}, u32[]{:S(2)}) collective-permute-start(f32[1536,256]{1,0:T(8,128)S(1)} %pad_maximum_fusion), channel_id=1, source_target_pairs={{0,1},{1,0},{2,3},{3,2},{4,5},{5,4},{6,7},{7,6},{8,9},{9,8},{10,11... | collective-permute-start | bytes 4718600 | tf_op jit(solution)/shard_map/ppermute | solution.py:60
  26.4 7.1 %collective-permute-start.10 = (bf16[2,32,1280]{2,1,0:T(8,128)(2,1)S(1)}, bf16[2,32,1280]{2,1,0:T(8,128)(2,1)S(1)}, u32[]{:S(2)}, u32[]{:S(2)}) collective-permute-start(bf16[2,32,1280]{2,1,0:T(8,128)(2,1)S(1)} %get-tuple-element.50), channel_id=1, source_target_pairs={{0,2},{2,0},{4,6},{6,4},{8,10},{10,8},{12,14},{14,12},{16,18},{18,... | collective-permute-start | bytes 491528 | tf_op jit(solution)/shard_map/ppermute | solution.py:54
  27.4 7.7 %collective-permute-start.11 = (bf16[2,32,1280]{2,1,0:T(8,128)(2,1)S(1)}, bf16[2,32,1280]{2,1,0:T(8,128)(2,1)S(1)}, u32[]{:S(2)}, u32[]{:S(2)}) collective-permute-start(bf16[2,32,1280]{2,1,0:T(8,128)(2,1)S(1)} %get-tuple-element.51), channel_id=1, source_target_pairs={{0,4},{2,6},{4,0},{6,2},{8,12},{10,14},{12,8},{14,10},{16,20},{18,... | collective-permute-start | bytes 491528 | tf_op jit(solution)/shard_map/ppermute | solution.py:54
  29.2 7.1 %collective-permute-start.12 = (bf16[2,32,1280]{2,1,0:T(8,128)(2,1)S(1)}, bf16[2,32,1280]{2,1,0:T(8,128)(2,1)S(1)}, u32[]{:S(2)}, u32[]{:S(2)}) collective-permute-start(bf16[2,32,1280]{2,1,0:T(8,128)(2,1)S(1)} %get-tuple-element.52), channel_id=1, source_target_pairs={{0,6},{2,4},{4,2},{6,0},{8,14},{10,12},{12,10},{14,8},{16,22},{18,... | collective-permute-start | bytes 491528 | tf_op jit(solution)/shard_map/ppermute | solution.py:54
  33.5 5.2 %collective-permute-start.9 = (f32[2,32,768]{2,1,0:T(8,128)S(1)}, f32[2,32,768]{2,1,0:T(8,128)S(1)}, u32[]{:S(2)}, u32[]{:S(2)}) collective-permute-start(f32[2,32,768]{2,1,0:T(8,128)S(1)} %fusion.9), channel_id=1, source_target_pairs={{0,1},{1,0},{2,3},{3,2},{4,5},{5,4},{6,7},{7,6},{8,9},{9,8},{10,11... | collective-permute-start | bytes 589832 | tf_op jit(solution)/shard_map/ppermute | solution.py:60
  38.7 4.3 %collective-permute-start.13 = (f32[2,32,768]{2,1,0:T(8,128)S(1)}, f32[2,32,768]{2,1,0:T(8,128)S(1)}, u32[]{:S(2)}, u32[]{:S(2)}) collective-permute-start(f32[2,32,768]{2,1,0:T(8,128)S(1)} %fusion.10), channel_id=1, source_target_pairs={{0,1},{1,0},{2,3},{3,2},{4,5},{5,4},{6,7},{7,6},{8,9},{9,8},{10,11... | collective-permute-start | bytes 589832 | tf_op jit(solution)/shard_map/ppermute | solution.py:60
  39.8 7.7 %collective-permute-start.18 = (bf16[2,32,1152]{2,1,0:T(8,128)(2,1)S(1)}, bf16[2,32,1152]{2,1,0:T(8,128)(2,1)S(1)}, u32[]{:S(2)}, u32[]{:S(2)}) collective-permute-start(bf16[2,32,1152]{2,1,0:T(8,128)(2,1)S(1)} %slice.65), channel_id=1, source_target_pairs={{0,6},{2,4},{4,2},{6,0},{8,14},{10,12},{12,10},{14,8},{16,22},{18,... | collective-permute-start | bytes 442376 | tf_op jit(solution)/shard_map/ppermute | solution.py:54
  41.9 8.3 %collective-permute-start.17 = (bf16[2,32,1152]{2,1,0:T(8,128)(2,1)S(1)}, bf16[2,32,1152]{2,1,0:T(8,128)(2,1)S(1)}, u32[]{:S(2)}, u32[]{:S(2)}) collective-permute-start(bf16[2,32,1152]{2,1,0:T(8,128)(2,1)S(1)} %slice.65), channel_id=1, source_target_pairs={{0,4},{2,6},{4,0},{6,2},{8,12},{10,14},{12,8},{14,10},{16,20},{18,... | collective-permute-start | bytes 442376 | tf_op jit(solution)/shard_map/ppermute | solution.py:54
  43.0 8.4 %collective-permute-start.16 = (bf16[2,32,1152]{2,1,0:T(8,128)(2,1)S(1)}, bf16[2,32,1152]{2,1,0:T(8,128)(2,1)S(1)}, u32[]{:S(2)}, u32[]{:S(2)}) collective-permute-start(bf16[2,32,1152]{2,1,0:T(8,128)(2,1)S(1)} %slice.65), channel_id=1, source_target_pairs={{0,2},{2,0},{4,6},{6,4},{8,10},{10,8},{12,14},{14,12},{16,18},{18,... | collective-permute-start | bytes 442376 | tf_op jit(solution)/shard_map/ppermute | solution.py:54
  47.5 5.8 %collective-permute-start.24 = (bf16[2,32,896]{2,1,0:T(8,128)(2,1)S(1)}, bf16[2,32,896]{2,1,0:T(8,128)(2,1)S(1)}, u32[]{:S(2)}, u32[]{:S(2)}) collective-permute-start(bf16[2,32,896]{2,1,0:T(8,128)(2,1)S(1)} %fusion.8), channel_id=1, source_target_pairs={{0,6},{2,4},{4,2},{6,0},{8,14},{10,12},{12,10},{14,8},{16,22},{18,... | collective-permute-start | bytes 344072 | tf_op jit(solution)/shard_map/ppermute | solution.py:54
  50.2 5.5 %collective-permute-start.23 = (bf16[2,32,896]{2,1,0:T(8,128)(2,1)S(1)}, bf16[2,32,896]{2,1,0:T(8,128)(2,1)S(1)}, u32[]{:S(2)}, u32[]{:S(2)}) collective-permute-start(bf16[2,32,896]{2,1,0:T(8,128)(2,1)S(1)} %fusion.8), channel_id=1, source_target_pairs={{0,4},{2,6},{4,0},{6,2},{8,12},{10,14},{12,8},{14,10},{16,20},{18,... | collective-permute-start | bytes 344072 | tf_op jit(solution)/shard_map/ppermute | solution.py:54
  51.4 6.5 %collective-permute-start.22 = (bf16[2,32,896]{2,1,0:T(8,128)(2,1)S(1)}, bf16[2,32,896]{2,1,0:T(8,128)(2,1)S(1)}, u32[]{:S(2)}, u32[]{:S(2)}) collective-permute-start(bf16[2,32,896]{2,1,0:T(8,128)(2,1)S(1)} %fusion.8), channel_id=1, source_target_pairs={{0,2},{2,0},{4,6},{6,4},{8,10},{10,8},{12,14},{14,12},{16,18},{18,... | collective-permute-start | bytes 344072 | tf_op jit(solution)/shard_map/ppermute | solution.py:54
  53.3 9.5 %collective-permute-start.19 = (bf16[32,1152]{1,0:T(8,128)(2,1)S(1)}, bf16[32,1152]{1,0:T(8,128)(2,1)S(1)}, u32[]{:S(2)}, u32[]{:S(2)}) collective-permute-start(bf16[32,1152]{1,0:T(8,128)(2,1)S(1)} %get-tuple-element.58), channel_id=1, source_target_pairs={{0,8},{2,10},{4,12},{6,14},{8,0},{10,2},{12,4},{14,6},{16,24},{18,... | collective-permute-start | bytes 221192 | tf_op jit(solution)/shard_map/ppermute | solution.py:57
  55.7 17.1 %collective-permute-start.20 = (bf16[32,1152]{1,0:T(8,128)(2,1)S(1)}, bf16[32,1152]{1,0:T(8,128)(2,1)S(1)}, u32[]{:S(2)}, u32[]{:S(2)}) collective-permute-start(bf16[32,1152]{1,0:T(8,128)(2,1)S(1)} %get-tuple-element.59), channel_id=1, source_target_pairs={{0,16},{2,18},{4,20},{6,22},{8,24},{10,26},{12,28},{14,30},{16,0},... | collective-permute-start | bytes 221192 | tf_op jit(solution)/shard_map/ppermute | solution.py:57
  57.8 14.9 %collective-permute-start.21 = (bf16[32,1152]{1,0:T(8,128)(2,1)S(1)}, bf16[32,1152]{1,0:T(8,128)(2,1)S(1)}, u32[]{:S(2)}, u32[]{:S(2)}) collective-permute-start(bf16[32,1152]{1,0:T(8,128)(2,1)S(1)} %get-tuple-element.60), channel_id=1, source_target_pairs={{0,24},{2,26},{4,28},{6,30},{8,16},{10,18},{12,20},{14,22},{16,8},... | collective-permute-start | bytes 221192 | tf_op jit(solution)/shard_map/ppermute | solution.py:57
  60.2 12.5 %collective-permute-start.25 = (bf16[32,896]{1,0:T(8,128)(2,1)S(1)}, bf16[32,896]{1,0:T(8,128)(2,1)S(1)}, u32[]{:S(2)}, u32[]{:S(2)}) collective-permute-start(bf16[32,896]{1,0:T(8,128)(2,1)S(1)} %get-tuple-element.61), channel_id=1, source_target_pairs={{0,8},{2,10},{4,12},{6,14},{8,0},{10,2},{12,4},{14,6},{16,24},{18,... | collective-permute-start | bytes 172040 | tf_op jit(solution)/shard_map/ppermute | solution.py:57
  62.8 10.0 %collective-permute-start.26 = (bf16[32,896]{1,0:T(8,128)(2,1)S(1)}, bf16[32,896]{1,0:T(8,128)(2,1)S(1)}, u32[]{:S(2)}, u32[]{:S(2)}) collective-permute-start(bf16[32,896]{1,0:T(8,128)(2,1)S(1)} %get-tuple-element.62), channel_id=1, source_target_pairs={{0,16},{2,18},{4,20},{6,22},{8,24},{10,26},{12,28},{14,30},{16,0},... | collective-permute-start | bytes 172040 | tf_op jit(solution)/shard_map/ppermute | solution.py:57
  65.2 7.6 %collective-permute-start.27 = (bf16[32,896]{1,0:T(8,128)(2,1)S(1)}, bf16[32,896]{1,0:T(8,128)(2,1)S(1)}, u32[]{:S(2)}, u32[]{:S(2)}) collective-permute-start(bf16[32,896]{1,0:T(8,128)(2,1)S(1)} %get-tuple-element.63), channel_id=1, source_target_pairs={{0,24},{2,26},{4,28},{6,30},{8,16},{10,18},{12,20},{14,22},{16,8},... | collective-permute-start | bytes 172040 | tf_op jit(solution)/shard_map/ppermute | solution.py:57
